TPU v7x, 256 devices: a whole 4x4x8 slice. The times are simulated.
256 devices in a mesh: gx: 4 (over x), gy: 8 (over z), gz: 8 (over y, core).
Axes of the slice: x: 4, y: 4, z: 8, core: 2. Of those that a mesh axis runs over, the one named last changes fastest.
Arguments:
- right_side: float32 [128, 256, 1024], P('gx', 'gy', 'gz'), may hold values from -1 to 1
- z_faces: float32 [1024], P('gz'), may hold values from 0.5 to 2, as said below
- xy_coupling: float32 [5], replicated, as said below
- block_inverse: float32 [5, 1024, 128], P(None, 'gz'), as said below
Outputs:
- solution: float32 [128, 256, 1024], P('gx', 'gy', 'gz')
- residual: float32 [128, 256, 1024], P('gx', 'gy', 'gz')
Inputs may be any that keep to these rules, and one draw needn't show every extreme that they name: z_faces is positive. xy_coupling[l] lies between 2.9 * 4^-l / 128^2 and 5.5 * 4^-l / 128^2. block_inverse[l] holds, block by block, the inverses of the 128 x 128 diagonal blocks of M_l built from z_faces and xy_coupling[l].
All inputs are finite; a program needn't handle non-finite values.
Results may differ from a plain program's by a relative error of at most 0.028.
Values sent between devices are 32-bit elements; how exact they have to be, the bound alone decides.
No kernel may reach another device: no remote copies, remote signals or barrier semaphores. Data moves between devices by JAX's collectives and lax.ppermute only.
A program may use at most 128 MiB of HBM per device.

v0:
```python
import math

import jax
import jax.numpy as jnp
from jax import lax
from jax.sharding import PartitionSpec as P

LEVELS = 5
SWEEPS = 2


damping = 0.8
highest = lax.Precision.HIGHEST


def joined_along(pieces, dim):
    dims = list(pieces.shape[1:])
    dims[dim] *= pieces.shape[0]
    return jnp.moveaxis(pieces, 0, dim).reshape(dims)


def copy_for_each(value, axis):
    size = lax.axis_size(axis)
    return lax.all_to_all(
        jnp.broadcast_to(value[None], (size, *value.shape)), axis, 0, 0, tiled=True
    )


def gather_directly(value, axis, dim):
    return joined_along(copy_for_each(value, axis), dim)


def extended(value, sides, width):
    edges = {}
    for axis, dim in sides:
        size, length = (lax.axis_size(axis), value.shape[dim])
        up = [(i, (i + 1) % size) for i in range(size - 1)]
        last = lax.slice_in_dim(value, length - width, length, axis=dim)
        initial = lax.slice_in_dim(value, 0, width, axis=dim)
        edges[dim] = (
            lax.ppermute(last, axis, up),
            lax.ppermute(initial, axis, [(b, a) for a, b in up]),
        )
    done = []
    for _, dim in sides:
        low, high = edges[dim]
        around = [(width, width) if d in done else (0, 0) for d in range(value.ndim)]
        value = jnp.concatenate([jnp.pad(low, around), value, jnp.pad(high, around)], axis=dim)
        done.append(dim)
    return value


def side_by_side(arrays, axis, dim, along):
    widths = [math.prod(a.shape[along:]) for a in arrays]
    both = jnp.concatenate(
        [a.reshape(*a.shape[:along], w) for a, w in zip(arrays, widths)], axis=along
    )
    whole = lax.all_gather(both, axis, axis=dim, tiled=True)
    pieces = jnp.split(whole, [sum(widths[:k]) for k in range(1, len(widths))], axis=along)
    return tuple(
        (b.reshape(*whole.shape[:along], *a.shape[along:]) for a, b in zip(arrays, pieces))
    )


def extended_2(cells, sides, width):
    for axis, dim in sides:
        count = lax.axis_size(axis)
        ends = count - 1
        head = lax.slice_in_dim(cells, 0, width, axis=dim)
        tail = lax.slice_in_dim(cells, cells.shape[dim] - width, cells.shape[dim], axis=dim)
        cells = jnp.concatenate(
            [
                lax.ppermute(tail, axis, [(i, (i + 1) % count) for i in range(ends)]),
                cells,
                lax.ppermute(head, axis, [((i + 1) % count, i) for i in range(ends)]),
            ],
            axis=dim,
        )
    return cells


def interface_setup(corner_aa, corner_ab, corner_ba, corner_bb, couplings):
    determinant = corner_aa * corner_bb - corner_ab * corner_ba
    corner_inverse = (
        jnp.stack(
            [jnp.stack([corner_bb, -corner_ab], -1), jnp.stack([-corner_ba, corner_aa], -1)], -2
        )
        / determinant[:, None, None]
    )
    blocks_count = corner_aa.shape[0]
    identity = jnp.eye(blocks_count, dtype=corner_inverse.dtype)
    diagonal_part = jnp.einsum("kab,kl->kalb", corner_inverse, identity, precision=highest).reshape(
        2 * blocks_count, 2 * blocks_count
    )
    link_values = jnp.zeros((2 * blocks_count - 1,), corner_inverse.dtype).at[1::2].set(-couplings)
    schur_matrix = diagonal_part + jnp.diag(link_values, 1) + jnp.diag(link_values, -1)
    return (corner_inverse, diagonal_part, jnp.linalg.cholesky(schur_matrix))


def make_solver(inverse_block, corner_rows, couplings, device_index, down_coupling, up_coupling):
    corner_inverse, diagonal_part, factor = interface_setup(
        corner_rows[:, 0], corner_rows[:, 1], corner_rows[:, 2], corner_rows[:, 3], couplings
    )
    block_len = inverse_block.shape[0]
    forward = lax.linalg.triangular_solve(factor, diagonal_part, left_side=True, lower=True)
    reach = lax.linalg.triangular_solve(
        factor, forward, left_side=True, lower=True, transpose_a=True
    )
    padded_reach = jnp.pad(reach, ((1, 1), (0, 0)))
    slice_rows = lax.dynamic_slice_in_dim(padded_reach, 2 * device_index, 4, 0)
    needed = jnp.stack([slice_rows[0], slice_rows[3]])

    def neighbours(end_values):
        zero_carry = jnp.zeros(end_values.shape, jnp.float32)
        nearby = zero_carry + jnp.dot(
            needed, gather_directly(end_values, "gz", 0), precision=highest
        )
        return (nearby[0], nearby[1])

    def solve(source):
        first_extent, second_extent, depth = source.shape
        line_count = first_extent * second_extent
        local_part = jnp.einsum("xyj,ij->xyi", source, inverse_block, precision=highest)
        end_values = jnp.stack(
            [
                local_part[:, :, 0].reshape(line_count),
                local_part[:, :, block_len - 1].reshape(line_count),
            ]
        )
        below_last, above_first = neighbours(end_values)
        return (
            local_part
            + (down_coupling * below_last).reshape(first_extent, second_extent, 1)
            * inverse_block[:, 0]
            + (up_coupling * above_first).reshape(first_extent, second_extent, 1)
            * inverse_block[:, block_len - 1]
        )

    return solve


def apply_operator(iterate, lateral_weight, down_faces, up_faces):
    padded = extended(iterate, (("gx", 0), ("gy", 1), ("gz", 2)), 1)
    lateral = (
        padded[:-2, 1:-1, 1:-1]
        + padded[2:, 1:-1, 1:-1]
        + padded[1:-1, :-2, 1:-1]
        + padded[1:-1, 2:, 1:-1]
    )
    return (
        lateral_weight * (4.0 * iterate - lateral)
        + down_faces * (iterate - padded[1:-1, 1:-1, :-2])
        + up_faces * (iterate - padded[1:-1, 1:-1, 2:])
    )


def restrict(field):
    first_extent, second_extent, depth = field.shape
    return field.reshape(first_extent // 2, 2, second_extent // 2, 2, depth).sum(axis=(1, 3)) * 0.25


def prolong(padded):
    first_extent = padded.shape[0] - 2
    second_extent = padded.shape[1] - 2
    depth = padded.shape[2]
    even_rows = 0.75 * padded[1:-1] + 0.25 * padded[:-2]
    odd_rows = 0.75 * padded[1:-1] + 0.25 * padded[2:]
    widened = jnp.stack([even_rows, odd_rows], 1).reshape(
        2 * first_extent, second_extent + 2, depth
    )
    even_rows = 0.75 * widened[:, 1:-1] + 0.25 * widened[:, :-2]
    odd_rows = 0.75 * widened[:, 1:-1] + 0.25 * widened[:, 2:]
    return jnp.stack([even_rows, odd_rows], 2).reshape(2 * first_extent, 2 * second_extent, depth)


def body(right_side, z_faces, xy_coupling, block_inverse):
    device_index = lax.axis_index("gz")
    levels_count = block_inverse.shape[0]
    last_cell = block_inverse.shape[1] - 1
    corner = jnp.stack(
        [
            block_inverse[:, 0, 0],
            block_inverse[:, 0, last_cell],
            block_inverse[:, last_cell, 0],
            block_inverse[:, last_cell, last_cell],
        ],
        -1,
    )[None]
    corners, firsts = side_by_side((corner, z_faces[:1]), "gz", 0, 1)
    couplings = firsts[1:]
    edge_faces = jnp.concatenate([firsts, jnp.ones((1,), jnp.float32)])
    top_face = lax.dynamic_slice_in_dim(edge_faces, device_index + 1, 1, 0)
    up_faces = jnp.concatenate([z_faces[1:], top_face])
    solvers = [
        make_solver(
            block_inverse[level],
            corners[:, level],
            couplings,
            device_index,
            z_faces[0],
            top_face[0],
        )
        for level in range(levels_count)
    ]

    def operator(iterate, level):
        return apply_operator(iterate, xy_coupling[level], z_faces, up_faces)

    def multigrid_cycle(source, level):
        iterate = damping * solvers[level](source)
        iterate = iterate + damping * solvers[level](source - operator(iterate, level))
        if level == LEVELS - 1:
            return iterate
        coarse = multigrid_cycle(restrict(source - operator(iterate, level)), level + 1)
        widened = extended_2(coarse, (("gx", 0), ("gy", 1)), 1)
        iterate = iterate + prolong(widened)
        for sweep in range(SWEEPS):
            iterate = iterate + damping * solvers[level](source - operator(iterate, level))
        return iterate

    solution = multigrid_cycle(right_side, 0)
    return (solution, right_side - operator(solution, 0))


def solution(mesh):
    return jax.shard_map(
        body,
        mesh=mesh,
        in_specs=(P("gx", "gy", "gz"), P("gz"), P(), P(None, "gz", None)),
        out_specs=(P("gx", "gy", "gz"), P("gx", "gy", "gz")),
        check_vma=False,
    )
```

profile of v0, /device:TPU:1, one launch (start us, length us, event | category | flops | bytes accessed | tf_op | source)
XLA Modules:
  0.0 711.7 jit_solution(5164038338720317318)
XLA Ops:
  3.6 6.5 all-to-all-start
  11.1 10.9 %all-gather = f32[8,1,21]{2,1,0:T(1,128)S(1)} all-gather(f32[1,1,21]{2,1,0:T(1,128)S(1)} %maximum_bitcast_fusion.10), channel_id=1, replica_groups=mesh['gx'=4,'gy'=8,'gz'=8] {'gz'}, dimensions={0}, use_global_device_ids=true | all-gather | bytes 756 | tf_op jit(solution)/shard_map/all_gather | solution.py:58
  149.9 5.2 collective-permute-start.20
  184.4 5.5 collective-permute-start.26
  217.2 5.5 collective-permute-start.32
  254.9 5.5 collective-permute-start.38
  271.3 7.9 %all_to_all.90 = f32[8,2,16]{2,1,0:T(2,128)S(1)} all-to-all(f32[8,2,16]{2,1,0:T(2,128)S(1)} %broadcast_in_dim.117), channel_id=1, replica_groups=mesh['gx'=4,'gy'=8,'gz'=8] {'gz'}, dimensions={0} | all-to-all | bytes 2048 | tf_op jit(solution)/shard_map/all_to_all | solution.py:24
  285.9 5.5 collective-permute-start.44
  317.8 5.5 collective-permute-start.50
  334.1 7.9 %all_to_all.91 = f32[8,2,4]{2,1,0:T(2,128)S(1)} all-to-all(f32[8,2,4]{2,1,0:T(2,128)S(1)} %broadcast_in_dim.119), channel_id=1, replica_groups=mesh['gx'=4,'gy'=8,'gz'=8] {'gz'}, dimensions={0} | all-to-all | bytes 512 | tf_op jit(solution)/shard_map/all_to_all | solution.py:24
  351.7 5.5 collective-permute-start.56
  367.6 4.8 collective-permute-start.60
  373.9 5.9 collective-permute-start.62
  386.0 7.9 %all_to_all.92 = f32[8,2,16]{2,1,0:T(2,128)S(1)} all-to-all(f32[8,2,16]{2,1,0:T(2,128)S(1)} %broadcast_in_dim.120), channel_id=1, replica_groups=mesh['gx'=4,'gy'=8,'gz'=8] {'gz'}, dimensions={0} | all-to-all | bytes 2048 | tf_op jit(solution)/shard_map/all_to_all | solution.py:24
  400.6 5.5 collective-permute-start.66
  417.0 7.9 %all_to_all.93 = f32[8,2,16]{2,1,0:T(2,128)S(1)} all-to-all(f32[8,2,16]{2,1,0:T(2,128)S(1)} %broadcast_in_dim.121), channel_id=1, replica_groups=mesh['gx'=4,'gy'=8,'gz'=8] {'gz'}, dimensions={0} | all-to-all | bytes 2048 | tf_op jit(solution)/shard_map/all_to_all | solution.py:24
  434.6 5.5 collective-permute-start.72
  454.0 5.9 collective-permute-start.78
  466.6 7.8 %all_to_all.94 = f32[8,1,128]{2,1,0:T(1,128)S(1)} all-to-all(f32[8,1,128]{2,1,0:T(1,128)S(1)} %reshape.906), channel_id=1, replica_groups=mesh['gx'=4,'gy'=8,'gz'=8] {'gz'}, dimensions={0} | all-to-all | bytes 8192 | tf_op jit(solution)/shard_map/all_to_all | solution.py:24
  481.8 4.7 collective-permute-start.82
  497.8 7.8 %all_to_all.95 = f32[8,1,128]{2,1,0:T(1,128)S(1)} all-to-all(f32[8,1,128]{2,1,0:T(1,128)S(1)} %reshape.908), channel_id=1, replica_groups=mesh['gx'=4,'gy'=8,'gz'=8] {'gz'}, dimensions={0} | all-to-all | bytes 8192 | tf_op jit(solution)/shard_map/all_to_all | solution.py:24
  516.1 5.5 collective-permute-start.88
  534.9 5.6 collective-permute-start.94
  548.3 7.9 %all_to_all.96 = f32[8,2,256]{2,1,0:T(2,128)S(1)} all-to-all(f32[8,2,256]{2,1,0:T(2,128)S(1)} %broadcast_in_dim.124), channel_id=1, replica_groups=mesh['gx'=4,'gy'=8,'gz'=8] {'gz'}, dimensions={0} | all-to-all | bytes 32768 | tf_op jit(solution)/shard_map/all_to_all | solution.py:24
  563.0 4.7 collective-permute-start.98
  580.3 7.9 %all_to_all.97 = f32[8,2,256]{2,1,0:T(2,128)S(1)} all-to-all(f32[8,2,256]{2,1,0:T(2,128)S(1)} %broadcast_in_dim.125), channel_id=1, replica_groups=mesh['gx'=4,'gy'=8,'gz'=8] {'gz'}, dimensions={0} | all-to-all | bytes 32768 | tf_op jit(solution)/shard_map/all_to_all | solution.py:24
  598.0 5.5 collective-permute-start.104
  617.6 5.7 collective-permute-start.110
  636.1 8.1 %all_to_all.98 = f32[8,2,1024]{2,1,0:T(2,128)S(1)} all-to-all(f32[8,2,1024]{2,1,0:T(2,128)S(1)} %broadcast_in_dim.126), channel_id=1, replica_groups=mesh['gx'=4,'gy'=8,'gz'=8] {'gz'}, dimensions={0} | all-to-all | bytes 131072 | tf_op jit(solution)/shard_map/all_to_all | solution.py:24
  645.7 4.7 collective-permute-start.114
  673.7 8.1 %all_to_all.99 = f32[8,2,1024]{2,1,0:T(2,128)S(1)} all-to-all(f32[8,2,1024]{2,1,0:T(2,128)S(1)} %broadcast_in_dim.127), channel_id=1, replica_groups=mesh['gx'=4,'gy'=8,'gz'=8] {'gz'}, dimensions={0} | all-to-all | bytes 131072 | tf_op jit(solution)/shard_map/all_to_all | solution.py:24
  683.3 5.5 collective-permute-start.120
  (732 shorter events, 503.9 us)
Async XLA Ops:
  3.6 40.9 %all-to-all-start = ((f32[8,2,1024]{2,1,0:T(2,128)}), f32[8,2,1024]{2,1,0:T(2,128)S(1)}, u32[]{:S(2)}, u32[]{:S(2)}) async-start(f32[8,2,1024]{2,1,0:T(2,128)} %broadcast_in_dim.110), calls=%async_computation | async-start | bytes 131072 | tf_op jit(solution)/shard_map/all_to_all | solution.py:24
  50.5 16.9 %collective-permute-start = (f32[1,32,128]{2,1,0:T(8,128)S(1)}, f32[1,32,128]{2,1,0:T(8,128)S(1)}, u32[]{:S(2)}, u32[]{:S(2)}) collective-permute-start(f32[1,32,128]{2,1,0:T(8,128)S(1)} %get-tuple-element.119), channel_id=1, source_target_pairs={{0,64},{64,128},{128,192},{1,65},{65,129},{129,193},{2,66},{66,130... | collective-permute-start | bytes 49160 | tf_op jit(solution)/shard_map/ppermute | solution.py:41
  85.7 19.5 %collective-permute-start.6 = (f32[1,32,128]{2,1,0:T(8,128)S(1)}, f32[1,32,128]{2,1,0:T(8,128)S(1)}, u32[]{:S(2)}, u32[]{:S(2)}) collective-permute-start(f32[1,32,128]{2,1,0:T(8,128)S(1)} %get-tuple-element.113), channel_id=1, source_target_pairs={{0,64},{64,128},{128,192},{1,65},{65,129},{129,193},{2,66},{66,130... | collective-permute-start | bytes 49160 | tf_op jit(solution)/shard_map/ppermute | solution.py:41
  121.8 16.5 %collective-permute-start.12 = (f32[1,16,128]{2,1,0:T(8,128)S(1)}, f32[1,16,128]{2,1,0:T(8,128)S(1)}, u32[]{:S(2)}, u32[]{:S(2)}) collective-permute-start(f32[1,16,128]{2,1,0:T(8,128)S(1)} %get-tuple-element.156), channel_id=1, source_target_pairs={{0,64},{64,128},{128,192},{1,65},{65,129},{129,193},{2,66},{66,130... | collective-permute-start | bytes 24584 | tf_op jit(solution)/shard_map/ppermute | solution.py:41
  155.2 16.5 %collective-permute-start.18 = (f32[1,16,128]{2,1,0:T(8,128)S(1)}, f32[1,16,128]{2,1,0:T(8,128)S(1)}, u32[]{:S(2)}, u32[]{:S(2)}) collective-permute-start(f32[1,16,128]{2,1,0:T(8,128)S(1)} %get-tuple-element.150), channel_id=1, source_target_pairs={{0,64},{64,128},{128,192},{1,65},{65,129},{129,193},{2,66},{66,130... | collective-permute-start | bytes 24584 | tf_op jit(solution)/shard_map/ppermute | solution.py:41
  184.4 15.7 %collective-permute-start.26 = (f32[8,1,128]{2,1,0:T(1,128)S(1)}, f32[8,1,128]{2,1,0:T(1,128)S(1)}, u32[]{:S(2)}, u32[]{:S(2)}) collective-permute-start(f32[8,1,128]{2,1,0:T(1,128)S(1)} %get-tuple-element.190), channel_id=1, source_target_pairs={{0,8},{8,16},{16,24},{24,32},{32,40},{40,48},{48,56},{1,9},{9,17},... | collective-permute-start | bytes 12296 | tf_op jit(solution)/shard_map/ppermute | solution.py:41
  189.9 15.5 %collective-permute-start.24 = (f32[1,8,128]{2,1,0:T(8,128)S(1)}, f32[1,8,128]{2,1,0:T(8,128)S(1)}, u32[]{:S(2)}, u32[]{:S(2)}) collective-permute-start(f32[1,8,128]{2,1,0:T(8,128)S(1)} %get-tuple-element.188), channel_id=1, source_target_pairs={{0,64},{64,128},{128,192},{1,65},{65,129},{129,193},{2,66},{66,130... | collective-permute-start | bytes 12296 | tf_op jit(solution)/shard_map/ppermute | solution.py:41
  217.2 15.7 %collective-permute-start.32 = (f32[8,1,128]{2,1,0:T(1,128)S(1)}, f32[8,1,128]{2,1,0:T(1,128)S(1)}, u32[]{:S(2)}, u32[]{:S(2)}) collective-permute-start(f32[8,1,128]{2,1,0:T(1,128)S(1)} %get-tuple-element.184), channel_id=1, source_target_pairs={{0,8},{8,16},{16,24},{24,32},{32,40},{40,48},{48,56},{1,9},{9,17},... | collective-permute-start | bytes 12296 | tf_op jit(solution)/shard_map/ppermute | solution.py:41
  222.7 15.5 %collective-permute-start.30 = (f32[1,8,128]{2,1,0:T(8,128)S(1)}, f32[1,8,128]{2,1,0:T(8,128)S(1)}, u32[]{:S(2)}, u32[]{:S(2)}) collective-permute-start(f32[1,8,128]{2,1,0:T(8,128)S(1)} %get-tuple-element.182), channel_id=1, source_target_pairs={{0,64},{64,128},{128,192},{1,65},{65,129},{129,193},{2,66},{66,130... | collective-permute-start | bytes 12296 | tf_op jit(solution)/shard_map/ppermute | solution.py:41
  249.3 20.8 %collective-permute-start.36 = (f32[1,4,128]{2,1,0:T(4,128)S(1)}, f32[1,4,128]{2,1,0:T(4,128)S(1)}, u32[]{:S(2)}, u32[]{:S(2)}) collective-permute-start(f32[1,4,128]{2,1,0:T(4,128)S(1)} %get-tuple-element.231), channel_id=1, source_target_pairs={{0,64},{64,128},{128,192},{1,65},{65,129},{129,193},{2,66},{66,130... | collective-permute-start | bytes 6152 | tf_op jit(solution)/shard_map/ppermute | solution.py:41
  253.6 16.5 %collective-permute-start.37 = (f32[1,4,128]{2,1,0:T(4,128)S(1)}, f32[1,4,128]{2,1,0:T(4,128)S(1)}, u32[]{:S(2)}, u32[]{:S(2)}) collective-permute-start(f32[1,4,128]{2,1,0:T(4,128)S(1)} %get-tuple-element.232), channel_id=1, source_target_pairs={{64,0},{128,64},{192,128},{65,1},{129,65},{193,129},{66,2},{130,66... | collective-permute-start | bytes 6152 | tf_op jit(solution)/shard_map/ppermute | solution.py:42
  280.3 20.8 %collective-permute-start.42 = (f32[1,4,128]{2,1,0:T(4,128)S(1)}, f32[1,4,128]{2,1,0:T(4,128)S(1)}, u32[]{:S(2)}, u32[]{:S(2)}) collective-permute-start(f32[1,4,128]{2,1,0:T(4,128)S(1)} %get-tuple-element.225), channel_id=1, source_target_pairs={{0,64},{64,128},{128,192},{1,65},{65,129},{129,193},{2,66},{66,130... | collective-permute-start | bytes 6152 | tf_op jit(solution)/shard_map/ppermute | solution.py:41
  284.6 16.5 %collective-permute-start.43 = (f32[1,4,128]{2,1,0:T(4,128)S(1)}, f32[1,4,128]{2,1,0:T(4,128)S(1)}, u32[]{:S(2)}, u32[]{:S(2)}) collective-permute-start(f32[1,4,128]{2,1,0:T(4,128)S(1)} %get-tuple-element.226), channel_id=1, source_target_pairs={{64,0},{128,64},{192,128},{65,1},{129,65},{193,129},{66,2},{130,66... | collective-permute-start | bytes 6152 | tf_op jit(solution)/shard_map/ppermute | solution.py:42
  312.2 20.7 %collective-permute-start.48 = (f32[1,2,128]{2,1,0:T(2,128)S(1)}, f32[1,2,128]{2,1,0:T(2,128)S(1)}, u32[]{:S(2)}, u32[]{:S(2)}) collective-permute-start(f32[1,2,128]{2,1,0:T(2,128)S(1)} %get-tuple-element.254), channel_id=1, source_target_pairs={{0,64},{64,128},{128,192},{1,65},{65,129},{129,193},{2,66},{66,130... | collective-permute-start | bytes 3080 | tf_op jit(solution)/shard_map/ppermute | solution.py:41
  316.5 16.4 %collective-permute-start.49 = (f32[1,2,128]{2,1,0:T(2,128)S(1)}, f32[1,2,128]{2,1,0:T(2,128)S(1)}, u32[]{:S(2)}, u32[]{:S(2)}) collective-permute-start(f32[1,2,128]{2,1,0:T(2,128)S(1)} %get-tuple-element.255), channel_id=1, source_target_pairs={{64,0},{128,64},{192,128},{65,1},{129,65},{193,129},{66,2},{130,66... | collective-permute-start | bytes 3080 | tf_op jit(solution)/shard_map/ppermute | solution.py:42
  363.1 21.6 %collective-permute-start.58 = (f32[1,4,128]{2,1,0:T(4,128)S(1)}, f32[1,4,128]{2,1,0:T(4,128)S(1)}, u32[]{:S(2)}, u32[]{:S(2)}) collective-permute-start(f32[1,4,128]{2,1,0:T(4,128)S(1)} %get-tuple-element.213), channel_id=1, source_target_pairs={{0,64},{64,128},{128,192},{1,65},{65,129},{129,193},{2,66},{66,130... | collective-permute-start | bytes 6152 | tf_op jit(solution)/shard_map/ppermute | solution.py:41
  366.3 18.4 %collective-permute-start.59 = (f32[1,4,128]{2,1,0:T(4,128)S(1)}, f32[1,4,128]{2,1,0:T(4,128)S(1)}, u32[]{:S(2)}, u32[]{:S(2)}) collective-permute-start(f32[1,4,128]{2,1,0:T(4,128)S(1)} %get-tuple-element.214), channel_id=1, source_target_pairs={{64,0},{128,64},{192,128},{65,1},{129,65},{193,129},{66,2},{130,66... | collective-permute-start | bytes 6152 | tf_op jit(solution)/shard_map/ppermute | solution.py:42
  395.0 20.8 %collective-permute-start.64 = (f32[1,4,128]{2,1,0:T(4,128)S(1)}, f32[1,4,128]{2,1,0:T(4,128)S(1)}, u32[]{:S(2)}, u32[]{:S(2)}) collective-permute-start(f32[1,4,128]{2,1,0:T(4,128)S(1)} %get-tuple-element.207), channel_id=1, source_target_pairs={{0,64},{64,128},{128,192},{1,65},{65,129},{129,193},{2,66},{66,130... | collective-permute-start | bytes 6152 | tf_op jit(solution)/shard_map/ppermute | solution.py:41
  399.3 16.5 %collective-permute-start.65 = (f32[1,4,128]{2,1,0:T(4,128)S(1)}, f32[1,4,128]{2,1,0:T(4,128)S(1)}, u32[]{:S(2)}, u32[]{:S(2)}) collective-permute-start(f32[1,4,128]{2,1,0:T(4,128)S(1)} %get-tuple-element.208), channel_id=1, source_target_pairs={{64,0},{128,64},{192,128},{65,1},{129,65},{193,129},{66,2},{130,66... | collective-permute-start | bytes 6152 | tf_op jit(solution)/shard_map/ppermute | solution.py:42
  444.9 20.3 %collective-permute-start.74 = (f32[1,8,128]{2,1,0:T(8,128)S(1)}, f32[1,8,128]{2,1,0:T(8,128)S(1)}, u32[]{:S(2)}, u32[]{:S(2)}) collective-permute-start(f32[1,8,128]{2,1,0:T(8,128)S(1)} %get-tuple-element.176), channel_id=1, source_target_pairs={{0,64},{64,128},{128,192},{1,65},{65,129},{129,193},{2,66},{66,130... | collective-permute-start | bytes 12296 | tf_op jit(solution)/shard_map/ppermute | solution.py:41
  447.7 17.5 %collective-permute-start.75 = (f32[1,8,128]{2,1,0:T(8,128)S(1)}, f32[1,8,128]{2,1,0:T(8,128)S(1)}, u32[]{:S(2)}, u32[]{:S(2)}) collective-permute-start(f32[1,8,128]{2,1,0:T(8,128)S(1)} %get-tuple-element.177), channel_id=1, source_target_pairs={{64,0},{128,64},{192,128},{65,1},{129,65},{193,129},{66,2},{130,66... | collective-permute-start | bytes 12296 | tf_op jit(solution)/shard_map/ppermute | solution.py:42
  476.2 20.2 %collective-permute-start.80 = (f32[1,8,128]{2,1,0:T(8,128)S(1)}, f32[1,8,128]{2,1,0:T(8,128)S(1)}, u32[]{:S(2)}, u32[]{:S(2)}) collective-permute-start(f32[1,8,128]{2,1,0:T(8,128)S(1)} %get-tuple-element.170), channel_id=1, source_target_pairs={{0,64},{64,128},{128,192},{1,65},{65,129},{129,193},{2,66},{66,130... | collective-permute-start | bytes 12296 | tf_op jit(solution)/shard_map/ppermute | solution.py:41
  480.5 16.0 %collective-permute-start.81 = (f32[1,8,128]{2,1,0:T(8,128)S(1)}, f32[1,8,128]{2,1,0:T(8,128)S(1)}, u32[]{:S(2)}, u32[]{:S(2)}) collective-permute-start(f32[1,8,128]{2,1,0:T(8,128)S(1)} %get-tuple-element.171), channel_id=1, source_target_pairs={{64,0},{128,64},{192,128},{65,1},{129,65},{193,129},{66,2},{130,66... | collective-permute-start | bytes 12296 | tf_op jit(solution)/shard_map/ppermute | solution.py:42
  526.6 20.2 %collective-permute-start.90 = (f32[1,16,128]{2,1,0:T(8,128)S(1)}, f32[1,16,128]{2,1,0:T(8,128)S(1)}, u32[]{:S(2)}, u32[]{:S(2)}) collective-permute-start(f32[1,16,128]{2,1,0:T(8,128)S(1)} %get-tuple-element.144), channel_id=1, source_target_pairs={{0,64},{64,128},{128,192},{1,65},{65,129},{129,193},{2,66},{66,130... | collective-permute-start | bytes 24584 | tf_op jit(solution)/shard_map/ppermute | solution.py:41
  528.5 18.3 %collective-permute-start.91 = (f32[1,16,128]{2,1,0:T(8,128)S(1)}, f32[1,16,128]{2,1,0:T(8,128)S(1)}, u32[]{:S(2)}, u32[]{:S(2)}) collective-permute-start(f32[1,16,128]{2,1,0:T(8,128)S(1)} %get-tuple-element.145), channel_id=1, source_target_pairs={{64,0},{128,64},{192,128},{65,1},{129,65},{193,129},{66,2},{130,66... | collective-permute-start | bytes 24584 | tf_op jit(solution)/shard_map/ppermute | solution.py:42
  557.4 21.3 %collective-permute-start.96 = (f32[1,16,128]{2,1,0:T(8,128)S(1)}, f32[1,16,128]{2,1,0:T(8,128)S(1)}, u32[]{:S(2)}, u32[]{:S(2)}) collective-permute-start(f32[1,16,128]{2,1,0:T(8,128)S(1)} %get-tuple-element.138), channel_id=1, source_target_pairs={{0,64},{64,128},{128,192},{1,65},{65,129},{129,193},{2,66},{66,130... | collective-permute-start | bytes 24584 | tf_op jit(solution)/shard_map/ppermute | solution.py:41
  561.7 17.1 %collective-permute-start.97 = (f32[1,16,128]{2,1,0:T(8,128)S(1)}, f32[1,16,128]{2,1,0:T(8,128)S(1)}, u32[]{:S(2)}, u32[]{:S(2)}) collective-permute-start(f32[1,16,128]{2,1,0:T(8,128)S(1)} %get-tuple-element.139), channel_id=1, source_target_pairs={{64,0},{128,64},{192,128},{65,1},{129,65},{193,129},{66,2},{130,66... | collective-permute-start | bytes 24584 | tf_op jit(solution)/shard_map/ppermute | solution.py:42
  614.2 19.6 %collective-permute-start.106 = (f32[1,32,128]{2,1,0:T(8,128)S(1)}, f32[1,32,128]{2,1,0:T(8,128)S(1)}, u32[]{:S(2)}, u32[]{:S(2)}) collective-permute-start(f32[1,32,128]{2,1,0:T(8,128)S(1)} %get-tuple-element.107), channel_id=1, source_target_pairs={{0,64},{64,128},{128,192},{1,65},{65,129},{129,193},{2,66},{66,130... | collective-permute-start | bytes 49160 | tf_op jit(solution)/shard_map/ppermute | solution.py:41
  616.1 17.7 %collective-permute-start.107 = (f32[1,32,128]{2,1,0:T(8,128)S(1)}, f32[1,32,128]{2,1,0:T(8,128)S(1)}, u32[]{:S(2)}, u32[]{:S(2)}) collective-permute-start(f32[1,32,128]{2,1,0:T(8,128)S(1)} %get-tuple-element.108), channel_id=1, source_target_pairs={{64,0},{128,64},{192,128},{65,1},{129,65},{193,129},{66,2},{130,66... | collective-permute-start | bytes 49160 | tf_op jit(solution)/shard_map/ppermute | solution.py:42
  651.7 19.7 %collective-permute-start.112 = (f32[1,32,128]{2,1,0:T(8,128)S(1)}, f32[1,32,128]{2,1,0:T(8,128)S(1)}, u32[]{:S(2)}, u32[]{:S(2)}) collective-permute-start(f32[1,32,128]{2,1,0:T(8,128)S(1)} %get-tuple-element.101), channel_id=1, source_target_pairs={{0,64},{64,128},{128,192},{1,65},{65,129},{129,193},{2,66},{66,130... | collective-permute-start | bytes 49160 | tf_op jit(solution)/shard_map/ppermute | solution.py:41
  683.3 16.0 %collective-permute-start.120 = (f32[32,1,128]{2,1,0:T(1,128)S(1)}, f32[32,1,128]{2,1,0:T(1,128)S(1)}, u32[]{:S(2)}, u32[]{:S(2)}) collective-permute-start(f32[32,1,128]{2,1,0:T(1,128)S(1)} %get-tuple-element.97), channel_id=1, source_target_pairs={{0,8},{8,16},{16,24},{24,32},{32,40},{40,48},{48,56},{1,9},{9,17},... | collective-permute-start | bytes 49160 | tf_op jit(solution)/shard_map/ppermute | solution.py:41
  690.0 19.7 %collective-permute-start.118 = (f32[1,32,128]{2,1,0:T(8,128)S(1)}, f32[1,32,128]{2,1,0:T(8,128)S(1)}, u32[]{:S(2)}, u32[]{:S(2)}) collective-permute-start(f32[1,32,128]{2,1,0:T(8,128)S(1)} %get-tuple-element.95), channel_id=1, source_target_pairs={{0,64},{64,128},{128,192},{1,65},{65,129},{129,193},{2,66},{66,130... | collective-permute-start | bytes 49160 | tf_op jit(solution)/shard_map/ppermute | solution.py:41
  (105 other events, 893.0 us)
where the time goes:
time: 718 us; the launch traced here: 712 us
  starting transfers between devices  384 us (53%)
  waiting for transfers between devices  139 us (19%)
  blocking collectives  90.1 us (13%)
  other arithmetic  46.6 us (6%)
  local copies, waits for them, and re-layouts  26.5 us (4%)
  matrix products  21.8 us (3%)
    ppermute x54, starting transfers between devices, extended(): lax.ppermute(last, axis, up)  222 us
    ppermute x54, starting transfers between devices, extended(): lax.ppermute(initial, axis, [(b, a) for a, b in up])  81.8 us
    all_to_all x10, blocking collectives, copy_for_each(): lax.all_to_all(jnp.broadcast_to(value[None], (size, *value.shape)), axis,...  79.2 us
    ppermute x54, waiting for transfers between devices, extended(): lax.ppermute(initial, axis, [(b, a) for a, b in up])  64.5 us
    ppermute x8, starting transfers between devices, extended_2(): lax.ppermute(tail, axis, [(i, (i + 1) % count) for i in range(ends)])  39 us
    all_to_all x8, starting transfers between devices, copy_for_each(): lax.all_to_all(jnp.broadcast_to(value[None], (size, *value.shape)), axis,...  30.5 us
    all_to_all x8, waiting for transfers between devices, copy_for_each(): lax.all_to_all(jnp.broadcast_to(value[None], (size, *value.shape)), axis,...  28.8 us
    ppermute x8, waiting for transfers between devices, extended_2(): lax.ppermute(head, axis, [((i + 1) % count, i) for i in range(ends)])  26.7 us
  transfers between devices with their start and end apart: 132, of which 38 were waited for; matrix products, arithmetic and copies ran while one was open for 4% of the time, Pallas kernels for 0%

commit v1 on v0

v1 whole, which is shorter than its diff:
```python
import functools

import jax
import jax.numpy as jnp
from jax import lax
from jax.experimental import pallas as pl
from jax.experimental.pallas import tpu as pltpu
from jax.sharding import PartitionSpec as P

LEVELS = 5
POWERS = 4
HIGHEST = lax.Precision.HIGHEST
F32 = jnp.float32
VMEM_LIMIT = 56 * 1024 * 1024


def contract(a, b, da, db):
    return lax.dot_general(
        a, b, (((da,), (db,)), ((), ())), precision=HIGHEST, preferred_element_type=F32
    )


def nn(a, b):
    return contract(a, b, 1, 0)


def nt(a, b):
    return contract(a, b, 1, 1)


def tn(a, b):
    return contract(a, b, 0, 0)


def rows(lo, hi, fn, step=4):
    full = (hi - lo) // step
    if full:
        def group(k, carry):
            for q in range(step):
                fn(lo + k * step + q)
            return carry

        lax.fori_loop(0, full, group, 0)
    for i in range(lo + full * step, hi):
        fn(i)


def sublane_index(length):
    return lax.broadcasted_iota(jnp.int32, (length, 128), 0)


def shifted(v, zero_ends):
    n = v.shape[0]
    low, high = pltpu.roll(v, 1, 0), pltpu.roll(v, n - 1, 0)
    if zero_ends:
        at = sublane_index(n)
        low = jnp.where(at > 0, low, 0.0)
        high = jnp.where(at < n - 1, high, 0.0)
    return low, high


class Window:
    def __init__(self, shape, origin=None, grid=None):
        self.x, self.y = shape
        self.whole = origin is None
        if not self.whole:
            self.x0, y0 = origin
            self.nx, ny = grid
            at = sublane_index(self.y) + y0
            self.in_y = jnp.where((at >= 0) & (at < ny), 1.0, 0.0).astype(F32)

    def mask(self, i, v):
        if self.whole:
            return v
        at = self.x0 + i
        inside = jnp.where((at >= 0) & (at < self.nx), 1.0, 0.0).astype(F32)
        return v * (self.in_y * inside)

    def around(self, ref, i):
        low, high = shifted(ref[i], self.whole)
        total = low + high
        if self.whole:
            below = ref[jnp.maximum(i - 1, 0)] * jnp.where(i > 0, 1.0, 0.0).astype(F32)
            above = ref[jnp.minimum(i + 1, self.x - 1)] * jnp.where(i < self.x - 1, 1.0, 0.0).astype(F32)
            return total + (below + above)
        return total + (ref[i - 1] + ref[i + 1])

    def span(self, trim):
        return (0, self.x) if self.whole else (trim, self.x - trim)


def line_powers(field, ends, power_ref, link_ref, count, out_refs):
    for j in range(count):
        value = nt(field, power_ref[j]) + tn(ends, link_ref[j])
        out_refs[j][...] = value.reshape(out_refs[j].shape)


def smoothed_residual(win, field_ref, x1, x2, t, out, trim):
    lo, hi = win.span(trim - 1)

    def inner(i):
        t[i] = 0.32 * x1[i] + win.mask(i, 0.64 * win.around(x2, i))

    rows(lo, hi, inner)
    lo, hi = win.span(trim)

    def outer(i):
        out[i] = 0.04 * field_ref[i] + win.around(t, i)

    rows(lo, hi, outer)


def horner(win, xs, weights, t0, t1, trim):
    src = xs[-1]
    scale = weights[-1]
    buffers = (t0, t1)
    for n, j in enumerate(range(len(xs) - 2, 0, -1)):
        dst = buffers[n % 2]
        lo, hi = win.span(trim - j)

        def one(i, src=src, dst=dst, j=j, scale=scale):
            dst[i] = weights[j] * xs[j][i] + win.mask(i, scale * win.around(src, i))

        rows(lo, hi, one)
        src, scale = dst, 1.0
    return src, scale


def restrict(src, scratch, out, x_at, y_at):
    count_x, count_y = out.shape[0], out.shape[1]
    for i in range(count_x):
        scratch[i] = src[x_at + 2 * i] + src[x_at + 2 * i + 1]
    for i in range(count_x):
        even = scratch[i, pl.ds(y_at, count_y, stride=2), :]
        odd = scratch[i, pl.ds(y_at + 1, count_y, stride=2), :]
        out[i] = (even + odd) * 0.25


def prolong(src, src_whole, out, win, x_from, y_from, count_x, count_y):
    last = src.shape[0] - 1
    for i in range(count_x):
        at = x_from + i
        centre = src[at]
        below = src[at - 1] if at > 0 else jnp.zeros_like(centre)
        above = src[at + 1] if at < last else jnp.zeros_like(centre)
        for odd, other in ((0, below), (1, above)):
            v = 0.75 * centre + 0.25 * other
            low, high = shifted(v, src_whole)
            for parity, side in ((0, low), (1, high)):
                w = 0.75 * v + 0.25 * side
                out[2 * i + odd, pl.ds(parity, count_y, stride=2), :] = w[y_from : y_from + count_y]
    if not win.whole:
        rows(0, 2 * count_x, lambda i: out.__setitem__(i, win.mask(i, out[i])))


def send(out_ref, value):
    for m in range(out_ref.shape[0]):
        out_ref[m] = value


def powers_kernel(g_ref, e_ref, zf_ref, power_ref, ends_ref, link_ref, up_ref, table_ref):
    levels, n = g_ref.shape[0], g_ref.shape[1]
    table_ref[...] = jnp.zeros_like(table_ref)
    link_ref[...] = jnp.zeros_like(link_ref)
    for level in range(levels):
        e = e_ref[level]
        inverse_e = 1.0 / jnp.full((1, n), e, F32)
        one = g_ref[level] * e
        two = nn(one, one)
        three = nn(two, one)
        four = nn(two, two)
        ends = []
        for j, value in enumerate((one, two, three, four)):
            power_ref[level, j] = value
            for s, row in enumerate((value[0:1], value[n - 1 : n])):
                ends_ref[level, 2 * j + s : 2 * j + s + 1] = row
                table_ref[0, 2 * j + s, level : level + 1] = row
                ends.append(row)
        for j in range(POWERS):
            for i in range(j + 1):
                for t in range(2):
                    link_ref[level, j, 2 * i + t : 2 * i + t + 1] = ends[2 * (j - i) + t] * inverse_e
        table_ref[0, 9, level : level + 1] = inverse_e
    table_ref[0, 8] = jnp.broadcast_to(zf_ref[...], (8, n))
    for m in range(1, table_ref.shape[0]):
        table_ref[m] = table_ref[0]
    at = lax.broadcasted_iota(jnp.int32, (1, n), 1)
    up_ref[...] = jnp.zeros_like(up_ref)
    up_ref[0:4] = ends_ref[0, 0:4]
    up_ref[4:5] = jnp.where(at == 0, 1.0, 0.0).astype(F32)
    up_ref[5:6] = jnp.where(at == n - 1, 1.0, 0.0).astype(F32)


def coupling_kernel(where_ref, table_ref, e_ref, zf_ref, om_ref, om_up_ref, m_ref, m_link_ref, held):
    blocks, n = table_ref.shape[0], table_ref.shape[3]
    k_own = where_ref[2]
    wide = (8, n)
    lane = lax.broadcasted_iota(jnp.int32, wide, 1)
    inverse_e = table_ref[0, 9]

    def entry(m, row, column):
        at = 0 if column == 0 else n - 1
        return jnp.broadcast_to(table_ref[m, row][:, at : at + 1], wide)

    corner = [
        [
            [[entry(m, 2 * i + s, t) * inverse_e for t in range(2)] for s in range(2)]
            for m in range(blocks)
        ]
        for i in range(POWERS)
    ]
    face = [entry(m, 8, 0) for m in range(blocks)]

    gain_v, gain_d, gain_p, gain_g = [corner[0][0][1][1]], [None], [None], [None]
    for k in range(1, blocks):
        (a, b), (c, d) = corner[0][k]
        g = face[k]
        gv = g * g * gain_v[k - 1]
        dk = 1.0 / (1.0 - a * gv)
        gain_d.append(dk)
        gain_p.append(dk * b)
        gain_g.append(gv)
        gain_v.append(d + c * gv * gain_p[k])

    def solve(low, high):
        u, pu = [high[0]], [None]
        for k in range(1, blocks):
            (a, b), (c, d) = corner[0][k]
            gu = face[k] * u[k - 1]
            pu.append(gain_d[k] * (low[k] + a * gu))
            u.append(high[k] + c * (gu + gain_g[k] * pu[k]))
        zero = jnp.zeros(wide, F32)
        alpha, beta = [zero] * blocks, [zero] * blocks
        for k in range(blocks - 1, 0, -1):
            p = pu[k] + gain_p[k] * beta[k]
            beta[k - 1] = face[k] * p
            alpha[k] = face[k] * (u[k - 1] + gain_v[k - 1] * beta[k - 1])
        return alpha, beta

    unit = [
        [jnp.where(lane == 8 * m + s, 1.0, 0.0).astype(F32) for m in range(blocks)] for s in range(2)
    ]
    response = [solve(unit[0], unit[1])]
    for i in range(1, POWERS):
        source = [[None] * blocks, [None] * blocks]
        for m in range(blocks):
            for s in range(2):
                total = None
                for q in range(i):
                    c = corner[i - q][m][s]
                    term = c[0] * response[q][0][m] + c[1] * response[q][1][m]
                    total = term if total is None else total + term
                source[s][m] = total
        response.append(solve(source[0], source[1]))
    for i in range(POWERS):
        for t in range(2):
            for m in range(blocks):
                held[m, 2 * i + t] = response[i][t][m]
    om_ref[...] = jnp.zeros_like(om_ref)
    for i in range(POWERS):
        for t in range(2):
            total = held[k_own, 2 * i + t]
            for j in range(1, i + 1):
                total = total + pltpu.roll(held[k_own, 2 * (i - j) + t], 2 * j, 1)
            for level in range(LEVELS):
                om_ref[level, 2 * i + t : 2 * i + t + 1] = total[level : level + 1]
    om_up_ref[...] = om_ref[0]
    lane = lane[0:1]
    om_up_ref[4:5] = jnp.where((lane == 8 * (k_own - 1) + 5) & (k_own > 0), 1.0, 0.0).astype(F32)
    om_up_ref[5:6] = jnp.where((lane == 8 * (k_own + 1) + 4) & (k_own < blocks - 1), 1.0, 0.0).astype(F32)
    om_up_ref[6:8] = jnp.zeros((2, n), F32)

    above = jnp.minimum(k_own + 1, blocks - 1)
    top = table_ref[above, 8][0:1, 0:1]
    top = jnp.where(jnp.full((1, 1), k_own, jnp.int32) < blocks - 1, top, 1.0)
    down = zf_ref[...]
    up = jnp.where(lane == n - 1, jnp.broadcast_to(top, (1, n)), pltpu.roll(down, n - 1, 1))
    row = lax.broadcasted_iota(jnp.int32, (n, n), 0)
    column = lax.broadcasted_iota(jnp.int32, (n, n), 1)
    down_all, up_all = jnp.broadcast_to(down, (n, n)), jnp.broadcast_to(up, (n, n))
    m_ref[...] = jnp.where(
        row == column,
        down_all + up_all + 4.0 * e_ref[0],
        jnp.where(row == column - 1, -down_all, jnp.where(row == column + 1, -up_all, 0.0)),
    )
    m_link_ref[...] = jnp.zeros_like(m_link_ref)
    m_link_ref[4:5] = jnp.where(lane == 0, -down, 0.0)
    m_link_ref[5:6] = jnp.where(lane == n - 1, -up, 0.0)


def flat(ref):
    return ref[...].reshape(ref.shape[0] * ref.shape[1], ref.shape[2])


def ends_kernel(f_ref, v_ref, out_ref):
    send(out_ref, nt(v_ref[...], flat(f_ref)))


def ends_from(om_ref, got_ref):
    return nn(om_ref[:, : got_ref.shape[0]], got_ref[...])


def down_kernel(halo, grid, where_ref, f_ref, got_ref, om_ref, power_ref, link_ref, out_ref, x1, x2, t, r, pair):
    hx, hy = halo
    sx, sy = f_ref.shape[0] - 2 * hx, f_ref.shape[1] - 2 * hy
    win = Window(f_ref.shape[:2], (where_ref[0] * sx - hx, where_ref[1] * sy - hy), grid)
    ends = ends_from(om_ref, got_ref)
    line_powers(flat(f_ref), ends, power_ref, link_ref, 2, (x1, x2))
    smoothed_residual(win, f_ref, x1, x2, t, r, hx)
    restrict(r, pair, out_ref, hx, hy)


KNOWN = (0.9984, 0.9728, 0.8192, 0.4096)
TWICE = (0.0016, 0.0256, 0.1536, 0.4096, 0.4096)


def known_kernel(
    halo, trim, grid, twice, where_ref, e_ref, f_ref, got_ref, om_ref, power_ref, link_ref, *rest
):
    hx, hy = halo
    level = 0 if twice else 1
    outs, (x1, x2, x3, x4, t0, t1) = rest[:-6], rest[-6:]
    sx, sy = f_ref.shape[0] - 2 * hx, f_ref.shape[1] - 2 * hy
    win = Window(f_ref.shape[:2], (where_ref[0] * sx - hx, where_ref[1] * sy - hy), grid)
    ends = ends_from(om_ref, got_ref)
    xs = (x1, x2, x3, x4)
    line_powers(flat(f_ref), ends, power_ref, link_ref, POWERS, xs)
    inverse_e = 1.0 / jnp.full((f_ref.shape[1], 128), e_ref[level], F32)
    src, scale = horner(win, xs, KNOWN, t0, t1, trim)
    lo, hi = win.span(trim)
    if twice:
        known_out, twice_out = outs

        def known(i):
            v = (KNOWN[0] * x1[i] + scale * win.around(src, i)) * inverse_e
            known_out[i - hx] = v[hy : hy + sy]

        rows(lo, hi, known)
        src2, scale2 = horner(win, (f_ref,) + xs, TWICE, t0, t1, trim)

        def again(i):
            v = TWICE[0] * f_ref[i] + scale2 * win.around(src2, i)
            twice_out[i - hx] = v[hy : hy + sy]

        rows(lo, hi, again)
    else:
        (known_out,) = outs
        known_out[...] = jnp.zeros_like(known_out)

        def known(i):
            v = (KNOWN[0] * x1[i] + scale * win.around(src, i)) * inverse_e
            known_out[i] = win.mask(i, v)

        rows(lo, hi, known)


def spread_kernel(parts_ref, v_ref, f_ref, out_ref):
    many, sx, sy = parts_ref.shape[:3]
    across = f_ref.shape[1] // sy
    for p in range(many):
        ix, iy = p // across, p % across
        f_ref[ix * sx : (ix + 1) * sx, iy * sy : (iy + 1) * sy] = parts_ref[p]
    send(out_ref, nt(v_ref[...], flat(f_ref)))


def whole_down_kernel(
    level, region, where_ref, e_ref, f_ref, got_ref, om_ref, power_ref, link_ref, v_ref,
    coarse_ref, out_ref, known_ref, x1, x2, x3, x4, t0, t1, pair, *padded
):
    win = Window(f_ref.shape[:2])
    ends = ends_from(om_ref, got_ref)
    xs = (x1, x2, x3, x4)
    line_powers(flat(f_ref), ends, power_ref, link_ref, POWERS, xs)
    smoothed_residual(win, f_ref, x1, x2, t0, t1, 2)
    restrict(t1, pair, coarse_ref, 0, 0)
    send(out_ref, nt(v_ref[...], flat(coarse_ref)))
    inverse_e = 1.0 / jnp.full((f_ref.shape[1], 128), e_ref[level], F32)
    src, scale = horner(win, xs, KNOWN, t0, t1, 4)
    if region is None:
        def known(i):
            known_ref[i] = (KNOWN[0] * x1[i] + scale * win.around(src, i)) * inverse_e

        rows(0, win.x, known)
    else:
        (pad,) = padded
        margin = region
        clear_edges(pad, margin)

        def known(i):
            v = (KNOWN[0] * x1[i] + scale * win.around(src, i)) * inverse_e
            pad[i + margin, margin : margin + win.y] = v

        rows(0, win.x, known)
        cut(where_ref, pad, known_ref, margin)


def clear_edges(pad, margin):
    x, y = pad.shape[:2]
    zero_rows = jnp.zeros((margin, y, 128), F32)
    zero_cols = jnp.zeros((x, margin, 128), F32)
    pad[0:margin] = zero_rows
    pad[x - margin : x] = zero_rows
    pad[:, 0:margin] = zero_cols
    pad[:, y - margin : y] = zero_cols


def cut(where_ref, pad, out_ref, margin):
    sx, sy = out_ref.shape[0] - 2 * margin, out_ref.shape[1] - 2 * margin
    x_at = where_ref[0] * sx
    y_at = pl.multiple_of(where_ref[1] * sy, 8)

    def one(i):
        out_ref[i] = pad[x_at + i, pl.ds(y_at, out_ref.shape[1]), :]

    rows(0, out_ref.shape[0], one)


def bottom_kernel(e_ref, f_ref, got_ref, om_ref, power_ref, link_ref, v_ref, w_ref, out_ref, x1, x2, c):
    win = Window(f_ref.shape[:2])
    ends = ends_from(om_ref, got_ref)
    line_powers(flat(f_ref), ends, power_ref, link_ref, 2, (x1, x2))
    inverse_e = 1.0 / jnp.full((f_ref.shape[1], 128), e_ref[LEVELS - 1], F32)

    def one(i):
        c[i] = (0.96 * x1[i] + 0.64 * win.around(x2, i)) * inverse_e

    rows(0, win.x, one)
    prolong(c, True, w_ref, Window(w_ref.shape[:2]), 0, 0, win.x, win.y)
    send(out_ref, nt(v_ref[...], flat(w_ref)))


def corrected(win, w_ref, known_ref, x1, x2, t, c, trim):
    smoothed_residual(win, w_ref, x1, x2, t, c, trim)
    lo, hi = win.span(trim)

    def add(i):
        c[i] = win.mask(i, c[i] + known_ref[i])

    rows(lo, hi, add)


def whole_up_kernel(
    margin, where_ref, w_ref, known_ref, got_ref, om_ref, power_ref, link_ref, v_ref,
    fine_ref, out_ref, x1, x2, t, c, fine, pad
):
    win = Window(w_ref.shape[:2])
    ends = ends_from(om_ref, got_ref)
    line_powers(flat(w_ref), ends, power_ref, link_ref, 2, (x1, x2))
    corrected(win, w_ref, known_ref, x1, x2, t, c, 2)
    prolong(c, True, fine, Window(fine.shape[:2]), 0, 0, win.x, win.y)
    clear_edges(pad, margin)

    def place(i):
        pad[i + margin, margin : margin + fine.shape[1]] = fine[i]

    rows(0, fine.shape[0], place)
    cut(where_ref, pad, fine_ref, margin)
    send(out_ref, nt(v_ref[...], flat(fine_ref)))


def up_kernel(
    halo, fine_halo, grid, where_ref, w_ref, known_ref, got_ref, om_ref, power_ref, link_ref, v_ref,
    fine_ref, out_ref, x1, x2, t, c
):
    hx, hy = halo
    fx, fy = fine_halo
    sx, sy = w_ref.shape[0] - 2 * hx, w_ref.shape[1] - 2 * hy
    ix, iy = where_ref[0], where_ref[1]
    win = Window(w_ref.shape[:2], (ix * sx - hx, iy * sy - hy), grid)
    fine_win = Window(
        fine_ref.shape[:2], (2 * ix * sx - fx, 2 * iy * sy - fy), (2 * grid[0], 2 * grid[1])
    )
    ends = ends_from(om_ref, got_ref)
    line_powers(flat(w_ref), ends, power_ref, link_ref, 2, (x1, x2))
    c[...] = jnp.zeros_like(c)
    corrected(win, w_ref, known_ref, x1, x2, t, c, 2)
    odd = fx % 2
    count_x = (fine_ref.shape[0] + 2 * odd) // 2
    if odd:
        x_from = hx - (fx + 1) // 2
        prolong_odd(c, fine_ref, fine_win, x_from, hy - fy // 2, count_x, fine_ref.shape[1] // 2)
    else:
        prolong(c, False, fine_ref, fine_win, hx - fx // 2, hy - fy // 2, count_x, fine_ref.shape[1] // 2)
    send(out_ref, nt(v_ref[...], flat(fine_ref)))


def prolong_odd(src, out, win, x_from, y_from, count_x, count_y):
    for i in range(count_x):
        at = x_from + i
        for odd, other in ((0, at - 1), (1, at + 1)):
            row = 2 * i + odd - 1
            if row < 0 or row >= out.shape[0]:
                continue
            v = 0.75 * src[at] + 0.25 * src[other]
            low, high = shifted(v, False)
            for parity, side in ((0, low), (1, high)):
                w = 0.75 * v + 0.25 * side
                out[row, pl.ds(parity, count_y, stride=2), :] = w[y_from : y_from + count_y]
    rows(0, out.shape[0], lambda i: out.__setitem__(i, win.mask(i, out[i])))


def final_kernel(
    halo, grid, where_ref, e_ref, w_ref, known_ref, twice_ref, got_ref, om_ref, power_ref, link_ref,
    m_ref, m_link_ref, u_ref, r_ref, x1, x2, xm, t0, t1
):
    hx, hy = halo
    sx, sy = w_ref.shape[0] - 2 * hx, w_ref.shape[1] - 2 * hy
    win = Window(w_ref.shape[:2], (where_ref[0] * sx - hx, where_ref[1] * sy - hy), grid)
    ends = ends_from(om_ref, got_ref)
    field = flat(w_ref)
    line_powers(field, ends, power_ref, link_ref, 2, (x1, x2))
    xm[...] = (nt(field, m_ref[...]) + tn(ends, m_link_ref[...])).reshape(xm.shape)
    e = e_ref[0]

    def first(i):
        t0[i] = win.mask(i, win.around(x2, i))

    lo, hi = win.span(hx - 2)
    rows(lo, hi, first)

    def second(i):
        t1[i] = (0.32 * e) * x1[i] - (0.64 * e) * t0[i]

    rows(lo, hi, second)
    lo, hi = win.span(hx - 1)

    def fourth(i):
        x2[i] = (0.28 * e) * w_ref[i] + win.mask(i, win.around(t1, i))

    rows(lo, hi, fourth)

    def fifth(i):
        t0[i] = 0.32 * x1[i] + 0.64 * t0[i]

    rows(lo, hi, fifth)
    lo, hi = win.span(hx)

    def last(i):
        at = i - hx
        u = 0.04 * w_ref[i] + win.around(t0, i)
        u_ref[at] = known_ref[at] + u[hy : hy + sy]
        r = 0.04 * xm[i] + win.around(x2, i)
        r_ref[at] = twice_ref[at] - r[hy : hy + sy]

    rows(lo, hi, last)


def call(kernel, outs, scratch, smem, *args, flops=0):
    specs = [
        pl.BlockSpec(memory_space=pltpu.SMEM if k in smem else pltpu.VMEM) for k in range(len(args))
    ]
    out_specs = [pl.BlockSpec(memory_space=pltpu.VMEM) for _ in outs]
    return pl.pallas_call(
        kernel,
        out_shape=[jax.ShapeDtypeStruct(s, F32) for s in outs],
        in_specs=specs,
        out_specs=out_specs,
        scratch_shapes=[pltpu.VMEM(s, F32) for s in scratch],
        compiler_params=pltpu.CompilerParams(vmem_limit_bytes=VMEM_LIMIT),
        cost_estimate=pl.CostEstimate(flops=int(flops) or 1000000, bytes_accessed=1000000, transcendentals=0),
    )(*args)


def exchange(copies, axes="gz"):
    got = lax.all_to_all(copies, axes, 0, 0, tiled=True)
    return got


def stacked(copies):
    got = exchange(copies)
    return got.reshape(got.shape[0] * got.shape[1], got.shape[2])


def with_halo(value, width_x, width_y):
    def both(v, axis, dim, width):
        size, length = lax.axis_size(axis), v.shape[dim]
        up = [(i, i + 1) for i in range(size - 1)]
        last = lax.slice_in_dim(v, length - width, length, axis=dim)
        first = lax.slice_in_dim(v, 0, width, axis=dim)
        low = lax.ppermute(last, axis, up)
        high = lax.ppermute(first, axis, [(b, a) for a, b in up])
        return jnp.concatenate([low, v, high], axis=dim)

    return both(both(value, "gy", 1, width_y), "gx", 0, width_x)


def body(right_side, z_faces, xy_coupling, block_inverse):
    part = functools.partial
    gx, gy, gz = (lax.axis_size(a) for a in ("gx", "gy", "gz"))
    n = z_faces.shape[0]
    where = jnp.stack([lax.axis_index(a) for a in ("gx", "gy", "gz")]).astype(jnp.int32)
    sx, sy = right_side.shape[0], right_side.shape[1]
    grids = [(gx * (sx >> l), gy * (sy >> l)) for l in range(LEVELS)]
    e = xy_coupling
    faces = z_faces.reshape(1, n)

    power, ends, link, ends_up, table = call(
        powers_kernel,
        [(LEVELS, POWERS, n, n), (LEVELS, 8, n), (LEVELS, POWERS, 8, n), (8, n), (gz, 10, 8, n)],
        [],
        (1,),
        block_inverse, e, faces,
    )
    table = exchange(table)
    om, om_up, m_matrix, m_link = call(
        coupling_kernel,
        [(LEVELS, 8, n), (8, n), (n, n), (8, n)],
        [(gz, 8, 8, n)],
        (0, 2),
        where, table, e, faces,
    )

    h0 = (4, 4)
    ext0 = (sx + 8, sy + 8)
    f0 = with_halo(right_side, 4, 4)
    lines0 = ext0[0] * ext0[1]
    (copies,) = call(ends_kernel, [(gz, 8, lines0)], [], (), f0, ends[0])
    got0 = stacked(copies)
    cube0 = ext0 + (n,)
    (f1,) = call(
        part(down_kernel, h0, grids[0]),
        [(sx // 2, sy // 2, n)],
        [cube0, cube0, cube0, cube0, (sx // 2, ext0[1], n)],
        (0,),
        where, f0, got0, om[0], power[0], link[0],
    )
    known0, twice0 = call(
        part(known_kernel, h0, 4, grids[0], True),
        [(sx, sy, n), (sx, sy, n)],
        [cube0] * 6,
        (0, 1),
        where, e, f0, got0, om[0], power[0], link[0],
        flops=20000000000,
    )

    s1x, s1y = sx // 2, sy // 2
    h1 = (5, 8)
    ext1 = (s1x + 10, s1y + 16)
    cube1 = ext1 + (n,)
    f1 = with_halo(f1, 5, 8)
    (copies,) = call(ends_kernel, [(gz, 8, ext1[0] * ext1[1])], [], (), f1, ends[1])
    got1 = stacked(copies)
    s2x, s2y = s1x // 2, s1y // 2
    (f2,) = call(
        part(down_kernel, h1, grids[1]),
        [(s2x, s2y, n)],
        [cube1, cube1, cube1, cube1, (s2x, ext1[1], n)],
        (0,),
        where, f1, got1, om[1], power[1], link[1],
    )
    (known1,) = call(
        part(known_kernel, h1, 3, grids[1], False),
        [cube1],
        [cube1] * 6,
        (0, 1),
        where, e, f1, got1, om[1], power[1], link[1],
        flops=10000000000,
    )

    many = gx * gy
    parts = lax.all_to_all(
        jnp.broadcast_to(f2[None], (many, s2x, s2y, n)), ("gx", "gy"), 0, 0, tiled=True
    )
    cubes = [g + (n,) for g in grids]
    lines = [g[0] * g[1] for g in grids]
    f2, copies = call(spread_kernel, [cubes[2], (gz, 8, lines[2])], [], (), parts, ends[2])
    margin = 8
    region = (s2x + 2 * margin, s2y + 2 * margin, n)
    padded = (grids[2][0] + 2 * margin, grids[2][1] + 2 * margin, n)
    f3, copies, known2 = call(
        part(whole_down_kernel, 2, margin),
        [cubes[3], (gz, 8, lines[3]), region],
        [cubes[2]] * 6 + [(grids[3][0], grids[2][1], n), padded],
        (0, 1),
        where, e, f2, stacked(copies), om[2], power[2], link[2], ends[3],
    )
    f4, copies, known3 = call(
        part(whole_down_kernel, 3, None),
        [cubes[4], (gz, 8, lines[4]), cubes[3]],
        [cubes[3]] * 6 + [(grids[4][0], grids[3][1], n)],
        (0, 1),
        where, e, f3, stacked(copies), om[3], power[3], link[3], ends[4],
    )
    w3, copies = call(
        bottom_kernel,
        [cubes[3], (gz, 8, lines[3])],
        [cubes[4]] * 3,
        (0,),
        e, f4, stacked(copies), om[4], power[4], link[4], ends[3],
    )
    w2, copies = call(
        part(whole_up_kernel, margin),
        [region, (gz, 8, region[0] * region[1])],
        [cubes[3]] * 4 + [cubes[2], padded],
        (0,),
        where, w3, known3, stacked(copies), om[3], power[3], link[3], ends[2],
    )

    w1, copies = call(
        part(up_kernel, (margin, margin), h1, grids[2]),
        [cube1, (gz, 8, ext1[0] * ext1[1])],
        [region] * 4,
        (0,),
        where, w2, known2, stacked(copies), om[2], power[2], link[2], ends[1],
    )
    w0, copies = call(
        part(up_kernel, h1, h0, grids[1]),
        [cube0, (gz, 8, lines0)],
        [cube1] * 4,
        (0,),
        where, w1, known1, stacked(copies), om[1], power[1], link[1], ends_up,
    )
    u, r = call(
        part(final_kernel, h0, grids[0]),
        [(sx, sy, n), (sx, sy, n)],
        [cube0] * 5,
        (0, 1),
        where, e, w0, known0, twice0, stacked(copies), om_up, power[0], link[0], m_matrix, m_link,
    )
    return u, r


def solution(mesh):
    return jax.shard_map(
        body,
        mesh=mesh,
        in_specs=(P("gx", "gy", "gz"), P("gz"), P(), P(None, "gz", None)),
        out_specs=(P("gx", "gy", "gz"), P("gx", "gy", "gz")),
        check_vma=False,
    )
```

time: 718 us -> 261 us (0.36)
  starting transfers between devices: 384 us -> 39.9 us
  waiting for transfers between devices: 139 us -> 15.4 us
  Pallas kernels: 0 us -> 81 us
  other arithmetic: 46.6 us -> 4.11 us
  matrix products: 21.8 us -> 0 us
  blocking collectives: 90.1 us -> 108 us
  local copies, waits for them, and re-layouts: 26.5 us -> 9.93 us
    ppermute x124 -> x8, starting transfers between devices: 353 us -> 20 us  [the longest x4 14.9 us: both(): low = lax.ppermute(last, axis, up)]
    ppermute x124 -> x8, waiting for transfers between devices: 110 us -> 11.4 us  [the longest x4 11.3 us: both(): high = lax.ppermute(first, axis, [(b, a) for a, b in up])]
    pallas_call x0 -> x16, Pallas kernels: none -> 81 us  [call(): pl.pallas_call(kernel, out_shape=[jax.ShapeDtypeStruct(s, F32) for s in o...]
    all_to_all x10 -> x7, blocking collectives: 79.2 us -> 108 us  [the longest x6 72.2 us: exchange(): got = lax.all_to_all(copies, axes, 0, 0, tiled=True)]
    all_to_all x8 -> x4, waiting for transfers between devices: 28.8 us -> 3.93 us  [exchange(): got = lax.all_to_all(copies, axes, 0, 0, tiled=True)]
    another operation x71 -> x1, other arithmetic: 20.6 us -> 0.6 us  [body(): jnp.stack([lax.axis_index(a) for a in ('gx', 'gy', 'gz')]).astype(jnp.int32)]
    dot_general x36 -> x0, matrix products: 19.8 us -> none  [the longest x18 17.3 us: solve(): jnp.einsum('xyj,ij->xyi', source, inverse_block, precision=highest)]
    mul x23 -> x0, other arithmetic: 13.5 us -> none  [the longest x18 12.8 us: solve(): down_coupling * below_last]
  transfers between devices with their start and end apart: 132 -> 12, of which waited for: 38 -> 6; matrix products, arithmetic and copies ran while one was open for 4% -> 3% of each run, Pallas kernels for 0% -> 9%
where the time goes in v1:
time: 261 us; the launch traced here: 259 us
  blocking collectives  108 us (41%)
  Pallas kernels  81 us (31%)
  starting transfers between devices  39.9 us (15%)
  waiting for transfers between devices  15.4 us (6%)
  local copies, waits for them, and re-layouts  9.93 us (4%)
  other arithmetic  4.11 us (2%)
    pallas_call x16, Pallas kernels, call(): pl.pallas_call(kernel, out_shape=[jax.ShapeDtypeStruct(s, F32) for s in o...  81 us
    all_to_all x6, blocking collectives, exchange(): got = lax.all_to_all(copies, axes, 0, 0, tiled=True)  72.2 us
    all_to_all x1, blocking collectives, body(): lax.all_to_all(jnp.broadcast_to(f2[None], (many, s2x, s2y, n)), ('gx', 'g...  35.4 us
    all_to_all x4, starting transfers between devices, exchange(): got = lax.all_to_all(copies, axes, 0, 0, tiled=True)  19.8 us
    ppermute x4, starting transfers between devices, both(): low = lax.ppermute(last, axis, up)  14.9 us
    ppermute x4, waiting for transfers between devices, both(): high = lax.ppermute(first, axis, [(b, a) for a, b in up])  11.3 us
  transfers between devices with their start and end apart: 12, of which 6 were waited for; matrix products, arithmetic and copies ran while one was open for 3% of the time, Pallas kernels for 9%

profile of v1, /device:TPU:1, one launch (start us, length us, event | category | flops | bytes accessed | tf_op | source)
XLA Modules:
  0.0 258.6 jit_solution(7098015282514402703)
XLA Ops:
  1.6 4.4 %collective-permute-start = (f32[32,4,128]{2,1,0:T(4,128)S(1)}, f32[32,4,128]{2,1,0:T(4,128)S(1)}, u32[]{:S(2)}, u32[]{:S(2)}) collective-permute-start(f32[32,4,128]{2,1,0:T(4,128)S(1)} %get-tuple-element.63), channel_id=1, source_target_pairs={{0,8},{8,16},{16,24},{24,32},{32,40},{40,48},{48,56},{1,9},{9,17},... | collective-permute-start | bytes 196616 | tf_op jit(solution)/shard_map/ppermute | solution.py:580
  7.3 3.9 %shard_map.59 = (f32[5,4,128,128]{3,2,1,0:T(8,128)}, f32[5,8,128]{2,1,0:T(8,128)}, f32[5,4,8,128]{3,2,1,0:T(8,128)}, f32[8,128]{1,0:T(8,128)}, f32[8,10,8,128]{3,2,1,0:T(8,128)}) custom-call(f32[5,128,128]{2,1,0:T(8,128)} %g_ref.1, f32[5]{0:T(128)} %e_ref.15, f32[1,128]{1,0:T(1,128)} %bitcast.64), custom_call_target="tpu_custom_call" | custom-call | flops 1000000 | bytes 1000000 | tf_op jit(solution)/shard_map/pallas_call | solution.py:553
  11.2 5.4 %all-to-all-start.1 = ((f32[8,10,8,128]{3,2,1,0:T(8,128)}), f32[8,10,8,128]{3,2,1,0:T(8,128)S(1)}, u32[]{:S(2)}, u32[]{:S(2)}) async-start(f32[8,10,8,128]{3,2,1,0:T(8,128)} %get-tuple-element.30), calls=%async_computation.1 | async-start | bytes 655360 | tf_op jit(solution)/shard_map/all_to_all | solution.py:565
  19.1 3.1 %collective-permute-start.2 = (f32[4,40,128]{2,1,0:T(8,128)S(1)}, f32[4,40,128]{2,1,0:T(8,128)S(1)}, u32[]{:S(2)}, u32[]{:S(2)}) collective-permute-start(f32[4,40,128]{2,1,0:T(8,128)S(1)} %get-tuple-element.61), channel_id=1, source_target_pairs={{0,64},{64,128},{128,192},{1,65},{65,129},{129,193},{2,66},{66,130... | collective-permute-start | bytes 245768 | tf_op jit(solution)/shard_map/ppermute | solution.py:580
  24.1 3.7 %collective-permute-done.3 = f32[4,40,128]{2,1,0:T(8,128)S(1)} collective-permute-done((f32[4,40,128]{2,1,0:T(8,128)S(1)}, f32[4,40,128]{2,1,0:T(8,128)S(1)}, u32[]{:S(2)}, u32[]{:S(2)}) %collective-permute-start.3) | collective-permute-done | bytes 81952 | tf_op jit(solution)/shard_map/ppermute | solution.py:581
  31.5 5.8 %all-to-all-start = ((f32[8,8,1600]{2,1,0:T(8,128)}), f32[8,8,1600]{2,1,0:T(8,128)S(1)}, u32[]{:S(2)}, u32[]{:S(2)}) async-start(f32[8,8,1600]{2,1,0:T(8,128)} %shard_map.60), calls=%async_computation | async-start | bytes 851968 | tf_op jit(solution)/shard_map/all_to_all | solution.py:565
  42.0 3.3 %all-to-all-done = f32[8,8,1600]{2,1,0:T(8,128)S(1)} async-done(((f32[8,8,1600]{2,1,0:T(8,128)}), f32[8,8,1600]{2,1,0:T(8,128)S(1)}, u32[]{:S(2)}, u32[]{:S(2)}) %all-to-all-start) | async-done | bytes 409632 | tf_op jit(solution)/shard_map/all_to_all | solution.py:565
  46.1 5.6 %shard_map.62 = f32[16,16,128]{2,1,0:T(8,128)} custom-call(s32[3]{0:T(128)} %pad_add_fusion.where_ref, f32[40,40,128]{2,1,0:T(8,128)} %pad_maximum_fusion.f_ref, f32[64,1600]{1,0:T(8,128)} %bitcast.55, f32[8,128]{1,0:T(8,128)} %get-tuple-element.78.om_ref, f32[4,128,128]{2,1,0:T(8,128)} %get-tuple-element.60.power_ref, f32[4,8,128]{2,1,0:T(8,128)} %get-tuple-element.73.link_ref), custom_call_target="tpu_custom_call" | custom-call | flops 1000000 | bytes 1000000 | tf_op jit(solution)/shard_map/pallas_call | solution.py:553
  52.6 4.3 %collective-permute-start.4 = (f32[16,8,128]{2,1,0:T(8,128)S(1)}, f32[16,8,128]{2,1,0:T(8,128)S(1)}, u32[]{:S(2)}, u32[]{:S(2)}) collective-permute-start(f32[16,8,128]{2,1,0:T(8,128)S(1)} %get-tuple-element.67), channel_id=1, source_target_pairs={{0,8},{8,16},{16,24},{24,32},{32,40},{40,48},{48,56},{1,9},{9,17},... | collective-permute-start | bytes 196616 | tf_op jit(solution)/shard_map/ppermute | solution.py:580
  58.2 3.9 %collective-permute-done.5 = f32[16,8,128]{2,1,0:T(8,128)S(1)} collective-permute-done((f32[16,8,128]{2,1,0:T(8,128)S(1)}, f32[16,8,128]{2,1,0:T(8,128)S(1)}, u32[]{:S(2)}, u32[]{:S(2)}) %collective-permute-start.5) | collective-permute-done | bytes 65568 | tf_op jit(solution)/shard_map/ppermute | solution.py:581
  62.9 3.1 %collective-permute-start.6 = (f32[5,32,128]{2,1,0:T(8,128)S(1)}, f32[5,32,128]{2,1,0:T(8,128)S(1)}, u32[]{:S(2)}, u32[]{:S(2)}) collective-permute-start(f32[5,32,128]{2,1,0:T(8,128)S(1)} %get-tuple-element.65), channel_id=1, source_target_pairs={{0,64},{64,128},{128,192},{1,65},{65,129},{129,193},{2,66},{66,130... | collective-permute-start | bytes 245768 | tf_op jit(solution)/shard_map/ppermute | solution.py:580
  67.5 3.7 %collective-permute-done.7 = f32[5,32,128]{2,1,0:T(8,128)S(1)} collective-permute-done((f32[5,32,128]{2,1,0:T(8,128)S(1)}, f32[5,32,128]{2,1,0:T(8,128)S(1)}, u32[]{:S(2)}, u32[]{:S(2)}) %collective-permute-start.7) | collective-permute-done | bytes 81952 | tf_op jit(solution)/shard_map/ppermute | solution.py:581
  75.1 14.1 %all_to_all.55 = f32[8,8,832]{2,1,0:T(8,128)} all-to-all(f32[8,8,832]{2,1,0:T(8,128)} %shard_map.63), channel_id=1, replica_groups=mesh['gx'=4,'gy'=8,'gz'=8] {'gz'}, dimensions={0} | all-to-all | bytes 425984 | tf_op jit(solution)/shard_map/all_to_all | solution.py:565
  89.2 3.8 %shard_map.64 = f32[8,8,128]{2,1,0:T(8,128)} custom-call(s32[3]{0:T(128)} %pad_add_fusion.where_ref, f32[26,32,128]{2,1,0:T(8,128)} %pad_maximum_fusion.1.f_ref, f32[64,832]{1,0:T(8,128)} %bitcast.58, f32[8,128]{1,0:T(8,128)} %get-tuple-element.77.om_ref, f32[4,128,128]{2,1,0:T(8,128)} %get-tuple-element.59.power_ref, f32[4,8,128]{2,1,0:T(8,128)} %get-tuple-element.72.link_ref), custom_call_target="tpu_custom_call" | custom-call | flops 1000000 | bytes 1000000 | tf_op jit(solution)/shard_map/pallas_call | solution.py:553
  93.9 35.4 %all_to_all.56.parts_ref = f32[32,8,8,128]{3,2,1,0:T(8,128)} all-to-all(f32[32,8,8,128]{3,2,1,0:T(8,128)S(1)} %broadcast_in_dim.2), channel_id=1, replica_groups=mesh['gx'=4,'gy'=8,'gz'=8] {'gx','gy'}, dimensions={0} | all-to-all | bytes 2097152 | tf_op jit(solution)/shard_map/all_to_all | solution.py:661
  129.3 3.0 %shard_map.65 = (f32[32,64,128]{2,1,0:T(8,128)}, f32[8,8,2048]{2,1,0:T(8,128)}) custom-call(f32[32,8,8,128]{3,2,1,0:T(8,128)} %all_to_all.56.parts_ref, f32[8,128]{1,0:T(8,128)} %get-tuple-element.81.v_ref), custom_call_target="tpu_custom_call" | custom-call | flops 1000000 | bytes 1000000 | tf_op jit(solution)/shard_map/pallas_call | solution.py:553
  132.2 18.0 %all_to_all.57 = f32[8,8,2048]{2,1,0:T(8,128)} all-to-all(f32[8,8,2048]{2,1,0:T(8,128)} %get-tuple-element.35), channel_id=1, replica_groups=mesh['gx'=4,'gy'=8,'gz'=8] {'gz'}, dimensions={0} | all-to-all | bytes 1048576 | tf_op jit(solution)/shard_map/all_to_all | solution.py:565
  150.3 12.0 %shard_map.66 = (f32[16,32,128]{2,1,0:T(8,128)}, f32[8,8,512]{2,1,0:T(8,128)}, f32[24,24,128]{2,1,0:T(8,128)}) custom-call(s32[3]{0:T(128)} %pad_add_fusion.where_ref, f32[5]{0:T(128)} %e_ref.15, f32[32,64,128]{2,1,0:T(8,128)} %get-tuple-element.34.f_ref, f32[64,2048]{1,0:T(8,128)} %bitcast.53, f32[8,128]{1,0:T(8,128)} %get-tuple-element.76.om_ref, ...), custom_call_target="tpu_custom_call" | custom-call | flops 1000000 | bytes 1000000 | tf_op jit(solution)/shard_map/pallas_call | solution.py:553
  162.3 10.3 %all_to_all.58 = f32[8,8,512]{2,1,0:T(8,128)} all-to-all(f32[8,8,512]{2,1,0:T(8,128)} %get-tuple-element.37), channel_id=1, replica_groups=mesh['gx'=4,'gy'=8,'gz'=8] {'gz'}, dimensions={0} | all-to-all | bytes 262144 | tf_op jit(solution)/shard_map/all_to_all | solution.py:565
  172.5 4.9 %shard_map.67 = (f32[8,16,128]{2,1,0:T(8,128)}, f32[8,8,128]{2,1,0:T(8,128)}, f32[16,32,128]{2,1,0:T(8,128)}) custom-call(s32[3]{0:T(128)} %pad_add_fusion.where_ref, f32[5]{0:T(128)} %e_ref.15, f32[16,32,128]{2,1,0:T(8,128)} %get-tuple-element.36.f_ref, f32[64,512]{1,0:T(8,128)} %bitcast.62, f32[8,128]{1,0:T(8,128)} %get-tuple-element.75.om_ref, ...), custom_call_target="tpu_custom_call" | custom-call | flops 1000000 | bytes 1000000 | tf_op jit(solution)/shard_map/pallas_call | solution.py:553
  177.4 9.5 %all_to_all.59 = f32[8,8,128]{2,1,0:T(8,128)} all-to-all(f32[8,8,128]{2,1,0:T(8,128)} %get-tuple-element.39), channel_id=1, replica_groups=mesh['gx'=4,'gy'=8,'gz'=8] {'gz'}, dimensions={0} | all-to-all | bytes 65536 | tf_op jit(solution)/shard_map/all_to_all | solution.py:565
  186.9 2.9 %shard_map.68 = (f32[16,32,128]{2,1,0:T(8,128)}, f32[8,8,512]{2,1,0:T(8,128)}) custom-call(f32[5]{0:T(128)} %e_ref.15, f32[8,16,128]{2,1,0:T(8,128)} %get-tuple-element.38.f_ref, f32[64,128]{1,0:T(8,128)} %bitcast.63, f32[8,128]{1,0:T(8,128)} %get-tuple-element.74.om_ref, f32[4,128,128]{2,1,0:T(8,128)} %get-tuple-element.56.power_ref, ...), custom_call_target="tpu_custom_call" | custom-call | flops 1000000 | bytes 1000000 | tf_op jit(solution)/shard_map/pallas_call | solution.py:553
  189.8 9.9 %all_to_all.60 = f32[8,8,512]{2,1,0:T(8,128)} all-to-all(f32[8,8,512]{2,1,0:T(8,128)} %get-tuple-element.42), channel_id=1, replica_groups=mesh['gx'=4,'gy'=8,'gz'=8] {'gz'}, dimensions={0} | all-to-all | bytes 262144 | tf_op jit(solution)/shard_map/all_to_all | solution.py:565
  199.7 4.2 %shard_map.69 = (f32[24,24,128]{2,1,0:T(8,128)}, f32[8,8,576]{2,1,0:T(8,128)}) custom-call(s32[3]{0:T(128)} %pad_add_fusion.where_ref, f32[16,32,128]{2,1,0:T(8,128)} %get-tuple-element.40.w_ref, f32[16,32,128]{2,1,0:T(8,128)} %get-tuple-element.41.known_ref, f32[64,512]{1,0:T(8,128)} %bitcast.61, f32[8,128]{1,0:T(8,128)} %get-tuple-element.75.om_ref, ...), custom_call_target="tpu_custom_call" | custom-call | flops 1000000 | bytes 1000000 | tf_op jit(solution)/shard_map/pallas_call | solution.py:553
  203.9 10.4 %all_to_all.61 = f32[8,8,576]{2,1,0:T(8,128)} all-to-all(f32[8,8,576]{2,1,0:T(8,128)} %get-tuple-element.45), channel_id=1, replica_groups=mesh['gx'=4,'gy'=8,'gz'=8] {'gz'}, dimensions={0} | all-to-all | bytes 294912 | tf_op jit(solution)/shard_map/all_to_all | solution.py:565
  214.3 4.3 %shard_map.70 = (f32[26,32,128]{2,1,0:T(8,128)}, f32[8,8,832]{2,1,0:T(8,128)}) custom-call(s32[3]{0:T(128)} %pad_add_fusion.where_ref, f32[24,24,128]{2,1,0:T(8,128)} %get-tuple-element.43.w_ref, f32[24,24,128]{2,1,0:T(8,128)} %get-tuple-element.44.known_ref, f32[64,576]{1,0:T(8,128)} %bitcast.60, f32[8,128]{1,0:T(8,128)} %get-tuple-element.76.om_ref, ...), custom_call_target="tpu_custom_call" | custom-call | flops 1000000 | bytes 1000000 | tf_op jit(solution)/shard_map/pallas_call | solution.py:553
  218.6 4.2 %all-to-all-start.9 = ((f32[8,8,832]{2,1,0:T(8,128)}), f32[8,8,832]{2,1,0:T(8,128)S(1)}, u32[]{:S(2)}, u32[]{:S(2)}) async-start(f32[8,8,832]{2,1,0:T(8,128)} %get-tuple-element.47), calls=%async_computation.9 | async-start | bytes 458752 | tf_op jit(solution)/shard_map/all_to_all | solution.py:565
  222.9 5.6 %shard_map.71.known_ref = f32[26,32,128]{2,1,0:T(8,128)} custom-call(s32[3]{0:T(128)} %pad_add_fusion.where_ref, f32[5]{0:T(128)} %e_ref.15, f32[26,32,128]{2,1,0:T(8,128)} %pad_maximum_fusion.1.f_ref, f32[64,832]{1,0:T(8,128)} %bitcast.59, f32[8,128]{1,0:T(8,128)} %get-tuple-element.77.om_ref, f32[4,128,128]{2,1,0:T(8,128)} %get-tuple-element.59.power_ref, ...), custom_call_target="tpu_custom_call" | custom-call | flops 10000000000 | bytes 1000000 | tf_op jit(solution)/shard_map/pallas_call | solution.py:553
  229.7 5.6 %shard_map.72 = (f32[40,40,128]{2,1,0:T(8,128)}, f32[8,8,1600]{2,1,0:T(8,128)}) custom-call(s32[3]{0:T(128)} %pad_add_fusion.where_ref, f32[26,32,128]{2,1,0:T(8,128)} %get-tuple-element.46.w_ref, f32[26,32,128]{2,1,0:T(8,128)} %shard_map.71.known_ref, f32[64,832]{1,0:T(8,128)} %bitcast.57, f32[8,128]{1,0:T(8,128)} %get-tuple-element.77.om_ref, ...), custom_call_target="tpu_custom_call" | custom-call | flops 1000000 | bytes 1000000 | tf_op jit(solution)/shard_map/pallas_call | solution.py:553
  235.3 4.4 %all-to-all-start.10 = ((f32[8,8,1600]{2,1,0:T(8,128)}), f32[8,8,1600]{2,1,0:T(8,128)S(1)}, u32[]{:S(2)}, u32[]{:S(2)}) async-start(f32[8,8,1600]{2,1,0:T(8,128)} %get-tuple-element.52), calls=%async_computation.10 | async-start | bytes 851968 | tf_op jit(solution)/shard_map/all_to_all | solution.py:565
  239.7 9.9 %shard_map.73 = (f32[32,32,128]{2,1,0:T(8,128)}, f32[32,32,128]{2,1,0:T(8,128)}) custom-call(s32[3]{0:T(128)} %pad_add_fusion.where_ref, f32[5]{0:T(128)} %e_ref.15, f32[40,40,128]{2,1,0:T(8,128)} %pad_maximum_fusion.f_ref, f32[64,1600]{1,0:T(8,128)} %bitcast.56, f32[8,128]{1,0:T(8,128)} %get-tuple-element.78.om_ref, ...), custom_call_target="tpu_custom_call" | custom-call | flops 20000000000 | bytes 1000000 | tf_op jit(solution)/shard_map/pallas_call | solution.py:553
  250.4 8.3 %shard_map.74 = (f32[32,32,128]{2,1,0:T(8,128)}, f32[32,32,128]{2,1,0:T(8,128)}) custom-call(s32[3]{0:T(128)} %pad_add_fusion.where_ref, f32[5]{0:T(128)} %e_ref.15, f32[40,40,128]{2,1,0:T(8,128)} %get-tuple-element.49.w_ref, f32[32,32,128]{2,1,0:T(8,128)} %get-tuple-element.50.known_ref, f32[32,32,128]{2,1,0:T(8,128)} %get-tuple-element.51.twice_ref, ...), custom_call_target="tpu_custom_call" | custom-call | flops 1000000 | bytes 1000000 | tf_op jit(solution)/shard_map/pallas_call | solution.py:553
  (41 shorter events, 27.1 us)
Async XLA Ops:
  1.6 17.4 %collective-permute-start = (f32[32,4,128]{2,1,0:T(4,128)S(1)}, f32[32,4,128]{2,1,0:T(4,128)S(1)}, u32[]{:S(2)}, u32[]{:S(2)}) collective-permute-start(f32[32,4,128]{2,1,0:T(4,128)S(1)} %get-tuple-element.63), channel_id=1, source_target_pairs={{0,8},{8,16},{16,24},{24,32},{32,40},{40,48},{48,56},{1,9},{9,17},... | collective-permute-start | bytes 196616 | tf_op jit(solution)/shard_map/ppermute | solution.py:580
  6.0 13.0 %collective-permute-start.1 = (f32[32,4,128]{2,1,0:T(4,128)S(1)}, f32[32,4,128]{2,1,0:T(4,128)S(1)}, u32[]{:S(2)}, u32[]{:S(2)}) collective-permute-start(f32[32,4,128]{2,1,0:T(4,128)S(1)} %get-tuple-element.64), channel_id=1, source_target_pairs={{8,0},{16,8},{24,16},{32,24},{40,32},{48,40},{56,48},{9,1},{17,9},... | collective-permute-start | bytes 196616 | tf_op jit(solution)/shard_map/ppermute | solution.py:581
  11.2 20.3 %all-to-all-start.1 = ((f32[8,10,8,128]{3,2,1,0:T(8,128)}), f32[8,10,8,128]{3,2,1,0:T(8,128)S(1)}, u32[]{:S(2)}, u32[]{:S(2)}) async-start(f32[8,10,8,128]{3,2,1,0:T(8,128)} %get-tuple-element.30), calls=%async_computation.1 | async-start | bytes 655360 | tf_op jit(solution)/shard_map/all_to_all | solution.py:565
  16.6 2.4 copy-start
  16.6 6.9 %copy-start.6 = (f32[5,8,128]{2,1,0:T(8,128)S(1)}, f32[5,8,128]{2,1,0:T(8,128)}, u32[]{:S(2)}) copy-start(f32[5,8,128]{2,1,0:T(8,128)} %get-tuple-element.29) | copy-start | bytes 61444
  19.1 5.1 %collective-permute-start.2 = (f32[4,40,128]{2,1,0:T(8,128)S(1)}, f32[4,40,128]{2,1,0:T(8,128)S(1)}, u32[]{:S(2)}, u32[]{:S(2)}) collective-permute-start(f32[4,40,128]{2,1,0:T(8,128)S(1)} %get-tuple-element.61), channel_id=1, source_target_pairs={{0,64},{64,128},{128,192},{1,65},{65,129},{129,193},{2,66},{66,130... | collective-permute-start | bytes 245768 | tf_op jit(solution)/shard_map/ppermute | solution.py:580
  22.2 5.6 %collective-permute-start.3 = (f32[4,40,128]{2,1,0:T(8,128)S(1)}, f32[4,40,128]{2,1,0:T(8,128)S(1)}, u32[]{:S(2)}, u32[]{:S(2)}) collective-permute-start(f32[4,40,128]{2,1,0:T(8,128)S(1)} %get-tuple-element.62), channel_id=1, source_target_pairs={{64,0},{128,64},{192,128},{65,1},{129,65},{193,129},{66,2},{130,66... | collective-permute-start | bytes 245768 | tf_op jit(solution)/shard_map/ppermute | solution.py:581
  28.8 8.6 %copy-start.5 = (f32[5,4,8,128]{3,2,1,0:T(8,128)S(1)}, f32[5,4,8,128]{3,2,1,0:T(8,128)}, u32[]{:S(2)}) copy-start(f32[5,4,8,128]{3,2,1,0:T(8,128)} %get-tuple-element.33) | copy-start | bytes 245764
  31.5 7.1 %copy-start.3 = (f32[8,10,8,128]{3,2,1,0:T(8,128)}, f32[8,10,8,128]{3,2,1,0:T(8,128)S(1)}, u32[]{:S(2)}) copy-start(f32[8,10,8,128]{3,2,1,0:T(8,128)S(1)} %all-to-all-done.1.table_ref) | copy-start | bytes 983044
  31.5 13.8 %all-to-all-start = ((f32[8,8,1600]{2,1,0:T(8,128)}), f32[8,8,1600]{2,1,0:T(8,128)S(1)}, u32[]{:S(2)}, u32[]{:S(2)}) async-start(f32[8,8,1600]{2,1,0:T(8,128)} %shard_map.60), calls=%async_computation | async-start | bytes 851968 | tf_op jit(solution)/shard_map/all_to_all | solution.py:565
  45.3 0.8 copy-start.2
  52.6 5.6 %collective-permute-start.4 = (f32[16,8,128]{2,1,0:T(8,128)S(1)}, f32[16,8,128]{2,1,0:T(8,128)S(1)}, u32[]{:S(2)}, u32[]{:S(2)}) collective-permute-start(f32[16,8,128]{2,1,0:T(8,128)S(1)} %get-tuple-element.67), channel_id=1, source_target_pairs={{0,8},{8,16},{16,24},{24,32},{32,40},{40,48},{48,56},{1,9},{9,17},... | collective-permute-start | bytes 196616 | tf_op jit(solution)/shard_map/ppermute | solution.py:580
  56.9 5.2 %collective-permute-start.5 = (f32[16,8,128]{2,1,0:T(8,128)S(1)}, f32[16,8,128]{2,1,0:T(8,128)S(1)}, u32[]{:S(2)}, u32[]{:S(2)}) collective-permute-start(f32[16,8,128]{2,1,0:T(8,128)S(1)} %get-tuple-element.68), channel_id=1, source_target_pairs={{8,0},{16,8},{24,16},{32,24},{40,32},{48,40},{56,48},{9,1},{17,9},... | collective-permute-start | bytes 196616 | tf_op jit(solution)/shard_map/ppermute | solution.py:581
  62.9 4.6 %collective-permute-start.6 = (f32[5,32,128]{2,1,0:T(8,128)S(1)}, f32[5,32,128]{2,1,0:T(8,128)S(1)}, u32[]{:S(2)}, u32[]{:S(2)}) collective-permute-start(f32[5,32,128]{2,1,0:T(8,128)S(1)} %get-tuple-element.65), channel_id=1, source_target_pairs={{0,64},{64,128},{128,192},{1,65},{65,129},{129,193},{2,66},{66,130... | collective-permute-start | bytes 245768 | tf_op jit(solution)/shard_map/ppermute | solution.py:580
  66.0 5.2 %collective-permute-start.7 = (f32[5,32,128]{2,1,0:T(8,128)S(1)}, f32[5,32,128]{2,1,0:T(8,128)S(1)}, u32[]{:S(2)}, u32[]{:S(2)}) collective-permute-start(f32[5,32,128]{2,1,0:T(8,128)S(1)} %get-tuple-element.66), channel_id=1, source_target_pairs={{64,0},{128,64},{192,128},{65,1},{129,65},{193,129},{66,2},{130,66... | collective-permute-start | bytes 245768 | tf_op jit(solution)/shard_map/ppermute | solution.py:581
  218.6 10.4 %all-to-all-start.9 = ((f32[8,8,832]{2,1,0:T(8,128)}), f32[8,8,832]{2,1,0:T(8,128)S(1)}, u32[]{:S(2)}, u32[]{:S(2)}) async-start(f32[8,8,832]{2,1,0:T(8,128)} %get-tuple-element.47), calls=%async_computation.9 | async-start | bytes 458752 | tf_op jit(solution)/shard_map/all_to_all | solution.py:565
  229.0 0.7 copy-start.4
  235.3 14.3 %all-to-all-start.10 = ((f32[8,8,1600]{2,1,0:T(8,128)}), f32[8,8,1600]{2,1,0:T(8,128)S(1)}, u32[]{:S(2)}, u32[]{:S(2)}) async-start(f32[8,8,1600]{2,1,0:T(8,128)} %get-tuple-element.52), calls=%async_computation.10 | async-start | bytes 851968 | tf_op jit(solution)/shard_map/all_to_all | solution.py:565
  249.6 0.8 copy-start.1

commit v2 on v1

v2 whole, which is shorter than its diff:
```python
import functools

import jax
import jax.numpy as jnp
from jax import lax
from jax.experimental import pallas as pl
from jax.experimental.pallas import tpu as pltpu
from jax.sharding import PartitionSpec as P

LEVELS = 5
POWERS = 4
HIGHEST = lax.Precision.HIGHEST
F32 = jnp.float32
VMEM_LIMIT = 56 * 1024 * 1024


def contract(a, b, da, db):
    return lax.dot_general(
        a, b, (((da,), (db,)), ((), ())), precision=HIGHEST, preferred_element_type=F32
    )


def exact_nn(a, b):
    return contract(a, b, 1, 0)


def exact_nt(a, b):
    return contract(a, b, 1, 1)


def exact_tn(a, b):
    return contract(a, b, 0, 0)


def halves(a):
    if isinstance(a, tuple):
        return a
    high = a.astype(jnp.bfloat16)
    return high, (a - high.astype(F32)).astype(jnp.bfloat16)


def product(a, b, da, db):
    (ah, al), (bh, bl) = halves(a), halves(b)

    def dot(x, y):
        return lax.dot_general(x, y, (((da,), (db,)), ((), ())), preferred_element_type=F32)

    return dot(ah, bh) + (dot(ah, bl) + dot(al, bh))


def nn(a, b):
    return product(a, b, 1, 0)


def nt(a, b):
    return product(a, b, 1, 1)


def tn(a, b):
    return product(a, b, 0, 0)


def rows(lo, hi, fn, step=4):
    full = (hi - lo) // step
    if full:
        def group(k, carry):
            for q in range(step):
                fn(lo + k * step + q)
            return carry

        lax.fori_loop(0, full, group, 0)
    for i in range(lo + full * step, hi):
        fn(i)


def sublane_index(length):
    return lax.broadcasted_iota(jnp.int32, (length, 128), 0)


def shifted(v, zero_ends):
    n = v.shape[0]
    low, high = pltpu.roll(v, 1, 0), pltpu.roll(v, n - 1, 0)
    if zero_ends:
        at = sublane_index(n)
        low = jnp.where(at > 0, low, 0.0)
        high = jnp.where(at < n - 1, high, 0.0)
    return low, high


class Window:
    def __init__(self, shape, origin=None, grid=None):
        self.x, self.y = shape
        self.whole = origin is None
        self.lo, self.hi = (0, self.y) if self.whole else (1, self.y - 1)
        if not self.whole:
            self.x0, y0 = origin
            self.nx, ny = grid
            at = sublane_index(self.y - 2) + (y0 + 1)
            self.in_y = jnp.where((at >= 0) & (at < ny), 1.0, 0.0).astype(F32)

    def get(self, ref, i):
        return ref[i, self.lo : self.hi]

    def put(self, ref, i, v):
        ref[i, self.lo : self.hi] = v

    def mask(self, i, v):
        if self.whole:
            return v
        at = self.x0 + i
        inside = jnp.where((at >= 0) & (at < self.nx), 1.0, 0.0).astype(F32)
        return v * (self.in_y * inside)

    def around(self, ref, i):
        if self.whole:
            low, high = shifted(ref[i], True)
            below = ref[jnp.maximum(i - 1, 0)] * jnp.where(i > 0, 1.0, 0.0).astype(F32)
            above = ref[jnp.minimum(i + 1, self.x - 1)] * jnp.where(i < self.x - 1, 1.0, 0.0).astype(F32)
            return (low + high) + (below + above)
        y = self.y
        return (ref[i, 0 : y - 2] + ref[i, 2:y]) + (ref[i - 1, 1 : y - 1] + ref[i + 1, 1 : y - 1])

    def span(self, trim):
        return (0, self.x) if self.whole else (trim, self.x - trim)

    def each(self, trim, out, fn):
        lo, hi = self.span(trim)
        rows(lo, hi, lambda i: self.put(out, i, fn(i)))


def line_powers(field, ends, power_ref, link_ref, count, out_refs, exact=False):
    if not exact:
        field, ends = halves(field), halves(ends)
    for j in range(count):
        if exact:
            value = exact_nt(field, power_ref[j]) + exact_tn(ends, link_ref[j])
        else:
            value = nt(field, power_ref[j]) + tn(ends, link_ref[j])
        out_refs[j][...] = value.reshape(out_refs[j].shape)


def smoothed_residual(win, field_ref, x1, x2, t, out, trim, masked=False, add=None):
    win.each(trim - 1, t, lambda i: 0.32 * win.get(x1, i) + win.mask(i, 0.64 * win.around(x2, i)))

    def outer(i):
        v = 0.04 * win.get(field_ref, i) + win.around(t, i)
        if add is not None:
            v = v + win.get(add, i)
        return win.mask(i, v) if masked else v

    win.each(trim, out, outer)


def horner(win, xs, weights, t0, t1, trim):
    src = xs[-1]
    scale = weights[-1]
    buffers = (t0, t1)
    for n, j in enumerate(range(len(xs) - 2, 0, -1)):
        dst = buffers[n % 2]

        def one(i, src=src, j=j, scale=scale):
            return weights[j] * win.get(xs[j], i) + win.mask(i, scale * win.around(src, i))

        win.each(trim - j, dst, one)
        src, scale = dst, 1.0
    return src, scale


def restrict(src, scratch, out, x_at, y_at):
    count_x, count_y = out.shape[0], out.shape[1]
    for i in range(count_x):
        scratch[i] = src[x_at + 2 * i] + src[x_at + 2 * i + 1]
    for i in range(count_x):
        even = scratch[i, pl.ds(y_at, count_y, stride=2), :]
        odd = scratch[i, pl.ds(y_at + 1, count_y, stride=2), :]
        out[i] = (even + odd) * 0.25


def prolong(src, src_whole, out, win, x_from, y_from, count_x, count_y):
    last = src.shape[0] - 1
    for i in range(count_x):
        at = x_from + i
        centre = src[at]
        below = src[at - 1] if at > 0 else jnp.zeros_like(centre)
        above = src[at + 1] if at < last else jnp.zeros_like(centre)
        for odd, other in ((0, below), (1, above)):
            v = 0.75 * centre + 0.25 * other
            low, high = shifted(v, src_whole)
            for parity, side in ((0, low), (1, high)):
                w = 0.75 * v + 0.25 * side
                out[2 * i + odd, pl.ds(parity, count_y, stride=2), :] = w[y_from : y_from + count_y]
    if not win.whole:
        win.each(0, out, lambda i: win.mask(i, win.get(out, i)))


def send(out_ref, value):
    for m in range(out_ref.shape[0]):
        out_ref[m] = value


def powers_kernel(g_ref, e_ref, zf_ref, *outs):
    levels, n = g_ref.shape[0], g_ref.shape[1]
    power_refs, ends_refs, link_refs = outs[0:levels], outs[levels : 2 * levels], outs[2 * levels : 3 * levels]
    up_ref, basis_ref, table_ref = outs[3 * levels :]
    table_ref[...] = jnp.zeros_like(table_ref)
    for level in range(levels):
        power_ref, ends_ref, link_ref = power_refs[level], ends_refs[level], link_refs[level]
        link_ref[...] = jnp.zeros_like(link_ref)
        e = e_ref[level]
        inverse_e = 1.0 / jnp.full((1, n), e, F32)
        one = g_ref[level] * e
        two = exact_nn(one, one)
        three = exact_nn(two, one)
        four = exact_nn(two, two)
        ends = []
        for j, value in enumerate((one, two, three, four)):
            power_ref[j] = value
            for s, row in enumerate((value[0:1], value[n - 1 : n])):
                ends_ref[2 * j + s : 2 * j + s + 1] = row
                table_ref[0, 2 * j + s, level : level + 1] = row
                ends.append(row)
        for j in range(POWERS):
            for i in range(j + 1):
                for t in range(2):
                    link_ref[j, 2 * i + t : 2 * i + t + 1] = ends[2 * (j - i) + t] * inverse_e
        table_ref[0, 9, level : level + 1] = inverse_e
    table_ref[0, 8] = jnp.broadcast_to(zf_ref[...], (8, n))
    zero = ends_refs[0][0:4] * (1.0 / jnp.full((4, n), e_ref[0], F32))
    basis_ref[0:4] = zero
    basis_ref[4:8] = exact_nn(zero, power_refs[1][0])
    basis_ref[8:12] = exact_nn(zero, power_refs[1][1])
    basis_ref[12:16] = ends_refs[1][0:4] * (1.0 / jnp.full((4, n), e_ref[1], F32))
    basis = jnp.concatenate([basis_ref[...], jnp.zeros((n - 16, n), F32)], 0)
    at = lax.broadcasted_iota(jnp.int32, (8, n), 1)
    table_ref[0, 10] = jnp.where(at < 4, exact_nt(ends_refs[1][...], basis), 0.0)
    table_ref[0, 11] = exact_nt(ends_refs[2][...], basis)
    for m in range(1, table_ref.shape[0]):
        table_ref[m] = table_ref[0]
    at = lax.broadcasted_iota(jnp.int32, (1, n), 1)
    up_ref[...] = jnp.zeros_like(up_ref)
    up_ref[0:4] = ends_refs[0][0:4]
    up_ref[4:5] = jnp.where(at == 0, 1.0, 0.0).astype(F32)
    up_ref[5:6] = jnp.where(at == n - 1, 1.0, 0.0).astype(F32)


def coupling_kernel(
    where_ref, table_ref, e_ref, zf_ref, basis_ref, om0, om1, om2, om3, om4, om_up_ref, m_ref, m_link_ref, mix_ref, w2_ref, held, full
):
    blocks, n = table_ref.shape[0], table_ref.shape[3]
    k_own = where_ref[2]
    wide = (8, n)
    lane = lax.broadcasted_iota(jnp.int32, wide, 1)
    inverse_e = table_ref[0, 9]

    def entry(m, row, column):
        at = 0 if column == 0 else n - 1
        return jnp.broadcast_to(table_ref[m, row][:, at : at + 1], wide)

    corner = [
        [
            [[entry(m, 2 * i + s, t) * inverse_e for t in range(2)] for s in range(2)]
            for m in range(blocks)
        ]
        for i in range(POWERS)
    ]
    face = [entry(m, 8, 0) for m in range(blocks)]

    gain_v, gain_d, gain_p, gain_g = [corner[0][0][1][1]], [None], [None], [None]
    for k in range(1, blocks):
        (a, b), (c, d) = corner[0][k]
        g = face[k]
        gv = g * g * gain_v[k - 1]
        dk = 1.0 / (1.0 - a * gv)
        gain_d.append(dk)
        gain_p.append(dk * b)
        gain_g.append(gv)
        gain_v.append(d + c * gv * gain_p[k])

    def solve(low, high):
        u, pu = [high[0]], [None]
        for k in range(1, blocks):
            (a, b), (c, d) = corner[0][k]
            gu = face[k] * u[k - 1]
            pu.append(gain_d[k] * (low[k] + a * gu))
            u.append(high[k] + c * (gu + gain_g[k] * pu[k]))
        zero = jnp.zeros(wide, F32)
        alpha, beta = [zero] * blocks, [zero] * blocks
        for k in range(blocks - 1, 0, -1):
            p = pu[k] + gain_p[k] * beta[k]
            beta[k - 1] = face[k] * p
            alpha[k] = face[k] * (u[k - 1] + gain_v[k - 1] * beta[k - 1])
        return alpha, beta

    unit = [
        [jnp.where(lane == 8 * m + s, 1.0, 0.0).astype(F32) for m in range(blocks)] for s in range(2)
    ]
    response = [solve(unit[0], unit[1])]
    for i in range(1, POWERS):
        source = [[None] * blocks, [None] * blocks]
        for m in range(blocks):
            for s in range(2):
                total = None
                for q in range(i):
                    c = corner[i - q][m][s]
                    term = c[0] * response[q][0][m] + c[1] * response[q][1][m]
                    total = term if total is None else total + term
                source[s][m] = total
        response.append(solve(source[0], source[1]))
    for i in range(POWERS):
        for t in range(2):
            for m in range(blocks):
                held[m, 2 * i + t] = response[i][t][m]
    om_refs = (om0, om1, om2, om3, om4)
    for i in range(POWERS):
        for t in range(2):
            total = held[k_own, 2 * i + t]
            for j in range(1, i + 1):
                total = total + pltpu.roll(held[k_own, 2 * (i - j) + t], 2 * j, 1)
            for level in range(LEVELS):
                om_refs[level][2 * i + t : 2 * i + t + 1] = total[level : level + 1]
    om_up_ref[...] = om0[...]

    def every(i, t, m):
        total = held[m, 2 * i + t]
        if i == 1:
            total = total + pltpu.roll(held[m, t], 2, 1)
        return total

    def matrix(slot, level, groups, own):
        full[...] = jnp.zeros_like(full)
        for start, i, scale in groups:
            for m in range(blocks):
                for t in range(2):
                    row = start + 2 * m + t
                    full[row : row + 1] = scale * every(i, t, m)[level : level + 1]
        if own is not None:
            full[own : own + 8] = om_refs[level][...]
        mix_ref[slot] = full[...].T

    matrix(0, 0, [(0, 0, 0.32)], 64)
    matrix(1, 0, [(0, 1, 0.64), (16, 0, 0.64)], None)
    matrix(2, 1, [(96, 0, 0.32)], None)
    matrix(3, 1, [(96, 1, 0.64), (112, 0, 0.64)], None)
    matrix(4, 1, [], 0)
    row = lax.broadcasted_iota(jnp.int32, (n, n), 0)
    column = lax.broadcasted_iota(jnp.int32, (n, n), 1)

    def spread(m):
        return jnp.where(
            (row < 16) & (column == (row >> 1) * 16 + 2 * m + (row & 1)), 1.0, 0.0
        ).astype(F32)

    def gathered(slot):
        full[...] = jnp.zeros_like(full)
        for m in range(blocks):
            full[8 * m : 8 * m + 8] = exact_nn(table_ref[m, slot], spread(m))
        return full[...]

    one = gathered(10).T

    def diagonal(shift, scale):
        return jnp.where((row < 32) & (column == row + shift), scale, 0.0).astype(F32)

    mix_ref[5] = diagonal(0, 0.04)
    mix_ref[6] = exact_nn(one, mix_ref[2]) + diagonal(32, 0.32)
    mix_ref[7] = exact_nn(one, mix_ref[3]) + diagonal(64, 0.64)
    mix_ref[8] = exact_nn(one, mix_ref[4])
    w2_ref[...] = exact_nn(om2[...], gathered(11))
    basis = jnp.concatenate([basis_ref[...], jnp.zeros((n - 16, n), F32)], 0)
    chosen = exact_tn(spread(k_own), basis)
    mix_ref[9] = jnp.where(row < 32, chosen, 0.0)
    mix_ref[10] = chosen
    lane = lane[0:1]
    om_up_ref[4:5] = jnp.where((lane == 8 * (k_own - 1) + 5) & (k_own > 0), 1.0, 0.0).astype(F32)
    om_up_ref[5:6] = jnp.where((lane == 8 * (k_own + 1) + 4) & (k_own < blocks - 1), 1.0, 0.0).astype(F32)
    om_up_ref[6:8] = jnp.zeros((2, n), F32)

    above = jnp.minimum(k_own + 1, blocks - 1)
    top = table_ref[above, 8][0:1, 0:1]
    top = jnp.where(jnp.full((1, 1), k_own, jnp.int32) < blocks - 1, top, 1.0)
    down = zf_ref[...]
    up = jnp.where(lane == n - 1, jnp.broadcast_to(top, (1, n)), pltpu.roll(down, n - 1, 1))
    down_all, up_all = jnp.broadcast_to(down, (n, n)), jnp.broadcast_to(up, (n, n))
    m_ref[...] = jnp.where(
        row == column,
        down_all + up_all + 4.0 * e_ref[0],
        jnp.where(row == column - 1, -down_all, jnp.where(row == column + 1, -up_all, 0.0)),
    )
    m_link_ref[...] = jnp.zeros_like(m_link_ref)
    m_link_ref[4:5] = jnp.where(lane == 0, -down, 0.0)
    m_link_ref[5:6] = jnp.where(lane == n - 1, -up, 0.0)


def flat(ref):
    return ref[...].reshape(ref.shape[0] * ref.shape[1], ref.shape[2])


def ends_from(om_ref, got_ref):
    return exact_nn(om_ref[:, : got_ref.shape[0]], got_ref[...])


def restrict_into(src, scratch, out, x_at, y_at, count_y, y_to):
    for i in range(out.shape[0]):
        scratch[i] = src[x_at + 2 * i] + src[x_at + 2 * i + 1]
    for i in range(out.shape[0]):
        even = scratch[i, pl.ds(y_at, count_y, stride=2), :]
        odd = scratch[i, pl.ds(y_at + 1, count_y, stride=2), :]
        out[i, y_to : y_to + count_y] = (even + odd) * 0.25


def padded_lanes(count):
    return (count + 127) // 128 * 128


def windows(where_ref, s0, s1, ext0, ext1, grids):
    h0 = tuple((a - b) // 2 for a, b in zip(ext0, s0))
    h1 = tuple((a - b) // 2 for a, b in zip(ext1, s1))
    ix, iy = where_ref[0], where_ref[1]
    win0 = Window(ext0, (ix * s0[0] - h0[0], iy * s0[1] - h0[1]), grids[0])
    win1 = Window(ext1, (ix * s1[0] - h1[0], iy * s1[1] - h1[1]), grids[1])
    return win0, win1, h0, h1


def local_down_kernel(
    s0, s1, grids, where_ref, f_ref, power0, power1, v0, v1, v2, out_ref, f1_ref, f2_ref,
    x1, x2, t, r, pair, y1, y2, t1, r1, pair1
):
    ext0, ext1 = f_ref.shape[:2], f1_ref.shape[:2]
    win0, win1, h0, h1 = windows(where_ref, s0, s1, ext0, ext1, grids)
    field = halves(flat(f_ref))
    lanes0 = ext0[0] * ext0[1]
    lanes1 = ext1[0] * ext1[1]
    at1 = padded_lanes(lanes0)
    at2 = at1 + padded_lanes(lanes1)
    many = out_ref.shape[0]
    out_ref[0, :, at1 - 128 : at1] = jnp.zeros((8, 128), F32)
    out_ref[0, :, at2 - 128 : at2] = jnp.zeros((8, 128), F32)
    out_ref[0, :, at2 : at2 + 128] = jnp.zeros((8, 128), F32)
    out_ref[0, :, 0:lanes0] = nt(v0[...], field)
    x1[...] = nt(field, power0[0]).reshape(x1.shape)
    x2[...] = nt(field, power0[1]).reshape(x2.shape)
    smoothed_residual(win0, f_ref, x1, x2, t, r, 2, masked=True)
    f1_ref[...] = jnp.zeros_like(f1_ref)
    count = (ext0[1] - 4) // 2
    restrict_into(r, pair, f1_ref, 2, 2, count, (ext1[1] - count) // 2)
    field = halves(flat(f1_ref))
    out_ref[0, :, at1 : at1 + lanes1] = nt(v1[...], field)
    y1[...] = nt(field, power1[0]).reshape(y1.shape)
    y2[...] = nt(field, power1[1]).reshape(y2.shape)
    smoothed_residual(win1, f1_ref, y1, y2, t1, r1, h1[0])
    restrict(r1, pair1, f2_ref, h1[0], h1[1])
    lines2 = f2_ref.shape[0] * f2_ref.shape[1]
    out_ref[0, :, at2 : at2 + lines2] = nt(v2[...], flat(f2_ref))
    for m in range(1, many):
        out_ref[m] = out_ref[0]


def joined_down_kernel(
    s0, s1, ext0, grids, where_ref, got_ref, f1_local, f2_local, mix_ref, om2_ref, w2_ref,
    f1_ref, own1_ref, parts_ref, d1, d2, f, pair, y, h1s, h2s, f2s, pair1, z
):
    ext1 = f1_local.shape[:2]
    win0, win1, h0, h1 = windows(where_ref, s0, s1, ext0, ext1, grids)
    lanes0 = ext0[0] * ext0[1]
    lanes1 = ext1[0] * ext1[1]
    at1 = padded_lanes(lanes0)
    at2 = at1 + padded_lanes(lanes1)
    got0 = halves(got_ref[:, 0:lanes0])
    rows_in = got_ref.shape[0]
    d1[...] = tn(got0, mix_ref[0, 0:rows_in]).reshape(d1.shape)
    d2[...] = tn(got0, mix_ref[1, 0:rows_in]).reshape(d2.shape)

    win0.each(1, d1, lambda i: win0.get(d1, i) + win0.mask(i, win0.around(d2, i)))
    win0.each(2, f, lambda i: win0.mask(i, win0.around(d1, i)))
    y[...] = jnp.zeros_like(y)
    count = (ext0[1] - 4) // 2
    restrict_into(f, pair, y, 2, 2, count, (ext1[1] - count) // 2)
    yf = halves(flat(y))
    f1_ref[...] = f1_local[...] + nn(yf, mix_ref[9]).reshape(f1_ref.shape)
    got1 = halves(got_ref[:, at1 : at1 + lanes1])
    own1_ref[...] = (tn(got1, mix_ref[4, 0:rows_in]) + nn(yf, mix_ref[8])).reshape(own1_ref.shape)
    h1s[...] = (tn(got1, mix_ref[2, 0:rows_in]) + nn(yf, mix_ref[6])).reshape(h1s.shape)
    h2s[...] = (tn(got1, mix_ref[3, 0:rows_in]) + nn(yf, mix_ref[7])).reshape(h2s.shape)
    f2s[...] = nn(yf, mix_ref[5]).reshape(f2s.shape)
    trim = h1[0]
    win1.each(trim - 1, h1s, lambda i: win1.get(h1s, i) + win1.mask(i, win1.around(h2s, i)))
    win1.each(trim, f2s, lambda i: win1.get(f2s, i) + win1.around(h1s, i))
    restrict(f2s, pair1, z, h1[0], h1[1])
    zf = flat(z)
    lines2 = zf.shape[0]
    side = z.shape[0]
    parts_ref[0, 0:side] = f2_local[...] + nn(zf, mix_ref[10]).reshape(z.shape)
    own2 = nn(om2_ref[:, 0:rows_in], got_ref[:, at2 : at2 + lines2]) + nt(w2_ref[...], zf)
    parts_ref[0, side] = jnp.zeros((8, 128), F32)
    parts_ref[0, side, :, 0:lines2] = own2
    for m in range(1, parts_ref.shape[0]):
        parts_ref[m] = parts_ref[0]


KNOWN = (0.9984, 0.9728, 0.8192, 0.4096)
TWICE = (0.0016, 0.0256, 0.1536, 0.4096, 0.4096)


def lane_powers(field, coefficients, lane0, power_ref, link_ref, count, out_refs, exact=False):
    n = field.shape[1]
    if not exact:
        field, coefficients = halves(field), halves(coefficients)
    one, two = (exact_nt, exact_nn) if exact else (nt, nn)
    for j in range(count):
        pieces = [link_ref[j], jnp.zeros((n - 8 - lane0, n), F32)]
        if lane0:
            pieces = [jnp.zeros((lane0, n), F32)] + pieces
        value = one(field, power_ref[j]) + two(coefficients, jnp.concatenate(pieces, 0))
        out_refs[j][...] = value.reshape(out_refs[j].shape)


def known_zero_kernel(
    s0, ext0, grid, where_ref, e_ref, f_ref, got_ref, mix_ref, power_ref, link_ref,
    known_out, twice_out, own, f, x1, x2, x3, x4, t0, t1
):
    hx, hy = (f.shape[0] - s0[0]) // 2, (f.shape[1] - s0[1]) // 2
    cx, cy = (ext0[0] - f.shape[0]) // 2, (ext0[1] - f.shape[1]) // 2
    win = Window(f.shape[:2], (where_ref[0] * s0[0] - hx, where_ref[1] * s0[1] - hy), grid)
    coefficients = tn(got_ref[:, 0 : ext0[0] * ext0[1]], mix_ref[0, 0 : got_ref.shape[0]])
    own[...] = coefficients.reshape(ext0 + (128,))[cx : cx + f.shape[0], cy : cy + f.shape[1]]
    f[...] = f_ref[cx : cx + f.shape[0], cy : cy + f.shape[1]]
    xs = (x1, x2, x3, x4)
    lane_powers(flat(f), flat(own), 64, power_ref, link_ref, POWERS, xs)
    inverse_e = 1.0 / jnp.full((win.hi - win.lo, 128), e_ref[0], F32)
    at = hy - win.lo
    src, scale = horner(win, xs, KNOWN, t0, t1, hx)
    lo, hi = win.span(hx)

    def known(i):
        v = (KNOWN[0] * win.get(x1, i) + scale * win.around(src, i)) * inverse_e
        known_out[i - hx] = v[at : at + s0[1]]

    rows(lo, hi, known)
    src2, scale2 = horner(win, (f,) + xs, TWICE, t0, t1, hx)

    def again(i):
        v = TWICE[0] * win.get(f, i) + scale2 * win.around(src2, i)
        twice_out[i - hx] = v[at : at + s0[1]]

    rows(lo, hi, again)


def known_one_kernel(
    s1, grid, where_ref, e_ref, f_ref, own_ref, power_ref, link_ref, known_out, x1, x2, x3, x4, t0, t1
):
    hx, hy = (f_ref.shape[0] - s1[0]) // 2, (f_ref.shape[1] - s1[1]) // 2
    win = Window(f_ref.shape[:2], (where_ref[0] * s1[0] - hx, where_ref[1] * s1[1] - hy), grid)
    xs = (x1, x2, x3, x4)
    lane_powers(flat(f_ref), flat(own_ref), 0, power_ref, link_ref, POWERS, xs, exact=True)
    inverse_e = 1.0 / jnp.full((win.hi - win.lo, 128), e_ref[1], F32)
    src, scale = horner(win, xs, KNOWN, t0, t1, 3)
    known_out[...] = jnp.zeros_like(known_out)

    def known(i):
        return win.mask(i, (KNOWN[0] * win.get(x1, i) + scale * win.around(src, i)) * inverse_e)

    win.each(3, known_out, known)


def known_two_kernel(
    across, down, grid, where_ref, e_ref, parts_ref, power_ref, link_ref, known_out,
    fp, ap, x1, x2, x3, x4, t0, t1
):
    side = parts_ref.shape[2]
    lines = side * side
    ix, iy = where_ref[0], where_ref[1]
    for p in range(9):
        jx, jy = ix + p // 3 - 1, iy + p % 3 - 1
        inside = (jx >= 0) & (jx < across) & (jy >= 0) & (jy < down)
        at = jnp.clip(jx, 0, across - 1) * down + jnp.clip(jy, 0, down - 1)
        scale = jnp.where(inside, 1.0, 0.0).astype(F32)
        fp[p * lines : (p + 1) * lines] = (parts_ref[at, 0:side] * scale).reshape(lines, 128)
        ap[:, p * lines : (p + 1) * lines] = (parts_ref[at, side] * scale)[:, 0:lines]
    xs = (x1, x2, x3, x4)
    for j in range(POWERS):
        value = exact_nt(fp[...], power_ref[j]) + exact_tn(ap[...], link_ref[j])
        for p in range(9):
            px, py = p // 3 * side, p % 3 * side
            piece = value[p * lines : (p + 1) * lines].reshape(side, side, 128)
            xs[j][px : px + side, py : py + side] = piece
    win = Window(x1.shape[:2], ((ix - 1) * side, (iy - 1) * side), grid)
    inverse_e = 1.0 / jnp.full((win.hi - win.lo, 128), e_ref[2], F32)
    src, scale = horner(win, xs, KNOWN, t0, t1, 3)
    known_out[...] = jnp.zeros_like(known_out)

    def known(i):
        return win.mask(i, (KNOWN[0] * win.get(x1, i) + scale * win.around(src, i)) * inverse_e)

    win.each(3, known_out, known)


def gathered_down_kernel(
    across, down, parts_ref, power_ref, link_ref, v_ref, coarse_ref, out_ref, f, fp, ap, x1, x2, t, r, pair
):
    many, side = parts_ref.shape[0], parts_ref.shape[2]
    lines = side * side
    for p in range(many):
        px, py = p // down * side, p % down * side
        part = parts_ref[p, 0:side]
        f[px : px + side, py : py + side] = part
        fp[p * lines : (p + 1) * lines] = part.reshape(lines, 128)
        ap[:, p * lines : (p + 1) * lines] = parts_ref[p, side][:, 0:lines]
    fields, coefficients = halves(fp[...]), halves(ap[...])
    for j, x in enumerate((x1, x2)):
        value = nt(fields, power_ref[j]) + tn(coefficients, link_ref[j])
        for p in range(many):
            px, py = p // down * side, p % down * side
            x[px : px + side, py : py + side] = value[p * lines : (p + 1) * lines].reshape(side, side, 128)
    win = Window(f.shape[:2])
    smoothed_residual(win, f, x1, x2, t, r, 2)
    restrict(r, pair, coarse_ref, 0, 0)
    send(out_ref, nt(v_ref[...], flat(coarse_ref)))


def whole_down_kernel(
    f_ref, got_ref, om_ref, power_ref, link_ref, v_ref, coarse_ref, out_ref, x1, x2, t, r, pair
):
    win = Window(f_ref.shape[:2])
    ends = ends_from(om_ref, got_ref)
    line_powers(flat(f_ref), ends, power_ref, link_ref, 2, (x1, x2))
    smoothed_residual(win, f_ref, x1, x2, t, r, 2)
    restrict(r, pair, coarse_ref, 0, 0)
    send(out_ref, nt(v_ref[...], flat(coarse_ref)))


def whole_known_kernel(
    level, e_ref, f_ref, got_ref, om_ref, power_ref, link_ref, known_ref, x1, x2, x3, x4, t0, t1
):
    win = Window(f_ref.shape[:2])
    ends = ends_from(om_ref, got_ref)
    xs = (x1, x2, x3, x4)
    line_powers(flat(f_ref), ends, power_ref, link_ref, POWERS, xs, exact=True)
    inverse_e = 1.0 / jnp.full((f_ref.shape[1], 128), e_ref[level], F32)
    src, scale = horner(win, xs, KNOWN, t0, t1, 4)

    def known(i):
        known_ref[i] = (KNOWN[0] * x1[i] + scale * win.around(src, i)) * inverse_e

    rows(0, win.x, known)


def clear_edges(pad, margin):
    x, y = pad.shape[:2]
    zero_rows = jnp.zeros((margin, y, 128), F32)
    zero_cols = jnp.zeros((x, margin, 128), F32)
    pad[0:margin] = zero_rows
    pad[x - margin : x] = zero_rows
    pad[:, 0:margin] = zero_cols
    pad[:, y - margin : y] = zero_cols


def cut(where_ref, pad, out_ref, margin):
    sx, sy = out_ref.shape[0] - 2 * margin, out_ref.shape[1] - 2 * margin
    x_at = where_ref[0] * sx
    y_at = pl.multiple_of(where_ref[1] * sy, 8)

    def one(i):
        out_ref[i] = pad[x_at + i, pl.ds(y_at, out_ref.shape[1]), :]

    rows(0, out_ref.shape[0], one)


def bottom_kernel(e_ref, f_ref, got_ref, om_ref, power_ref, link_ref, v_ref, w_ref, out_ref, x1, x2, c):
    win = Window(f_ref.shape[:2])
    ends = ends_from(om_ref, got_ref)
    line_powers(flat(f_ref), ends, power_ref, link_ref, 2, (x1, x2), exact=True)
    inverse_e = 1.0 / jnp.full((f_ref.shape[1], 128), e_ref[LEVELS - 1], F32)

    def one(i):
        c[i] = (0.96 * x1[i] + 0.64 * win.around(x2, i)) * inverse_e

    rows(0, win.x, one)
    prolong(c, True, w_ref, Window(w_ref.shape[:2]), 0, 0, win.x, win.y)
    send(out_ref, exact_nt(v_ref[...], flat(w_ref)))


def whole_up_kernel(
    margin, where_ref, w_ref, known_ref, got_ref, om_ref, power_ref, link_ref, v_ref,
    fine_ref, out_ref, x1, x2, t, c, fine, pad
):
    win = Window(w_ref.shape[:2])
    ends = ends_from(om_ref, got_ref)
    line_powers(flat(w_ref), ends, power_ref, link_ref, 2, (x1, x2), exact=True)
    smoothed_residual(win, w_ref, x1, x2, t, c, 2, masked=True, add=known_ref)
    prolong(c, True, fine, Window(fine.shape[:2]), 0, 0, win.x, win.y)
    clear_edges(pad, margin)

    def place(i):
        pad[i + margin, margin : margin + fine.shape[1]] = fine[i]

    rows(0, fine.shape[0], place)
    cut(where_ref, pad, fine_ref, margin)
    send(out_ref, exact_nt(v_ref[...], flat(fine_ref)))


def up_kernel(
    halo, fine_halo, grid, where_ref, w_ref, known_ref, got_ref, om_ref, power_ref, link_ref, v_ref,
    fine_ref, out_ref, x1, x2, t, c
):
    hx, hy = halo
    fx, fy = fine_halo
    sx, sy = w_ref.shape[0] - 2 * hx, w_ref.shape[1] - 2 * hy
    ix, iy = where_ref[0], where_ref[1]
    win = Window(w_ref.shape[:2], (ix * sx - hx, iy * sy - hy), grid)
    fine_win = Window(
        fine_ref.shape[:2], (2 * ix * sx - fx, 2 * iy * sy - fy), (2 * grid[0], 2 * grid[1])
    )
    ends = ends_from(om_ref, got_ref)
    line_powers(flat(w_ref), ends, power_ref, link_ref, 2, (x1, x2), exact=True)
    c[...] = jnp.zeros_like(c)
    smoothed_residual(win, w_ref, x1, x2, t, c, 2, masked=True, add=known_ref)
    odd = fx % 2
    count_x = (fine_ref.shape[0] + 2 * odd) // 2
    if odd:
        x_from = hx - (fx + 1) // 2
        prolong_odd(c, fine_ref, fine_win, x_from, hy - fy // 2, count_x, fine_ref.shape[1] // 2)
    else:
        prolong(c, False, fine_ref, fine_win, hx - fx // 2, hy - fy // 2, count_x, fine_ref.shape[1] // 2)
    send(out_ref, exact_nt(v_ref[...], flat(fine_ref)))


def prolong_odd(src, out, win, x_from, y_from, count_x, count_y):
    for i in range(count_x):
        at = x_from + i
        for odd, other in ((0, at - 1), (1, at + 1)):
            row = 2 * i + odd - 1
            if row < 0 or row >= out.shape[0]:
                continue
            v = 0.75 * src[at] + 0.25 * src[other]
            low, high = shifted(v, False)
            for parity, side in ((0, low), (1, high)):
                w = 0.75 * v + 0.25 * side
                out[row, pl.ds(parity, count_y, stride=2), :] = w[y_from : y_from + count_y]
    win.each(0, out, lambda i: win.mask(i, win.get(out, i)))


def final_kernel(
    halo, grid, where_ref, e_ref, w_ref, known_ref, twice_ref, got_ref, om_ref, power_ref, link_ref,
    m_ref, m_link_ref, u_ref, r_ref, x1, x2, xm, t0, t1
):
    hx, hy = halo
    sx, sy = w_ref.shape[0] - 2 * hx, w_ref.shape[1] - 2 * hy
    win = Window(w_ref.shape[:2], (where_ref[0] * sx - hx, where_ref[1] * sy - hy), grid)
    ends = ends_from(om_ref, got_ref)
    field = flat(w_ref)
    line_powers(field, ends, power_ref, link_ref, 2, (x1, x2), exact=True)
    xm[...] = (exact_nt(field, m_ref[...]) + exact_tn(ends, m_link_ref[...])).reshape(xm.shape)
    e = e_ref[0]

    lo, hi = win.span(hx - 2)

    def inner(i):
        one = 0.32 * win.get(x1, i)
        two = win.mask(i, 0.64 * win.around(x2, i))
        win.put(t0, i, one + two)
        win.put(t1, i, e * (one - two))

    rows(lo, hi, inner)
    win.each(hx - 1, x2, lambda i: (0.28 * e) * win.get(w_ref, i) + win.mask(i, win.around(t1, i)))
    lo, hi = win.span(hx)
    cut_y = hy - win.lo

    def last(i):
        u = 0.04 * win.get(w_ref, i) + win.around(t0, i)
        u_ref[i - hx] = known_ref[i - hx] + u[cut_y : cut_y + sy]
        r = 0.04 * win.get(xm, i) + win.around(x2, i)
        r_ref[i - hx] = twice_ref[i - hx] - r[cut_y : cut_y + sy]

    rows(lo, hi, last)


def call(kernel, outs, scratch, smem, *args, flops=0):
    specs = [
        pl.BlockSpec(memory_space=pltpu.SMEM if k in smem else pltpu.VMEM) for k in range(len(args))
    ]
    out_specs = [pl.BlockSpec(memory_space=pltpu.VMEM) for _ in outs]
    return pl.pallas_call(
        kernel,
        out_shape=[jax.ShapeDtypeStruct(s, F32) for s in outs],
        in_specs=specs,
        out_specs=out_specs,
        scratch_shapes=[pltpu.VMEM(s, F32) for s in scratch],
        compiler_params=pltpu.CompilerParams(vmem_limit_bytes=VMEM_LIMIT),
        cost_estimate=pl.CostEstimate(flops=int(flops) or 1000000, bytes_accessed=1000000, transcendentals=0),
    )(*args)


def exchange(copies, axes="gz"):
    got = lax.all_to_all(copies, axes, 0, 0, tiled=True)
    return got


def stacked(copies):
    got = exchange(copies)
    return got.reshape(got.shape[0] * got.shape[1], got.shape[2])


def edges(v, axis, dim, width):
    size, length = lax.axis_size(axis), v.shape[dim]
    up = [(i, i + 1) for i in range(size - 1)]
    last = lax.slice_in_dim(v, length - width, length, axis=dim)
    first = lax.slice_in_dim(v, 0, width, axis=dim)
    return lax.ppermute(last, axis, up), lax.ppermute(first, axis, [(b, a) for a, b in up])


def halo_y(v, width):
    return edges(v, "gy", 1, width)


def halo_x(v, width):
    low, high = edges(v, "gx", 0, width)
    return jnp.concatenate([low, v, high], axis=0)


def body(right_side, z_faces, xy_coupling, block_inverse):
    part = functools.partial
    gx, gy, gz = (lax.axis_size(a) for a in ("gx", "gy", "gz"))
    n = z_faces.shape[0]
    where = jnp.stack([lax.axis_index(a) for a in ("gx", "gy", "gz")]).astype(jnp.int32)
    sx, sy = right_side.shape[0], right_side.shape[1]
    grids = [(gx * (sx >> l), gy * (sy >> l)) for l in range(LEVELS)]
    e = xy_coupling
    faces = z_faces.reshape(1, n)

    setup = call(
        powers_kernel,
        [(POWERS, n, n)] * LEVELS + [(8, n)] * LEVELS + [(POWERS, 8, n)] * LEVELS + [(8, n), (16, n), (gz, 12, 8, n)],
        [],
        (1,),
        block_inverse, e, faces,
    )
    power, ends, link = (setup[k * LEVELS : (k + 1) * LEVELS] for k in range(3))
    ends_up, basis, table = setup[3 * LEVELS :]
    low, high, table = lax.optimization_barrier((*halo_y(right_side, 12), table))
    f0 = halo_x(jnp.concatenate([low, right_side, high], axis=1), 12)
    table = exchange(table)
    *om, om_up, m_matrix, m_link, mix, w2_map = call(
        coupling_kernel,
        [(8, n)] * LEVELS + [(8, n), (n, n), (8, n), (11, n, n), (8, n)],
        [(gz, 8, 8, n), (n, n)],
        (0, 2),
        where, table, e, faces, basis,
    )

    s0, s1, s2 = (sx, sy), (sx // 2, sy // 2), (sx // 4, sy // 4)
    ext0, ext1 = (sx + 24, sy + 24), (sx // 2 + 10, sy // 2 + 16)
    cube0, cube1 = ext0 + (n,), ext1 + (n,)
    lines0, lines1 = ext0[0] * ext0[1], ext1[0] * ext1[1]
    lanes = padded_lanes(lines0) + padded_lanes(lines1) + padded_lanes(s2[0] * s2[1])
    copies, f1_local, f2_local = call(
        part(local_down_kernel, s0, s1, grids),
        [(gz, 8, lanes), cube1, s2 + (n,)],
        [cube0] * 4 + [(ext1[0], ext0[1], n)] + [cube1] * 4 + [(s2[0], ext1[1], n)],
        (0,),
        where, f0, power[0], power[1], ends[0], ends[1], ends[2],
    )
    got = stacked(copies)
    many = gx * gy
    f1, own1, parts = call(
        part(joined_down_kernel, s0, s1, ext0, grids),
        [cube1, cube1, (many, s2[0] + 1, s2[1], n)],
        [cube0] * 3 + [(ext1[0], ext0[1], n)] + [cube1] * 4 + [(s2[0], ext1[1], n), s2 + (n,)],
        (0,),
        where, got, f1_local, f2_local, mix, om[2], w2_map,
    )
    parts = lax.all_to_all(parts, ("gx", "gy"), 0, 0, tiled=True)
    inner0 = (sx + 8, sy + 8, n)
    known0, twice0 = call(
        part(known_zero_kernel, s0, ext0, grids[0]),
        [s0 + (n,), s0 + (n,)],
        [inner0] * 8,
        (0, 1),
        where, e, f0, got, mix, power[0], link[0],
        flops=20000000000,
    )
    (known1,) = call(
        part(known_one_kernel, s1, grids[1]),
        [cube1],
        [cube1] * 6,
        (0, 1),
        where, e, f1, own1, power[1], link[1],
        flops=10000000000,
    )
    parts, known0, twice0, known1 = lax.optimization_barrier((parts, known0, twice0, known1))

    cubes = [g + (n,) for g in grids]
    lines = [g[0] * g[1] for g in grids]
    margin = s2[0]
    region = (3 * s2[0], 3 * s2[1], n)
    padded = (grids[2][0] + 2 * margin, grids[2][1] + 2 * margin, n)
    f3, copies = call(
        part(gathered_down_kernel, gx, gy),
        [cubes[3], (gz, 8, lines[3])],
        [cubes[2], (lines[2], n), (8, lines[2])] + [cubes[2]] * 4 + [(grids[3][0], grids[2][1], n)],
        (),
        parts, power[2], link[2], ends[3],
    )
    got3 = stacked(copies)
    (known2,) = call(
        part(known_two_kernel, gx, gy, grids[2]),
        [region],
        [(region[0] * region[1], n), (8, region[0] * region[1])] + [region] * 6,
        (0, 1),
        where, e, parts, power[2], link[2],
        flops=8000000000,
    )
    got3, known2 = lax.optimization_barrier((got3, known2))
    f4, copies = call(
        whole_down_kernel,
        [cubes[4], (gz, 8, lines[4])],
        [cubes[3]] * 4 + [(grids[4][0], grids[3][1], n)],
        (),
        f3, got3, om[3], power[3], link[3], ends[4],
    )
    got4 = stacked(copies)
    (known3,) = call(
        part(whole_known_kernel, 3),
        [cubes[3]],
        [cubes[3]] * 6,
        (0,),
        e, f3, got3, om[3], power[3], link[3],
        flops=8000000000,
    )
    got4, known3 = lax.optimization_barrier((got4, known3))
    w3, copies = call(
        bottom_kernel,
        [cubes[3], (gz, 8, lines[3])],
        [cubes[4]] * 3,
        (0,),
        e, f4, got4, om[4], power[4], link[4], ends[3],
    )
    w2, copies = call(
        part(whole_up_kernel, margin),
        [region, (gz, 8, region[0] * region[1])],
        [cubes[3]] * 4 + [cubes[2], padded],
        (0,),
        where, w3, known3, stacked(copies), om[3], power[3], link[3], ends[2],
    )

    h0, h1 = (4, 4), (5, 8)
    cube0, lines0 = inner0, inner0[0] * inner0[1]
    w1, copies = call(
        part(up_kernel, (margin, margin), h1, grids[2]),
        [cube1, (gz, 8, lines1)],
        [region] * 4,
        (0,),
        where, w2, known2, stacked(copies), om[2], power[2], link[2], ends[1],
    )
    w0, copies = call(
        part(up_kernel, h1, h0, grids[1]),
        [cube0, (gz, 8, lines0)],
        [cube1] * 4,
        (0,),
        where, w1, known1, stacked(copies), om[1], power[1], link[1], ends_up,
    )
    u, r = call(
        part(final_kernel, h0, grids[0]),
        [(sx, sy, n), (sx, sy, n)],
        [cube0] * 5,
        (0, 1),
        where, e, w0, known0, twice0, stacked(copies), om_up, power[0], link[0], m_matrix, m_link,
    )
    return u, r


def solution(mesh):
    return jax.shard_map(
        body,
        mesh=mesh,
        in_specs=(P("gx", "gy", "gz"), P("gz"), P(), P(None, "gz", None)),
        out_specs=(P("gx", "gy", "gz"), P("gx", "gy", "gz")),
        check_vma=False,
    )
```

time: 261 us -> 208 us (0.80)
  blocking collectives: 108 us -> 44.9 us
  waiting for transfers between devices: 15.4 us -> 29 us
  starting transfers between devices: 39.9 us -> 50.1 us
  local copies, waits for them, and re-layouts: 9.93 us -> 4.43 us
  Pallas kernels: 81 us -> 75.6 us
    all_to_all x1 -> x0, blocking collectives: 35.4 us -> none  [body(): lax.all_to_all(jnp.broadcast_to(f2[None], (many, s2x, s2y, n)), ('gx', 'g...]
    all_to_all x6 -> x4, blocking collectives: 72.2 us -> 44.9 us  [exchange(): got = lax.all_to_all(copies, axes, 0, 0, tiled=True)]
    all_to_all x0 -> x1, waiting for transfers between devices: none -> 14.4 us  [body(): parts = lax.all_to_all(parts, ('gx', 'gy'), 0, 0, tiled=True)]
    all_to_all x0 -> x1, starting transfers between devices: none -> 12.7 us  [body(): parts = lax.all_to_all(parts, ('gx', 'gy'), 0, 0, tiled=True)]
    ppermute x8 -> x4, waiting for transfers between devices: 11.4 us -> 1.37 us  [the longest x2 1.36 us: edges(): lax.ppermute(first, axis, [(b, a) for a, b in up])]
    all_to_all x4, waiting for transfers between devices: 3.93 us -> 13.2 us  [exchange(): got = lax.all_to_all(copies, axes, 0, 0, tiled=True)]
    ppermute x8 -> x4, starting transfers between devices: 20 us -> 11.8 us  [the longest x2 9.21 us: edges(): lax.ppermute(last, axis, up)]
    all_to_all x4, starting transfers between devices: 19.8 us -> 25.6 us  [exchange(): got = lax.all_to_all(copies, axes, 0, 0, tiled=True)]
  transfers between devices with their start and end apart: 12 -> 9, of which waited for: 6 -> 5; matrix products, arithmetic and copies ran while one was open for 3% -> 1% of each run, Pallas kernels for 9% -> 17%
where the time goes in v2:
time: 208 us; the launch traced here: 207 us
  Pallas kernels  75.6 us (36%)
  starting transfers between devices  50.1 us (24%)
  blocking collectives  44.9 us (22%)
  waiting for transfers between devices  29 us (14%)
  local copies, waits for them, and re-layouts  4.43 us (2%)
    pallas_call x15, Pallas kernels, call(): pl.pallas_call(kernel, out_shape=[jax.ShapeDtypeStruct(s, F32) for s in o...  75.6 us
    all_to_all x4, blocking collectives, exchange(): got = lax.all_to_all(copies, axes, 0, 0, tiled=True)  44.9 us
    all_to_all x4, starting transfers between devices, exchange(): got = lax.all_to_all(copies, axes, 0, 0, tiled=True)  25.6 us
    all_to_all x1, waiting for transfers between devices, body(): parts = lax.all_to_all(parts, ('gx', 'gy'), 0, 0, tiled=True)  14.4 us
    all_to_all x4, waiting for transfers between devices, exchange(): got = lax.all_to_all(copies, axes, 0, 0, tiled=True)  13.2 us
    all_to_all x1, starting transfers between devices, body(): parts = lax.all_to_all(parts, ('gx', 'gy'), 0, 0, tiled=True)  12.7 us
    ppermute x2, starting transfers between devices, edges(): lax.ppermute(last, axis, up)  9.21 us
  transfers between devices with their start and end apart: 9, of which 5 were waited for; matrix products, arithmetic and copies ran while one was open for 1% of the time, Pallas kernels for 17%

profile of v2, /device:TPU:1, one launch (start us, length us, event | category | flops | bytes accessed | tf_op | source)
XLA Modules:
  0.0 206.7 jit_solution(15951680985560944571)
XLA Ops:
  1.8 1.3 collective-permute-start.1
  3.1 5.0 %collective-permute-start = (f32[32,12,128]{2,1,0:T(8,128)S(1)}, f32[32,12,128]{2,1,0:T(8,128)S(1)}, u32[]{:S(2)}, u32[]{:S(2)}) collective-permute-start(f32[32,12,128]{2,1,0:T(8,128)S(1)} %get-tuple-element.121), channel_id=1, source_target_pairs={{0,8},{8,16},{16,24},{24,32},{32,40},{40,48},{48,56},{1,9},{9,17},... | collective-permute-start | bytes 589832 | tf_op jit(solution)/shard_map/ppermute | solution.py:808
  8.1 3.8 %shard_map.59 = (f32[4,128,128]{2,1,0:T(8,128)}, f32[4,128,128]{2,1,0:T(8,128)}, f32[4,128,128]{2,1,0:T(8,128)}, f32[4,128,128]{2,1,0:T(8,128)}, f32[4,128,128]{...) custom-call(f32[5,128,128]{2,1,0:T(8,128)} %g_ref.1, ...), custom_call_target="tpu_custom_call" | custom-call | flops 1000000 | bytes 1000000 | tf_op jit(solution)/shard_map/pallas_call | solution.py:782
  12.0 4.2 %collective-permute-start.2 = (f32[12,56,128]{2,1,0:T(8,128)S(1)}, f32[12,56,128]{2,1,0:T(8,128)S(1)}, u32[]{:S(2)}, u32[]{:S(2)}) collective-permute-start(f32[12,56,128]{2,1,0:T(8,128)S(1)} %get-tuple-element.118), channel_id=1, source_target_pairs={{0,64},{64,128},{128,192},{1,65},{65,129},{129,193},{2,66},{66,130... | collective-permute-start | bytes 1032200 | tf_op jit(solution)/shard_map/ppermute | solution.py:808
  16.2 1.3 collective-permute-start.3
  17.5 6.4 %all-to-all-start.1 = ((f32[8,12,8,128]{3,2,1,0:T(8,128)}), f32[8,12,8,128]{3,2,1,0:T(8,128)S(1)}, u32[]{:S(2)}, u32[]{:S(2)}) async-start(f32[8,12,8,128]{3,2,1,0:T(8,128)} %get-tuple-element.71), calls=%async_computation.1 | async-start | bytes 786432 | tf_op jit(solution)/shard_map/all_to_all | solution.py:794
  24.4 1.4 collective-permute-done.3
  25.8 1.3 pad_maximum_fusion.f_ref
  27.1 6.9 %shard_map.60 = (f32[8,8,4224]{2,1,0:T(8,128)}, f32[26,32,128]{2,1,0:T(8,128)}, f32[8,8,128]{2,1,0:T(8,128)}) custom-call(s32[3]{0:T(128)} %pad_add_fusion.where_ref, f32[56,56,128]{2,1,0:T(8,128)} %pad_maximum_fusion.f_ref, f32[4,128,128]{2,1,0:T(8,128)} %get-tuple-element.63.power0.power_ref, f32[4,128,128]{2,1,0:T(8,128)} %get-tuple-element.64.power1.power_ref, ...), custom_call_target="tpu_custom_call" | custom-call | flops 1000000 | bytes 1000000 | tf_op jit(solution)/shard_map/pallas_call | solution.py:782
  34.0 7.2 %all-to-all-start = ((f32[8,8,4224]{2,1,0:T(8,128)}), f32[8,8,4224]{2,1,0:T(8,128)S(1)}, u32[]{:S(2)}, u32[]{:S(2)}) async-start(f32[8,8,4224]{2,1,0:T(8,128)} %get-tuple-element.68), calls=%async_computation | async-start | bytes 2162688 | tf_op jit(solution)/shard_map/all_to_all | solution.py:794
  41.3 3.3 %shard_map.61 = (f32[8,128]{1,0:T(8,128)}, f32[8,128]{1,0:T(8,128)}, f32[8,128]{1,0:T(8,128)}, f32[8,128]{1,0:T(8,128)}, f32[8,128]{1,0:T(8,128)}, /*index=5*/f3...) custom-call(s32[3]{0:T(128)} %pad_add_fusion.where_ref, ...), custom_call_target="tpu_custom_call" | custom-call | flops 1000000 | bytes 1000000 | tf_op jit(solution)/shard_map/pallas_call | solution.py:782
  44.5 12.0 %all-to-all-done = f32[8,8,4224]{2,1,0:T(8,128)S(1)} async-done(((f32[8,8,4224]{2,1,0:T(8,128)}), f32[8,8,4224]{2,1,0:T(8,128)S(1)}, u32[]{:S(2)}, u32[]{:S(2)}) %all-to-all-start) | async-done | bytes 1081376 | tf_op jit(solution)/shard_map/all_to_all | solution.py:794
  57.6 6.9 %shard_map.62 = (f32[26,32,128]{2,1,0:T(8,128)}, f32[26,32,128]{2,1,0:T(8,128)}, f32[32,9,8,128]{3,2,1,0:T(8,128)}) custom-call(s32[3]{0:T(128)} %pad_add_fusion.where_ref, f32[64,4224]{1,0:T(8,128)} %bitcast.11, f32[26,32,128]{2,1,0:T(8,128)} %get-tuple-element.69.f1_local, f32[8,8,128]{2,1,0:T(8,128)} %get-tuple-element.70.f2_local, ...), custom_call_target="tpu_custom_call" | custom-call | flops 1000000 | bytes 1000000 | tf_op jit(solution)/shard_map/pallas_call | solution.py:782
  64.5 12.7 %all-to-all-start.2 = ((f32[32,9,8,128]{3,2,1,0:T(8,128)}), f32[32,9,8,128]{3,2,1,0:T(8,128)S(1)}, u32[]{:S(2)}, u32[]{:S(2)}) async-start(f32[32,9,8,128]{3,2,1,0:T(8,128)} %get-tuple-element.76), calls=%async_computation.2 | async-start | bytes 2359296 | tf_op jit(solution)/shard_map/all_to_all | solution.py:871
  77.2 5.2 %shard_map.64.known_ref = f32[26,32,128]{2,1,0:T(8,128)} custom-call(s32[3]{0:T(128)} %pad_add_fusion.where_ref, f32[5]{0:T(128)} %e_ref.15, f32[26,32,128]{2,1,0:T(8,128)} %get-tuple-element.80.f_ref, f32[26,32,128]{2,1,0:T(8,128)} %get-tuple-element.81.own_ref, f32[4,128,128]{2,1,0:T(8,128)} %get-tuple-element.64.power1.power_ref, ...), custom_call_target="tpu_custom_call" | custom-call | flops 10000000000 | bytes 1000000 | tf_op jit(solution)/shard_map/pallas_call | solution.py:782
  82.4 8.0 %shard_map.63 = (f32[32,32,128]{2,1,0:T(8,128)}, f32[32,32,128]{2,1,0:T(8,128)}) custom-call(s32[3]{0:T(128)} %pad_add_fusion.where_ref, f32[5]{0:T(128)} %e_ref.15, f32[56,56,128]{2,1,0:T(8,128)} %pad_maximum_fusion.f_ref, f32[64,4224]{1,0:T(8,128)} %bitcast.12, f32[11,128,128]{2,1,0:T(8,128)} %get-tuple-element.73.mix_ref, ...), custom_call_target="tpu_custom_call" | custom-call | flops 20000000000 | bytes 1000000 | tf_op jit(solution)/shard_map/pallas_call | solution.py:782
  90.4 14.4 %all-to-all-done.2.parts_ref = f32[32,9,8,128]{3,2,1,0:T(8,128)S(1)} async-done(((f32[32,9,8,128]{3,2,1,0:T(8,128)}), f32[32,9,8,128]{3,2,1,0:T(8,128)S(1)}, u32[]{:S(2)}, u32[]{:S(2)}) %all-to-all-start.2) | async-done | bytes 1179680 | tf_op jit(solution)/shard_map/all_to_all | solution.py:871
  105.9 5.1 %shard_map.65 = (f32[16,32,128]{2,1,0:T(8,128)}, f32[8,8,512]{2,1,0:T(8,128)}) custom-call(f32[32,9,8,128]{3,2,1,0:T(8,128)} %copy-done.1, f32[4,128,128]{2,1,0:T(8,128)} %get-tuple-element.84.power_ref, f32[4,8,128]{2,1,0:T(8,128)} %get-tuple-element.85.link_ref, f32[8,128]{1,0:T(8,128)} %get-tuple-element.86.v_ref), custom_call_target="tpu_custom_call" | custom-call | flops 1000000 | bytes 1000000 | tf_op jit(solution)/shard_map/pallas_call | solution.py:782
  111.0 7.8 %all-to-all-start.3 = ((f32[8,8,512]{2,1,0:T(8,128)}), f32[8,8,512]{2,1,0:T(8,128)S(1)}, u32[]{:S(2)}, u32[]{:S(2)}) async-start(f32[8,8,512]{2,1,0:T(8,128)} %get-tuple-element.88), calls=%async_computation.3 | async-start | bytes 262144 | tf_op jit(solution)/shard_map/all_to_all | solution.py:794
  118.8 4.6 %shard_map.66.known_ref = f32[24,24,128]{2,1,0:T(8,128)} custom-call(s32[3]{0:T(128)} %pad_add_fusion.where_ref, f32[5]{0:T(128)} %e_ref.15, f32[32,9,8,128]{3,2,1,0:T(8,128)} %copy-done.1, f32[4,128,128]{2,1,0:T(8,128)} %get-tuple-element.84.power_ref, f32[4,8,128]{2,1,0:T(8,128)} %get-tuple-element.85.link_ref), custom_call_target="tpu_custom_call" | custom-call | flops 8000000000 | bytes 1000000 | tf_op jit(solution)/shard_map/pallas_call | solution.py:782
  124.7 3.0 %shard_map.67 = (f32[8,16,128]{2,1,0:T(8,128)}, f32[8,8,128]{2,1,0:T(8,128)}) custom-call(f32[16,32,128]{2,1,0:T(8,128)} %get-tuple-element.87.f_ref, f32[64,512]{1,0:T(8,128)} %bitcast.17, f32[8,128]{1,0:T(8,128)} %get-tuple-element.90.om_ref, f32[4,128,128]{2,1,0:T(8,128)} %get-tuple-element.91.power_ref, f32[4,8,128]{2,1,0:T(8,128)} %get-tuple-element.92.link_ref, ...), custom_call_target="tpu_custom_call" | custom-call | flops 1000000 | bytes 1000000 | tf_op jit(solution)/shard_map/pallas_call | solution.py:782
  127.8 4.2 %all-to-all-start.4 = ((f32[8,8,128]{2,1,0:T(8,128)}), f32[8,8,128]{2,1,0:T(8,128)S(1)}, u32[]{:S(2)}, u32[]{:S(2)}) async-start(f32[8,8,128]{2,1,0:T(8,128)} %get-tuple-element.95), calls=%async_computation.4 | async-start | bytes 65536 | tf_op jit(solution)/shard_map/all_to_all | solution.py:794
  131.9 4.2 %shard_map.68.known_ref = f32[16,32,128]{2,1,0:T(8,128)} custom-call(f32[5]{0:T(128)} %e_ref.15, f32[16,32,128]{2,1,0:T(8,128)} %get-tuple-element.87.f_ref, f32[64,512]{1,0:T(8,128)} %bitcast.18, f32[8,128]{1,0:T(8,128)} %get-tuple-element.90.om_ref, f32[4,128,128]{2,1,0:T(8,128)} %get-tuple-element.91.power_ref, f32[4,8,128]{2,1,0:T(8,128)} %get-tuple-element.92.link_ref), custom_call_target="tpu_custom_call" | custom-call | flops 8000000000 | bytes 1000000 | tf_op jit(solution)/shard_map/pallas_call | solution.py:782
  137.3 2.9 %shard_map.69 = (f32[16,32,128]{2,1,0:T(8,128)}, f32[8,8,512]{2,1,0:T(8,128)}) custom-call(f32[5]{0:T(128)} %e_ref.15, f32[8,16,128]{2,1,0:T(8,128)} %get-tuple-element.94.f_ref, f32[64,128]{1,0:T(8,128)} %bitcast.19, f32[8,128]{1,0:T(8,128)} %get-tuple-element.97.om_ref, f32[4,128,128]{2,1,0:T(8,128)} %get-tuple-element.98.power_ref, ...), custom_call_target="tpu_custom_call" | custom-call | flops 1000000 | bytes 1000000 | tf_op jit(solution)/shard_map/pallas_call | solution.py:782
  140.1 9.9 %all_to_all.45 = f32[8,8,512]{2,1,0:T(8,128)} all-to-all(f32[8,8,512]{2,1,0:T(8,128)} %get-tuple-element.102), channel_id=1, replica_groups=mesh['gx'=4,'gy'=8,'gz'=8] {'gz'}, dimensions={0} | all-to-all | bytes 262144 | tf_op jit(solution)/shard_map/all_to_all | solution.py:794
  150.1 4.2 %shard_map.70 = (f32[24,24,128]{2,1,0:T(8,128)}, f32[8,8,576]{2,1,0:T(8,128)}) custom-call(s32[3]{0:T(128)} %pad_add_fusion.where_ref, f32[16,32,128]{2,1,0:T(8,128)} %get-tuple-element.100.w_ref, f32[16,32,128]{2,1,0:T(8,128)} %shard_map.68.known_ref, f32[64,512]{1,0:T(8,128)} %bitcast.16, f32[8,128]{1,0:T(8,128)} %get-tuple-element.90.om_ref, ...), custom_call_target="tpu_custom_call" | custom-call | flops 1000000 | bytes 1000000 | tf_op jit(solution)/shard_map/pallas_call | solution.py:782
  154.3 10.4 %all_to_all.46 = f32[8,8,576]{2,1,0:T(8,128)} all-to-all(f32[8,8,576]{2,1,0:T(8,128)} %get-tuple-element.105), channel_id=1, replica_groups=mesh['gx'=4,'gy'=8,'gz'=8] {'gz'}, dimensions={0} | all-to-all | bytes 294912 | tf_op jit(solution)/shard_map/all_to_all | solution.py:794
  164.7 4.2 %shard_map.71 = (f32[26,32,128]{2,1,0:T(8,128)}, f32[8,8,832]{2,1,0:T(8,128)}) custom-call(s32[3]{0:T(128)} %pad_add_fusion.where_ref, f32[24,24,128]{2,1,0:T(8,128)} %get-tuple-element.103.w_ref, f32[24,24,128]{2,1,0:T(8,128)} %shard_map.66.known_ref, f32[64,576]{1,0:T(8,128)} %bitcast.15, f32[8,128]{1,0:T(8,128)} %get-tuple-element.74.om2_ref.om_ref, ...), custom_call_target="tpu_custom_call" | custom-call | flops 1000000 | bytes 1000000 | tf_op jit(solution)/shard_map/pallas_call | solution.py:782
  168.9 11.1 %all_to_all.47 = f32[8,8,832]{2,1,0:T(8,128)} all-to-all(f32[8,8,832]{2,1,0:T(8,128)} %get-tuple-element.108), channel_id=1, replica_groups=mesh['gx'=4,'gy'=8,'gz'=8] {'gz'}, dimensions={0} | all-to-all | bytes 425984 | tf_op jit(solution)/shard_map/all_to_all | solution.py:794
  180.0 5.5 %shard_map.72 = (f32[40,40,128]{2,1,0:T(8,128)}, f32[8,8,1600]{2,1,0:T(8,128)}) custom-call(s32[3]{0:T(128)} %pad_add_fusion.where_ref, f32[26,32,128]{2,1,0:T(8,128)} %get-tuple-element.106.w_ref, f32[26,32,128]{2,1,0:T(8,128)} %shard_map.64.known_ref, f32[64,832]{1,0:T(8,128)} %bitcast.14, f32[8,128]{1,0:T(8,128)} %get-tuple-element.109.om_ref, ...), custom_call_target="tpu_custom_call" | custom-call | flops 1000000 | bytes 1000000 | tf_op jit(solution)/shard_map/pallas_call | solution.py:782
  185.4 13.5 %all_to_all.48 = f32[8,8,1600]{2,1,0:T(8,128)} all-to-all(f32[8,8,1600]{2,1,0:T(8,128)} %get-tuple-element.114), channel_id=1, replica_groups=mesh['gx'=4,'gy'=8,'gz'=8] {'gz'}, dimensions={0} | all-to-all | bytes 819200 | tf_op jit(solution)/shard_map/all_to_all | solution.py:794
  198.9 7.8 %shard_map.73 = (f32[32,32,128]{2,1,0:T(8,128)}, f32[32,32,128]{2,1,0:T(8,128)}) custom-call(s32[3]{0:T(128)} %pad_add_fusion.where_ref, f32[5]{0:T(128)} %e_ref.15, f32[40,40,128]{2,1,0:T(8,128)} %get-tuple-element.111.w_ref, f32[32,32,128]{2,1,0:T(8,128)} %get-tuple-element.112.known_ref, f32[32,32,128]{2,1,0:T(8,128)} %get-tuple-element.113.twice_ref, ...), custom_call_target="tpu_custom_call" | custom-call | flops 1000000 | bytes 1000000 | tf_op jit(solution)/shard_map/pallas_call | solution.py:782
  (21 shorter events, 6.2 us)
Async XLA Ops:
  0.6 11.2 %copy-start = (f32[32,32,128]{2,1,0:T(8,128)S(1)}, f32[32,32,128]{2,1,0:T(8,128)}, u32[]{:S(2)}) copy-start(f32[32,32,128]{2,1,0:T(8,128)} %param.4) | copy-start | bytes 1572868
  1.8 10.1 %collective-permute-start.1 = (f32[32,12,128]{2,1,0:T(8,128)S(1)}, f32[32,12,128]{2,1,0:T(8,128)S(1)}, u32[]{:S(2)}, u32[]{:S(2)}) collective-permute-start(f32[32,12,128]{2,1,0:T(8,128)S(1)} %get-tuple-element.120), channel_id=1, source_target_pairs={{8,0},{16,8},{24,16},{32,24},{40,32},{48,40},{56,48},{9,1},{17,9},... | collective-permute-start | bytes 589832 | tf_op jit(solution)/shard_map/ppermute | solution.py:808
  3.1 8.8 %collective-permute-start = (f32[32,12,128]{2,1,0:T(8,128)S(1)}, f32[32,12,128]{2,1,0:T(8,128)S(1)}, u32[]{:S(2)}, u32[]{:S(2)}) collective-permute-start(f32[32,12,128]{2,1,0:T(8,128)S(1)} %get-tuple-element.121), channel_id=1, source_target_pairs={{0,8},{8,16},{16,24},{24,32},{32,40},{40,48},{48,56},{1,9},{9,17},... | collective-permute-start | bytes 589832 | tf_op jit(solution)/shard_map/ppermute | solution.py:808
  12.0 12.5 %collective-permute-start.2 = (f32[12,56,128]{2,1,0:T(8,128)S(1)}, f32[12,56,128]{2,1,0:T(8,128)S(1)}, u32[]{:S(2)}, u32[]{:S(2)}) collective-permute-start(f32[12,56,128]{2,1,0:T(8,128)S(1)} %get-tuple-element.118), channel_id=1, source_target_pairs={{0,64},{64,128},{128,192},{1,65},{65,129},{129,193},{2,66},{66,130... | collective-permute-start | bytes 1032200 | tf_op jit(solution)/shard_map/ppermute | solution.py:808
  16.2 9.6 %collective-permute-start.3 = (f32[12,56,128]{2,1,0:T(8,128)S(1)}, f32[12,56,128]{2,1,0:T(8,128)S(1)}, u32[]{:S(2)}, u32[]{:S(2)}) collective-permute-start(f32[12,56,128]{2,1,0:T(8,128)S(1)} %get-tuple-element.119), channel_id=1, source_target_pairs={{64,0},{128,64},{192,128},{65,1},{129,65},{193,129},{66,2},{130,66... | collective-permute-start | bytes 1032200 | tf_op jit(solution)/shard_map/ppermute | solution.py:808
  17.5 16.6 %all-to-all-start.1 = ((f32[8,12,8,128]{3,2,1,0:T(8,128)}), f32[8,12,8,128]{3,2,1,0:T(8,128)S(1)}, u32[]{:S(2)}, u32[]{:S(2)}) async-start(f32[8,12,8,128]{3,2,1,0:T(8,128)} %get-tuple-element.71), calls=%async_computation.1 | async-start | bytes 786432 | tf_op jit(solution)/shard_map/all_to_all | solution.py:794
  34.0 7.3 %copy-start.3 = (f32[8,12,8,128]{3,2,1,0:T(8,128)}, f32[8,12,8,128]{3,2,1,0:T(8,128)S(1)}, u32[]{:S(2)}) copy-start(f32[8,12,8,128]{3,2,1,0:T(8,128)S(1)} %all-to-all-done.1.table_ref) | copy-start | bytes 1179652
  34.0 22.6 %all-to-all-start = ((f32[8,8,4224]{2,1,0:T(8,128)}), f32[8,8,4224]{2,1,0:T(8,128)S(1)}, u32[]{:S(2)}, u32[]{:S(2)}) async-start(f32[8,8,4224]{2,1,0:T(8,128)} %get-tuple-element.68), calls=%async_computation | async-start | bytes 2162688 | tf_op jit(solution)/shard_map/all_to_all | solution.py:794
  56.6 1.0 copy-start.2
  64.5 40.3 %all-to-all-start.2 = ((f32[32,9,8,128]{3,2,1,0:T(8,128)}), f32[32,9,8,128]{3,2,1,0:T(8,128)S(1)}, u32[]{:S(2)}, u32[]{:S(2)}) async-start(f32[32,9,8,128]{3,2,1,0:T(8,128)} %get-tuple-element.76), calls=%async_computation.2 | async-start | bytes 2359296 | tf_op jit(solution)/shard_map/all_to_all | solution.py:871
  104.8 1.0 copy-start.1
  111.0 13.1 %all-to-all-start.3 = ((f32[8,8,512]{2,1,0:T(8,128)}), f32[8,8,512]{2,1,0:T(8,128)S(1)}, u32[]{:S(2)}, u32[]{:S(2)}) async-start(f32[8,8,512]{2,1,0:T(8,128)} %get-tuple-element.88), calls=%async_computation.3 | async-start | bytes 262144 | tf_op jit(solution)/shard_map/all_to_all | solution.py:794
  124.1 0.7 copy-start.4
  127.8 8.9 %all-to-all-start.4 = ((f32[8,8,128]{2,1,0:T(8,128)}), f32[8,8,128]{2,1,0:T(8,128)S(1)}, u32[]{:S(2)}, u32[]{:S(2)}) async-start(f32[8,8,128]{2,1,0:T(8,128)} %get-tuple-element.95), calls=%async_computation.4 | async-start | bytes 65536 | tf_op jit(solution)/shard_map/all_to_all | solution.py:794
  136.7 0.6 copy-start.5

commit v3 on v2

--- a/solution.py
+++ b/solution.py
@@ -201,7 +201,7 @@
 def powers_kernel(g_ref, e_ref, zf_ref, *outs):
     levels, n = g_ref.shape[0], g_ref.shape[1]
     power_refs, ends_refs, link_refs = outs[0:levels], outs[levels : 2 * levels], outs[2 * levels : 3 * levels]
-    up_ref, basis_ref, table_ref = outs[3 * levels :]
+    up_ref, basis_ref, basis_up_ref, table_ref = outs[3 * levels :]
     table_ref[...] = jnp.zeros_like(table_ref)
     for level in range(levels):
         power_ref, ends_ref, link_ref = power_refs[level], ends_refs[level], link_refs[level]
@@ -225,17 +225,22 @@
                     link_ref[j, 2 * i + t : 2 * i + t + 1] = ends[2 * (j - i) + t] * inverse_e
         table_ref[0, 9, level : level + 1] = inverse_e
     table_ref[0, 8] = jnp.broadcast_to(zf_ref[...], (8, n))
-    zero = ends_refs[0][0:4] * (1.0 / jnp.full((4, n), e_ref[0], F32))
+    def columns(level):
+        return ends_refs[level][0:4] * (1.0 / jnp.full((4, n), e_ref[level], F32))
+
+    zero = columns(0)
     basis_ref[0:4] = zero
     basis_ref[4:8] = exact_nn(zero, power_refs[1][0])
     basis_ref[8:12] = exact_nn(zero, power_refs[1][1])
-    basis_ref[12:16] = ends_refs[1][0:4] * (1.0 / jnp.full((4, n), e_ref[1], F32))
-    basis = jnp.concatenate([basis_ref[...], jnp.zeros((n - 16, n), F32)], 0)
-    at = lax.broadcasted_iota(jnp.int32, (8, n), 1)
-    table_ref[0, 10] = jnp.where(at < 4, exact_nt(ends_refs[1][...], basis), 0.0)
-    table_ref[0, 11] = exact_nt(ends_refs[2][...], basis)
-    for m in range(1, table_ref.shape[0]):
-        table_ref[m] = table_ref[0]
+    basis_ref[12:16] = columns(1)
+    three = columns(3)
+    two = [three, exact_nn(three, power_refs[2][0]), exact_nn(three, power_refs[2][1]), columns(2)]
+    two = jnp.concatenate(two, 0)
+    basis_up_ref[...] = jnp.zeros_like(basis_up_ref)
+    basis_up_ref[0:16] = two
+    basis_up_ref[16:32] = exact_nn(two, power_refs[1][0])
+    basis_up_ref[32:48] = exact_nn(two, power_refs[1][1])
+    basis_up_ref[48:52] = columns(1)
     at = lax.broadcasted_iota(jnp.int32, (1, n), 1)
     up_ref[...] = jnp.zeros_like(up_ref)
     up_ref[0:4] = ends_refs[0][0:4]
@@ -243,8 +248,22 @@
     up_ref[5:6] = jnp.where(at == n - 1, 1.0, 0.0).astype(F32)
 
 
+    full_basis = jnp.concatenate([basis_ref[...], jnp.zeros((n - 16, n), F32)], 0)
+    at = lax.broadcasted_iota(jnp.int32, (8, n), 1)
+    first = jnp.where(at < 4, exact_nt(ends_refs[1][...], full_basis), 0.0)
+    second = exact_nt(ends_refs[2][...], full_basis)
+    shifted_ends = jnp.concatenate([jnp.zeros((4, n), F32), ends_refs[2][0:4]], 0)
+    third = jnp.where(at < 4, exact_nt(shifted_ends, basis_up_ref[...]), 0.0)
+    fourth = jnp.where(at < 16, exact_nt(ends_refs[1][...], basis_up_ref[...]), 0.0)
+    fifth = exact_nt(up_ref[...], basis_up_ref[...])
+    total = first + pltpu.roll(second, 4, 1) + pltpu.roll(third, 20, 1)
+    table_ref[0, 10] = total + pltpu.roll(fourth, 24, 1) + pltpu.roll(fifth, 40, 1)
+    for m in range(1, table_ref.shape[0]):
+        table_ref[m] = table_ref[0]
+
+
 def coupling_kernel(
-    where_ref, table_ref, e_ref, zf_ref, basis_ref, om0, om1, om2, om3, om4, om_up_ref, m_ref, m_link_ref, mix_ref, w2_ref, held, full
+    where_ref, table_ref, e_ref, zf_ref, basis_ref, om0, om1, om2, om3, om4, om_up_ref, m_ref, m_link_ref, mix_ref, up_mix_ref, w2_ref, held, full
 ):
     blocks, n = table_ref.shape[0], table_ref.shape[3]
     k_own = where_ref[2]
@@ -320,60 +339,103 @@
                 om_refs[level][2 * i + t : 2 * i + t + 1] = total[level : level + 1]
     om_up_ref[...] = om0[...]
 
-    def every(i, t, m):
+    lane = lane[0:1]
+    om_up_ref[4:5] = jnp.where((lane == 8 * (k_own - 1) + 5) & (k_own > 0), 1.0, 0.0).astype(F32)
+    om_up_ref[5:6] = jnp.where((lane == 8 * (k_own + 1) + 4) & (k_own < blocks - 1), 1.0, 0.0).astype(F32)
+    om_up_ref[6:8] = jnp.zeros((2, n), F32)
+
+    row = lax.broadcasted_iota(jnp.int32, (n, n), 0)
+    column = lax.broadcasted_iota(jnp.int32, (n, n), 1)
+
+    def every(i, t, m, offset):
         total = held[m, 2 * i + t]
         if i == 1:
             total = total + pltpu.roll(held[m, t], 2, 1)
-        return total
-
-    def matrix(slot, level, groups, own):
+        return pltpu.roll(total, offset, 1) if offset else total
+
+    def matrix(level, groups, own=None, offset=0):
         full[...] = jnp.zeros_like(full)
         for start, i, scale in groups:
             for m in range(blocks):
                 for t in range(2):
-                    row = start + 2 * m + t
-                    full[row : row + 1] = scale * every(i, t, m)[level : level + 1]
+                    at = start + 2 * m + t
+                    full[at : at + 1] = scale * every(i, t, m, offset)[level : level + 1]
         if own is not None:
             full[own : own + 8] = om_refs[level][...]
-        mix_ref[slot] = full[...].T
-
-    matrix(0, 0, [(0, 0, 0.32)], 64)
-    matrix(1, 0, [(0, 1, 0.64), (16, 0, 0.64)], None)
-    matrix(2, 1, [(96, 0, 0.32)], None)
-    matrix(3, 1, [(96, 1, 0.64), (112, 0, 0.64)], None)
-    matrix(4, 1, [], 0)
-    row = lax.broadcasted_iota(jnp.int32, (n, n), 0)
-    column = lax.broadcasted_iota(jnp.int32, (n, n), 1)
-
-    def spread(m):
-        return jnp.where(
-            (row < 16) & (column == (row >> 1) * 16 + 2 * m + (row & 1)), 1.0, 0.0
-        ).astype(F32)
-
-    def gathered(slot):
-        full[...] = jnp.zeros_like(full)
-        for m in range(blocks):
-            full[8 * m : 8 * m + 8] = exact_nn(table_ref[m, slot], spread(m))
-        return full[...]
-
-    one = gathered(10).T
+        return full[...].T
+
+    def gathered(offset, count):
+        tiles = jnp.concatenate([table_ref[m, 10] for m in range(blocks)], 0)
+        at = row - offset
+        place = (at >= 0) & (at < count) & (at == (column >> 4) * 2 + (column & 1))
+        value = exact_nn(tiles, jnp.where(place, 1.0, 0.0).astype(F32))
+        high = 8 * blocks
+        value = jnp.where((row[0:high] >> 3) == ((column[0:high] >> 1) & 7), value, 0.0)
+        return jnp.concatenate([value, jnp.zeros((n - high, n), F32)], 0)
 
     def diagonal(shift, scale):
         return jnp.where((row < 32) & (column == row + shift), scale, 0.0).astype(F32)
 
-    mix_ref[5] = diagonal(0, 0.04)
-    mix_ref[6] = exact_nn(one, mix_ref[2]) + diagonal(32, 0.32)
-    mix_ref[7] = exact_nn(one, mix_ref[3]) + diagonal(64, 0.64)
-    mix_ref[8] = exact_nn(one, mix_ref[4])
-    w2_ref[...] = exact_nn(om2[...], gathered(11))
+    def rest(slot_ref, base, level, once, twice, table):
+        slot_ref[base] = once
+        slot_ref[base + 1] = twice
+        slot_ref[base + 2] = diagonal(0, 0.04)
+        slot_ref[base + 3] = exact_nn(table, once) + diagonal(32, 0.32)
+        slot_ref[base + 4] = exact_nn(table, twice) + diagonal(64, 0.64)
+
+    mix_ref[0] = matrix(0, [(0, 0, 0.32)], 64)
+    mix_ref[1] = matrix(0, [(0, 1, 0.64), (16, 0, 0.64)])
+    one = gathered(0, 4).T
+    rest(mix_ref, 2, 1, matrix(1, [(96, 0, 0.32)]), matrix(1, [(96, 1, 0.64), (112, 0, 0.64)]), one)
+    mix_ref[7] = matrix(1, [], 0)
+    mix_ref[8] = exact_nn(one, mix_ref[7])
+    w2_ref[...] = exact_nn(om2[...], gathered(4, 16))
     basis = jnp.concatenate([basis_ref[...], jnp.zeros((n - 16, n), F32)], 0)
-    chosen = exact_tn(spread(k_own), basis)
+    own_rows = jnp.where(
+        (row < 16) & (column == (row >> 1) * 16 + 2 * k_own + (row & 1)), 1.0, 0.0
+    ).astype(F32)
+    chosen = exact_tn(own_rows, basis)
     mix_ref[9] = jnp.where(row < 32, chosen, 0.0)
     mix_ref[10] = chosen
-    lane = lane[0:1]
-    om_up_ref[4:5] = jnp.where((lane == 8 * (k_own - 1) + 5) & (k_own > 0), 1.0, 0.0).astype(F32)
-    om_up_ref[5:6] = jnp.where((lane == 8 * (k_own + 1) + 4) & (k_own < blocks - 1), 1.0, 0.0).astype(F32)
-    om_up_ref[6:8] = jnp.zeros((2, n), F32)
+
+    up_mix_ref[0] = matrix(3, [(0, 0, 0.32)])
+    up_mix_ref[1] = matrix(3, [(0, 1, 0.64), (16, 0, 0.64)])
+    once = matrix(2, [(96, 0, 0.32)], offset=4)
+    twice = matrix(2, [(96, 1, 0.64), (112, 0, 0.64)], offset=4)
+    rest(up_mix_ref, 2, 2, once, twice, gathered(20, 4).T)
+    both = matrix(1, [(0, 0, 1.0), (16, 1, 1.0)])
+    through = exact_nn(gathered(24, 16).T, both)
+    up_rows = om_up_ref[...]
+    for k, scale in enumerate((0.04, 0.32, 0.64)):
+        full[...] = jnp.zeros_like(full)
+        full[16 * k : 16 * k + 16] = scale * own_rows[0:16]
+        full[64:72] = scale * exact_nn(up_rows, gathered(40 + 16 * k, 16))
+        up_mix_ref[7 + k] = full[...].T
+    last = exact_nn(up_rows, gathered(88, 4))
+    wide_lane = lax.broadcasted_iota(jnp.int32, (8, n), 1)
+    full[...] = jnp.zeros_like(full)
+    for t in range(2):
+        full[48 + t : 49 + t] = jnp.where(lane == 2 * k_own + t, 0.32, 0.0).astype(F32)
+    full[64:72] = jnp.where(wide_lane < 16, 0.32 * last, 0.0)
+    mixed = full[...].T
+    up_mix_ref[8] = up_mix_ref[8] + exact_nn(through, mixed)
+    up_mix_ref[10] = exact_nn(both, mixed)
+    full[...] = jnp.zeros_like(full)
+    for t in range(2):
+        full[48 + t : 49 + t] = jnp.where(lane == 16 + 2 * k_own + t, 0.64, 0.0).astype(F32)
+        full[50 + t : 51 + t] = jnp.where(lane == 2 * k_own + t, 0.64, 0.0).astype(F32)
+    swapped = jnp.where(
+        wide_lane < 16,
+        pltpu.roll(last, n - 16, 1),
+        jnp.where(wide_lane < 32, pltpu.roll(last, 16, 1), 0.0),
+    )
+    full[64:72] = 0.64 * swapped
+    mixed = full[...].T
+    up_mix_ref[9] = up_mix_ref[9] + exact_nn(through, mixed)
+    up_mix_ref[11] = exact_nn(both, mixed)
+    full[...] = jnp.zeros_like(full)
+    full[64:72] = up_rows
+    up_mix_ref[12] = full[...].T
 
     above = jnp.minimum(k_own + 1, blocks - 1)
     top = table_ref[above, 8][0:1, 0:1]
@@ -478,10 +540,10 @@
     yf = halves(flat(y))
     f1_ref[...] = f1_local[...] + nn(yf, mix_ref[9]).reshape(f1_ref.shape)
     got1 = halves(got_ref[:, at1 : at1 + lanes1])
-    own1_ref[...] = (tn(got1, mix_ref[4, 0:rows_in]) + nn(yf, mix_ref[8])).reshape(own1_ref.shape)
-    h1s[...] = (tn(got1, mix_ref[2, 0:rows_in]) + nn(yf, mix_ref[6])).reshape(h1s.shape)
-    h2s[...] = (tn(got1, mix_ref[3, 0:rows_in]) + nn(yf, mix_ref[7])).reshape(h2s.shape)
-    f2s[...] = nn(yf, mix_ref[5]).reshape(f2s.shape)
+    own1_ref[...] = (tn(got1, mix_ref[7, 0:rows_in]) + nn(yf, mix_ref[8])).reshape(own1_ref.shape)
+    h1s[...] = (tn(got1, mix_ref[2, 0:rows_in]) + nn(yf, mix_ref[5])).reshape(h1s.shape)
+    h2s[...] = (tn(got1, mix_ref[3, 0:rows_in]) + nn(yf, mix_ref[6])).reshape(h2s.shape)
+    f2s[...] = nn(yf, mix_ref[4]).reshape(f2s.shape)
     trim = h1[0]
     win1.each(trim - 1, h1s, lambda i: win1.get(h1s, i) + win1.mask(i, win1.around(h2s, i)))
     win1.each(trim, f2s, lambda i: win1.get(f2s, i) + win1.around(h1s, i))
@@ -665,63 +727,154 @@
     rows(0, out_ref.shape[0], one)
 
 
-def bottom_kernel(e_ref, f_ref, got_ref, om_ref, power_ref, link_ref, v_ref, w_ref, out_ref, x1, x2, c):
+UP_LANES = (1664, 896, 512)
+
+
+def place_on_region(where_ref, fine, pad, out_ref, margin):
+    clear_edges(pad, margin)
+
+    def place(i):
+        pad[i + margin, margin : margin + fine.shape[1]] = fine[i]
+
+    rows(0, fine.shape[0], place)
+    cut(where_ref, pad, out_ref, margin)
+
+
+def up_windows(where_ref, s0, grids, region, ext1, ext0):
+    s1, s2 = (s0[0] // 2, s0[1] // 2), (s0[0] // 4, s0[1] // 4)
+    wins = []
+    for level, (shape, s) in enumerate(((ext0, s0), (ext1, s1), (region, s2))):
+        hx, hy = (shape[0] - s[0]) // 2, (shape[1] - s[1]) // 2
+        wins.append(Window(shape, (where_ref[0] * s[0] - hx, where_ref[1] * s[1] - hy), grids[level]))
+    return wins
+
+
+def to_level_one(src, out, win):
+    prolong_odd(src, out, win, 5, 4, (out.shape[0] + 2) // 2, out.shape[1] // 2)
+
+
+def to_level_zero(src, out, win):
+    prolong(src, False, out, win, 3, 6, out.shape[0] // 2, out.shape[1] // 2)
+
+
+def local_up_kernel(
+    s0, grids, margin, where_ref, e_ref, f_ref, got_ref, om_ref, power4, link4, known3, known2, known1,
+    power3, power2, power1, v3, v2, v1, v0, out_ref, c1_ref,
+    b1, b2, c4, w3, p1, p2, pt, c3, fine, pad, w2, q1, q2, qt, c2, w1, r1, r2, rt, w0
+):
     win = Window(f_ref.shape[:2])
     ends = ends_from(om_ref, got_ref)
-    line_powers(flat(f_ref), ends, power_ref, link_ref, 2, (x1, x2), exact=True)
+    line_powers(flat(f_ref), ends, power4, link4, 2, (b1, b2), exact=True)
     inverse_e = 1.0 / jnp.full((f_ref.shape[1], 128), e_ref[LEVELS - 1], F32)
 
     def one(i):
-        c[i] = (0.96 * x1[i] + 0.64 * win.around(x2, i)) * inverse_e
+        c4[i] = (0.96 * b1[i] + 0.64 * win.around(b2, i)) * inverse_e
 
     rows(0, win.x, one)
-    prolong(c, True, w_ref, Window(w_ref.shape[:2]), 0, 0, win.x, win.y)
-    send(out_ref, exact_nt(v_ref[...], flat(w_ref)))
-
-
-def whole_up_kernel(
-    margin, where_ref, w_ref, known_ref, got_ref, om_ref, power_ref, link_ref, v_ref,
-    fine_ref, out_ref, x1, x2, t, c, fine, pad
+    win3 = Window(w3.shape[:2])
+    prolong(c4, True, w3, win3, 0, 0, win.x, win.y)
+    win0, win1, win2 = up_windows(where_ref, s0, grids, w2.shape[:2], w1.shape[:2], w0.shape[:2])
+    at1, at2 = UP_LANES[0], UP_LANES[0] + UP_LANES[1]
+    out_ref[0] = jnp.zeros(out_ref.shape[1:], F32)
+
+    def local(win, w, known, power, x1, x2, t, c):
+        field = flat(w)
+        x1[...] = exact_nt(field, power[0]).reshape(x1.shape)
+        x2[...] = exact_nt(field, power[1]).reshape(x2.shape)
+        c[...] = jnp.zeros_like(c)
+        smoothed_residual(win, w, x1, x2, t, c, 2, masked=True, add=known)
+
+    def words(v_ref, w, first_row, at):
+        value = exact_nt(v_ref[...], flat(w))
+        out_ref[0, first_row : first_row + 4, at : at + value.shape[1]] = value[0:4]
+
+    words(v3, w3, 0, at2)
+    local(win3, w3, known3, power3, p1, p2, pt, c3)
+    prolong(c3, True, fine, Window(fine.shape[:2]), 0, 0, win3.x, win3.y)
+    place_on_region(where_ref, fine, pad, w2, margin)
+    words(v2, w2, 4, at1)
+    local(win2, w2, known2, power2, q1, q2, qt, c2)
+    to_level_one(c2, w1, win1)
+    words(v1, w1, 0, at1)
+    local(win1, w1, known1, power1, r1, r2, rt, c1_ref)
+    to_level_zero(c1_ref, w0, win0)
+    value = exact_nt(v0[...], flat(w0))
+    out_ref[0, :, 0 : value.shape[1]] = value
+    for m in range(1, out_ref.shape[0]):
+        out_ref[m] = out_ref[0]
+
+
+def finish_kernel(
+    s0, grids, margin, where_ref, e_ref, got_ref, c1_local, known_ref, twice_ref, mix_ref, basis_ref,
+    power_ref, link_ref, m_ref, m_link_ref, u_ref, r_ref,
+    d1, d2, d3, fine, pad, y2, g1, g2, g3, y1, h1, h2, h3, c1, w, q, x1, x2, xm, t0, t1
 ):
-    win = Window(w_ref.shape[:2])
-    ends = ends_from(om_ref, got_ref)
-    line_powers(flat(w_ref), ends, power_ref, link_ref, 2, (x1, x2), exact=True)
-    smoothed_residual(win, w_ref, x1, x2, t, c, 2, masked=True, add=known_ref)
-    prolong(c, True, fine, Window(fine.shape[:2]), 0, 0, win.x, win.y)
-    clear_edges(pad, margin)
-
-    def place(i):
-        pad[i + margin, margin : margin + fine.shape[1]] = fine[i]
-
-    rows(0, fine.shape[0], place)
-    cut(where_ref, pad, fine_ref, margin)
-    send(out_ref, exact_nt(v_ref[...], flat(fine_ref)))
-
-
-def up_kernel(
-    halo, fine_halo, grid, where_ref, w_ref, known_ref, got_ref, om_ref, power_ref, link_ref, v_ref,
-    fine_ref, out_ref, x1, x2, t, c
-):
-    hx, hy = halo
-    fx, fy = fine_halo
-    sx, sy = w_ref.shape[0] - 2 * hx, w_ref.shape[1] - 2 * hy
-    ix, iy = where_ref[0], where_ref[1]
-    win = Window(w_ref.shape[:2], (ix * sx - hx, iy * sy - hy), grid)
-    fine_win = Window(
-        fine_ref.shape[:2], (2 * ix * sx - fx, 2 * iy * sy - fy), (2 * grid[0], 2 * grid[1])
-    )
-    ends = ends_from(om_ref, got_ref)
-    line_powers(flat(w_ref), ends, power_ref, link_ref, 2, (x1, x2), exact=True)
-    c[...] = jnp.zeros_like(c)
-    smoothed_residual(win, w_ref, x1, x2, t, c, 2, masked=True, add=known_ref)
-    odd = fx % 2
-    count_x = (fine_ref.shape[0] + 2 * odd) // 2
-    if odd:
-        x_from = hx - (fx + 1) // 2
-        prolong_odd(c, fine_ref, fine_win, x_from, hy - fy // 2, count_x, fine_ref.shape[1] // 2)
-    else:
-        prolong(c, False, fine_ref, fine_win, hx - fx // 2, hy - fy // 2, count_x, fine_ref.shape[1] // 2)
-    send(out_ref, exact_nt(v_ref[...], flat(fine_ref)))
+    win0, win1, win2 = up_windows(where_ref, s0, grids, y2.shape[:2], y1.shape[:2], w.shape[:2])
+    lines0, lines1 = w.shape[0] * w.shape[1], y1.shape[0] * y1.shape[1]
+    lines2, lines3 = y2.shape[0] * y2.shape[1], d1.shape[0] * d1.shape[1]
+    at1, at2 = UP_LANES[0], UP_LANES[0] + UP_LANES[1]
+    k = got_ref.shape[0]
+
+    got3 = halves(got_ref[:, at2 : at2 + lines3])
+    d1[...] = tn(got3, mix_ref[0, 0:k]).reshape(d1.shape)
+    d2[...] = tn(got3, mix_ref[1, 0:k]).reshape(d2.shape)
+    win3 = Window(d1.shape[:2])
+    win3.each(0, d1, lambda i: win3.get(d1, i) + win3.around(d2, i))
+    win3.each(0, d3, lambda i: win3.around(d1, i))
+    prolong(d3, True, fine, Window(fine.shape[:2]), 0, 0, win3.x, win3.y)
+    place_on_region(where_ref, fine, pad, y2, margin)
+
+    def coefficients(win, got, y, once, twice, maps, a1, a2, a3, trim):
+        y, got = halves(flat(y)), halves(got)
+        a1[...] = (tn(got, once[0:k]) + nn(y, maps[1])).reshape(a1.shape)
+        a2[...] = (tn(got, twice[0:k]) + nn(y, maps[2])).reshape(a2.shape)
+        a3[...] = nn(y, maps[0]).reshape(a3.shape)
+        win.each(trim - 1, a1, lambda i: win.get(a1, i) + win.mask(i, win.around(a2, i)))
+        win.each(trim, a3, lambda i: win.mask(i, win.get(a3, i) + win.around(a1, i)))
+
+    maps = (mix_ref[4], mix_ref[5], mix_ref[6])
+    got2 = got_ref[:, at1 : at1 + lines2]
+    coefficients(win2, got2, y2, mix_ref[2], mix_ref[3], maps, g1, g2, g3, 2)
+    to_level_one(g3, y1, win1)
+    maps = (mix_ref[7], mix_ref[8], mix_ref[9])
+    got1 = got_ref[:, at1 : at1 + lines1]
+    coefficients(win1, got1, y1, mix_ref[10], mix_ref[11], maps, h1, h2, h3, 2)
+    c1[...] = c1_local[...] + exact_nn(flat(h3), basis_ref[...]).reshape(c1.shape)
+    to_level_zero(c1, w, win0)
+    to_level_zero(h3, q, win0)
+    q[...] = q[...] + tn(got_ref[:, 0:lines0], mix_ref[12, 0:k]).reshape(q.shape)
+
+    hx, hy = (w.shape[0] - s0[0]) // 2, (w.shape[1] - s0[1]) // 2
+    sy = s0[1]
+    win = win0
+    field, ends = flat(w), flat(q)
+    lane_powers(field, ends, 64, power_ref, link_ref, 2, (x1, x2), exact=True)
+    n = field.shape[1]
+    m_link = jnp.concatenate([jnp.zeros((64, n), F32), m_link_ref[...], jnp.zeros((n - 72, n), F32)], 0)
+    xm[...] = (exact_nt(field, m_ref[...]) + exact_nn(ends, m_link)).reshape(xm.shape)
+    e = e_ref[0]
+    w_ref = w
+
+    lo, hi = win.span(hx - 2)
+
+    def inner(i):
+        one = 0.32 * win.get(x1, i)
+        two = win.mask(i, 0.64 * win.around(x2, i))
+        win.put(t0, i, one + two)
+        win.put(t1, i, e * (one - two))
+
+    rows(lo, hi, inner)
+    win.each(hx - 1, x2, lambda i: (0.28 * e) * win.get(w_ref, i) + win.mask(i, win.around(t1, i)))
+    lo, hi = win.span(hx)
+    cut_y = hy - win.lo
+
+    def last(i):
+        u = 0.04 * win.get(w_ref, i) + win.around(t0, i)
+        u_ref[i - hx] = known_ref[i - hx] + u[cut_y : cut_y + sy]
+        r = 0.04 * win.get(xm, i) + win.around(x2, i)
+        r_ref[i - hx] = twice_ref[i - hx] - r[cut_y : cut_y + sy]
+
+    rows(lo, hi, last)
 
 
 def prolong_odd(src, out, win, x_from, y_from, count_x, count_y):
@@ -737,41 +890,6 @@
                 w = 0.75 * v + 0.25 * side
                 out[row, pl.ds(parity, count_y, stride=2), :] = w[y_from : y_from + count_y]
     win.each(0, out, lambda i: win.mask(i, win.get(out, i)))
-
-
-def final_kernel(
-    halo, grid, where_ref, e_ref, w_ref, known_ref, twice_ref, got_ref, om_ref, power_ref, link_ref,
-    m_ref, m_link_ref, u_ref, r_ref, x1, x2, xm, t0, t1
-):
-    hx, hy = halo
-    sx, sy = w_ref.shape[0] - 2 * hx, w_ref.shape[1] - 2 * hy
-    win = Window(w_ref.shape[:2], (where_ref[0] * sx - hx, where_ref[1] * sy - hy), grid)
-    ends = ends_from(om_ref, got_ref)
-    field = flat(w_ref)
-    line_powers(field, ends, power_ref, link_ref, 2, (x1, x2), exact=True)
-    xm[...] = (exact_nt(field, m_ref[...]) + exact_tn(ends, m_link_ref[...])).reshape(xm.shape)
-    e = e_ref[0]
-
-    lo, hi = win.span(hx - 2)
-
-    def inner(i):
-        one = 0.32 * win.get(x1, i)
-        two = win.mask(i, 0.64 * win.around(x2, i))
-        win.put(t0, i, one + two)
-        win.put(t1, i, e * (one - two))
-
-    rows(lo, hi, inner)
-    win.each(hx - 1, x2, lambda i: (0.28 * e) * win.get(w_ref, i) + win.mask(i, win.around(t1, i)))
-    lo, hi = win.span(hx)
-    cut_y = hy - win.lo
-
-    def last(i):
-        u = 0.04 * win.get(w_ref, i) + win.around(t0, i)
-        u_ref[i - hx] = known_ref[i - hx] + u[cut_y : cut_y + sy]
-        r = 0.04 * win.get(xm, i) + win.around(x2, i)
-        r_ref[i - hx] = twice_ref[i - hx] - r[cut_y : cut_y + sy]
-
-    rows(lo, hi, last)
 
 
 def call(kernel, outs, scratch, smem, *args, flops=0):
@@ -829,19 +947,19 @@
 
     setup = call(
         powers_kernel,
-        [(POWERS, n, n)] * LEVELS + [(8, n)] * LEVELS + [(POWERS, 8, n)] * LEVELS + [(8, n), (16, n), (gz, 12, 8, n)],
+        [(POWERS, n, n)] * LEVELS + [(8, n)] * LEVELS + [(POWERS, 8, n)] * LEVELS + [(8, n), (16, n), (n, n), (gz, 11, 8, n)],
         [],
         (1,),
         block_inverse, e, faces,
     )
     power, ends, link = (setup[k * LEVELS : (k + 1) * LEVELS] for k in range(3))
-    ends_up, basis, table = setup[3 * LEVELS :]
+    ends_up, basis, basis_up, table = setup[3 * LEVELS :]
     low, high, table = lax.optimization_barrier((*halo_y(right_side, 12), table))
     f0 = halo_x(jnp.concatenate([low, right_side, high], axis=1), 12)
     table = exchange(table)
-    *om, om_up, m_matrix, m_link, mix, w2_map = call(
+    *om, om_up, m_matrix, m_link, mix, up_mix, w2_map = call(
         coupling_kernel,
-        [(8, n)] * LEVELS + [(8, n), (n, n), (8, n), (11, n, n), (8, n)],
+        [(8, n)] * LEVELS + [(8, n), (n, n), (8, n), (11, n, n), (13, n, n), (8, n)],
         [(gz, 8, 8, n), (n, n)],
         (0, 2),
         where, table, e, faces, basis,
@@ -927,43 +1045,22 @@
         flops=8000000000,
     )
     got4, known3 = lax.optimization_barrier((got4, known3))
-    w3, copies = call(
-        bottom_kernel,
-        [cubes[3], (gz, 8, lines[3])],
-        [cubes[4]] * 3,
-        (0,),
-        e, f4, got4, om[4], power[4], link[4], ends[3],
-    )
-    w2, copies = call(
-        part(whole_up_kernel, margin),
-        [region, (gz, 8, region[0] * region[1])],
-        [cubes[3]] * 4 + [cubes[2], padded],
-        (0,),
-        where, w3, known3, stacked(copies), om[3], power[3], link[3], ends[2],
-    )
-
-    h0, h1 = (4, 4), (5, 8)
-    cube0, lines0 = inner0, inner0[0] * inner0[1]
-    w1, copies = call(
-        part(up_kernel, (margin, margin), h1, grids[2]),
-        [cube1, (gz, 8, lines1)],
-        [region] * 4,
-        (0,),
-        where, w2, known2, stacked(copies), om[2], power[2], link[2], ends[1],
-    )
-    w0, copies = call(
-        part(up_kernel, h1, h0, grids[1]),
-        [cube0, (gz, 8, lines0)],
-        [cube1] * 4,
-        (0,),
-        where, w1, known1, stacked(copies), om[1], power[1], link[1], ends_up,
+
+    copies, c1_local = call(
+        part(local_up_kernel, s0, grids, margin),
+        [(gz, 8, sum(UP_LANES)), cube1],
+        [cubes[4]] * 3 + [cubes[3]] * 5 + [cubes[2], padded] + [region] * 5 + [cube1] * 4 + [inner0],
+        (0, 1),
+        where, e, f4, got4, om[4], power[4], link[4], known3, known2, known1,
+        power[3], power[2], power[1], ends[3], ends[2], ends[1], ends_up,
     )
     u, r = call(
-        part(final_kernel, h0, grids[0]),
-        [(sx, sy, n), (sx, sy, n)],
-        [cube0] * 5,
+        part(finish_kernel, s0, grids, margin),
+        [s0 + (n,), s0 + (n,)],
+        [cubes[3]] * 3 + [cubes[2], padded] + [region] * 4 + [cube1] * 5 + [inner0] * 7,
         (0, 1),
-        where, e, w0, known0, twice0, stacked(copies), om_up, power[0], link[0], m_matrix, m_link,
+        where, e, stacked(copies), c1_local, known0, twice0, up_mix, basis_up,
+        power[0], link[0], m_matrix, m_link,
     )
     return u, r
 

time: 208 us -> 178 us (0.86)
  blocking collectives: 44.9 us -> 17 us
    all_to_all x4 -> x1, blocking collectives: 44.9 us -> 17 us  [exchange(): got = lax.all_to_all(copies, axes, 0, 0, tiled=True)]
    pallas_call x15 -> x12, Pallas kernels: 75.6 us -> 76.3 us  [call(): pl.pallas_call(kernel, out_shape=[jax.ShapeDtypeStruct(s, F32) for s in o...]
  transfers between devices with their start and end apart: 9 -> 9, of which waited for: 5 -> 5; matrix products, arithmetic and copies ran while one was open for 1% -> 1% of each run, Pallas kernels for 17% -> 22%
where the time goes in v3:
time: 178 us; the launch traced here: 177 us
  Pallas kernels  76.3 us (43%)
  starting transfers between devices  49.4 us (28%)
  waiting for transfers between devices  27.3 us (15%)
  blocking collectives  17 us (10%)
  local copies, waits for them, and re-layouts  4.43 us (2%)
  other arithmetic  2.04 us (1%)
    pallas_call x12, Pallas kernels, call(): pl.pallas_call(kernel, out_shape=[jax.ShapeDtypeStruct(s, F32) for s in o...  76.3 us
    all_to_all x4, starting transfers between devices, exchange(): got = lax.all_to_all(copies, axes, 0, 0, tiled=True)  25.6 us
    all_to_all x1, blocking collectives, exchange(): got = lax.all_to_all(copies, axes, 0, 0, tiled=True)  17 us
    all_to_all x1, waiting for transfers between devices, body(): parts = lax.all_to_all(parts, ('gx', 'gy'), 0, 0, tiled=True)  14.4 us
    all_to_all x1, starting transfers between devices, body(): parts = lax.all_to_all(parts, ('gx', 'gy'), 0, 0, tiled=True)  12.7 us
    all_to_all x4, waiting for transfers between devices, exchange(): got = lax.all_to_all(copies, axes, 0, 0, tiled=True)  11.6 us
    ppermute x2, starting transfers between devices, edges(): lax.ppermute(last, axis, up)  8.54 us
  transfers between devices with their start and end apart: 9, of which 5 were waited for; matrix products, arithmetic and copies ran while one was open for 1% of the time, Pallas kernels for 22%

profile of v3, /device:TPU:1, one launch (start us, length us, event | category | flops | bytes accessed | tf_op | source)
XLA Modules:
  0.0 177.2 jit_solution(6469383286527565182)
XLA Ops:
  0.6 1.1 fusion
  1.8 1.3 collective-permute-start.1
  3.1 5.0 %collective-permute-start = (f32[32,12,128]{2,1,0:T(8,128)S(1)}, f32[32,12,128]{2,1,0:T(8,128)S(1)}, u32[]{:S(2)}, u32[]{:S(2)}) collective-permute-start(f32[32,12,128]{2,1,0:T(8,128)S(1)} %get-tuple-element.109), channel_id=1, source_target_pairs={{0,8},{8,16},{16,24},{24,32},{32,40},{40,48},{48,56},{1,9},{9,17},... | collective-permute-start | bytes 589832 | tf_op jit(solution)/shard_map/ppermute | solution.py:926
  8.1 4.4 %shard_map.59 = (f32[4,128,128]{2,1,0:T(8,128)}, f32[4,128,128]{2,1,0:T(8,128)}, f32[4,128,128]{2,1,0:T(8,128)}, f32[4,128,128]{2,1,0:T(8,128)}, f32[4,128,128]{...) custom-call(f32[5,128,128]{2,1,0:T(8,128)} %g_ref.1, ...), custom_call_target="tpu_custom_call" | custom-call | flops 1000000 | bytes 1000000 | tf_op jit(solution)/shard_map/pallas_call | solution.py:900
  12.6 3.5 %collective-permute-start.2 = (f32[12,56,128]{2,1,0:T(8,128)S(1)}, f32[12,56,128]{2,1,0:T(8,128)S(1)}, u32[]{:S(2)}, u32[]{:S(2)}) collective-permute-start(f32[12,56,128]{2,1,0:T(8,128)S(1)} %get-tuple-element.106), channel_id=1, source_target_pairs={{0,64},{64,128},{128,192},{1,65},{65,129},{129,193},{2,66},{66,130... | collective-permute-start | bytes 1032200 | tf_op jit(solution)/shard_map/ppermute | solution.py:926
  16.2 1.3 collective-permute-start.3
  17.5 6.4 %all-to-all-start.1 = ((f32[8,11,8,128]{3,2,1,0:T(8,128)}), f32[8,11,8,128]{3,2,1,0:T(8,128)S(1)}, u32[]{:S(2)}, u32[]{:S(2)}) async-start(f32[8,11,8,128]{3,2,1,0:T(8,128)} %get-tuple-element.65), calls=%async_computation.1 | async-start | bytes 720896 | tf_op jit(solution)/shard_map/all_to_all | solution.py:912
  23.8 0.6 pad_add_fusion.where_ref
  24.5 1.3 collective-permute-done.3
  25.8 1.3 pad_maximum_fusion.f_ref
  27.1 6.9 %shard_map.60 = (f32[8,8,4224]{2,1,0:T(8,128)}, f32[26,32,128]{2,1,0:T(8,128)}, f32[8,8,128]{2,1,0:T(8,128)}) custom-call(s32[3]{0:T(128)} %pad_add_fusion.where_ref, f32[56,56,128]{2,1,0:T(8,128)} %pad_maximum_fusion.f_ref, f32[4,128,128]{2,1,0:T(8,128)} %get-tuple-element.57.power0.power_ref, f32[4,128,128]{2,1,0:T(8,128)} %get-tuple-element.58.power1.power_ref, ...), custom_call_target="tpu_custom_call" | custom-call | flops 1000000 | bytes 1000000 | tf_op jit(solution)/shard_map/pallas_call | solution.py:900
  34.0 7.2 %all-to-all-start = ((f32[8,8,4224]{2,1,0:T(8,128)}), f32[8,8,4224]{2,1,0:T(8,128)S(1)}, u32[]{:S(2)}, u32[]{:S(2)}) async-start(f32[8,8,4224]{2,1,0:T(8,128)} %get-tuple-element.62), calls=%async_computation | async-start | bytes 2162688 | tf_op jit(solution)/shard_map/all_to_all | solution.py:912
  41.3 4.9 %shard_map.61 = (f32[8,128]{1,0:T(8,128)}, f32[8,128]{1,0:T(8,128)}, f32[8,128]{1,0:T(8,128)}, f32[8,128]{1,0:T(8,128)}, f32[8,128]{1,0:T(8,128)}, /*index=5*/f3...) custom-call(s32[3]{0:T(128)} %pad_add_fusion.where_ref, ...), custom_call_target="tpu_custom_call" | custom-call | flops 1000000 | bytes 1000000 | tf_op jit(solution)/shard_map/pallas_call | solution.py:900
  46.2 10.4 %all-to-all-done = f32[8,8,4224]{2,1,0:T(8,128)S(1)} async-done(((f32[8,8,4224]{2,1,0:T(8,128)}), f32[8,8,4224]{2,1,0:T(8,128)S(1)}, u32[]{:S(2)}, u32[]{:S(2)}) %all-to-all-start) | async-done | bytes 1081376 | tf_op jit(solution)/shard_map/all_to_all | solution.py:912
  56.6 1.0 copy-done.2
  57.6 6.9 %shard_map.62 = (f32[26,32,128]{2,1,0:T(8,128)}, f32[26,32,128]{2,1,0:T(8,128)}, f32[32,9,8,128]{3,2,1,0:T(8,128)}) custom-call(s32[3]{0:T(128)} %pad_add_fusion.where_ref, f32[64,4224]{1,0:T(8,128)} %bitcast.8, f32[26,32,128]{2,1,0:T(8,128)} %get-tuple-element.63.f1_local, f32[8,8,128]{2,1,0:T(8,128)} %get-tuple-element.64.f2_local, ...), custom_call_target="tpu_custom_call" | custom-call | flops 1000000 | bytes 1000000 | tf_op jit(solution)/shard_map/pallas_call | solution.py:900
  64.5 12.7 %all-to-all-start.2 = ((f32[32,9,8,128]{3,2,1,0:T(8,128)}), f32[32,9,8,128]{3,2,1,0:T(8,128)S(1)}, u32[]{:S(2)}, u32[]{:S(2)}) async-start(f32[32,9,8,128]{3,2,1,0:T(8,128)} %get-tuple-element.70), calls=%async_computation.2 | async-start | bytes 2359296 | tf_op jit(solution)/shard_map/all_to_all | solution.py:989
  77.2 5.2 %shard_map.64.known1 = f32[26,32,128]{2,1,0:T(8,128)} custom-call(s32[3]{0:T(128)} %pad_add_fusion.where_ref, f32[5]{0:T(128)} %e_ref.15, f32[26,32,128]{2,1,0:T(8,128)} %get-tuple-element.74.f_ref, f32[26,32,128]{2,1,0:T(8,128)} %get-tuple-element.75.own_ref, f32[4,128,128]{2,1,0:T(8,128)} %get-tuple-element.58.power1.power_ref, ...), custom_call_target="tpu_custom_call" | custom-call | flops 10000000000 | bytes 1000000 | tf_op jit(solution)/shard_map/pallas_call | solution.py:900
  82.4 8.0 %shard_map.63 = (f32[32,32,128]{2,1,0:T(8,128)}, f32[32,32,128]{2,1,0:T(8,128)}) custom-call(s32[3]{0:T(128)} %pad_add_fusion.where_ref, f32[5]{0:T(128)} %e_ref.15, f32[56,56,128]{2,1,0:T(8,128)} %pad_maximum_fusion.f_ref, f32[64,4224]{1,0:T(8,128)} %bitcast.9, f32[11,128,128]{2,1,0:T(8,128)} %get-tuple-element.67.mix_ref, ...), custom_call_target="tpu_custom_call" | custom-call | flops 20000000000 | bytes 1000000 | tf_op jit(solution)/shard_map/pallas_call | solution.py:900
  90.4 14.4 %all-to-all-done.2.parts_ref = f32[32,9,8,128]{3,2,1,0:T(8,128)S(1)} async-done(((f32[32,9,8,128]{3,2,1,0:T(8,128)}), f32[32,9,8,128]{3,2,1,0:T(8,128)S(1)}, u32[]{:S(2)}, u32[]{:S(2)}) %all-to-all-start.2) | async-done | bytes 1179680 | tf_op jit(solution)/shard_map/all_to_all | solution.py:989
  104.9 1.0 copy-done.1
  105.9 5.1 %shard_map.65 = (f32[16,32,128]{2,1,0:T(8,128)}, f32[8,8,512]{2,1,0:T(8,128)}) custom-call(f32[32,9,8,128]{3,2,1,0:T(8,128)} %copy-done.1, f32[4,128,128]{2,1,0:T(8,128)} %get-tuple-element.78.power_ref.power2, f32[4,8,128]{2,1,0:T(8,128)} %get-tuple-element.79.link_ref, f32[8,128]{1,0:T(8,128)} %get-tuple-element.80.v_ref.v3), custom_call_target="tpu_custom_call" | custom-call | flops 1000000 | bytes 1000000 | tf_op jit(solution)/shard_map/pallas_call | solution.py:900
  111.0 7.8 %all-to-all-start.3 = ((f32[8,8,512]{2,1,0:T(8,128)}), f32[8,8,512]{2,1,0:T(8,128)S(1)}, u32[]{:S(2)}, u32[]{:S(2)}) async-start(f32[8,8,512]{2,1,0:T(8,128)} %get-tuple-element.82), calls=%async_computation.3 | async-start | bytes 262144 | tf_op jit(solution)/shard_map/all_to_all | solution.py:912
  118.8 4.6 %shard_map.66.known2 = f32[24,24,128]{2,1,0:T(8,128)} custom-call(s32[3]{0:T(128)} %pad_add_fusion.where_ref, f32[5]{0:T(128)} %e_ref.15, f32[32,9,8,128]{3,2,1,0:T(8,128)} %copy-done.1, f32[4,128,128]{2,1,0:T(8,128)} %get-tuple-element.78.power_ref.power2, f32[4,8,128]{2,1,0:T(8,128)} %get-tuple-element.79.link_ref), custom_call_target="tpu_custom_call" | custom-call | flops 8000000000 | bytes 1000000 | tf_op jit(solution)/shard_map/pallas_call | solution.py:900
  123.5 0.7 all-to-all-done.3
  124.1 0.7 copy-done.4
  124.8 3.0 %shard_map.67 = (f32[8,16,128]{2,1,0:T(8,128)}, f32[8,8,128]{2,1,0:T(8,128)}) custom-call(f32[16,32,128]{2,1,0:T(8,128)} %get-tuple-element.81.f_ref, f32[64,512]{1,0:T(8,128)} %bitcast.11, f32[8,128]{1,0:T(8,128)} %get-tuple-element.84.om_ref, f32[4,128,128]{2,1,0:T(8,128)} %get-tuple-element.85.power_ref.power3, f32[4,8,128]{2,1,0:T(8,128)} %get-tuple-element.86.link_ref, ...), custom_call_target="tpu_custom_call" | custom-call | flops 1000000 | bytes 1000000 | tf_op jit(solution)/shard_map/pallas_call | solution.py:900
  127.8 4.2 %all-to-all-start.4 = ((f32[8,8,128]{2,1,0:T(8,128)}), f32[8,8,128]{2,1,0:T(8,128)S(1)}, u32[]{:S(2)}, u32[]{:S(2)}) async-start(f32[8,8,128]{2,1,0:T(8,128)} %get-tuple-element.89), calls=%async_computation.4 | async-start | bytes 65536 | tf_op jit(solution)/shard_map/all_to_all | solution.py:912
  132.0 4.2 %shard_map.68.known3 = f32[16,32,128]{2,1,0:T(8,128)} custom-call(f32[5]{0:T(128)} %e_ref.15, f32[16,32,128]{2,1,0:T(8,128)} %get-tuple-element.81.f_ref, f32[64,512]{1,0:T(8,128)} %bitcast.12, f32[8,128]{1,0:T(8,128)} %get-tuple-element.84.om_ref, f32[4,128,128]{2,1,0:T(8,128)} %get-tuple-element.85.power_ref.power3, f32[4,8,128]{2,1,0:T(8,128)} %get-tuple-element.86.link_ref), custom_call_target="tpu_custom_call" | custom-call | flops 8000000000 | bytes 1000000 | tf_op jit(solution)/shard_map/pallas_call | solution.py:900
  137.3 8.9 %shard_map.69 = (f32[8,8,3072]{2,1,0:T(8,128)}, f32[26,32,128]{2,1,0:T(8,128)}) custom-call(s32[3]{0:T(128)} %pad_add_fusion.where_ref, f32[5]{0:T(128)} %e_ref.15, f32[8,16,128]{2,1,0:T(8,128)} %get-tuple-element.88.f_ref, f32[64,128]{1,0:T(8,128)} %bitcast.13, f32[8,128]{1,0:T(8,128)} %get-tuple-element.91.om_ref, ...), custom_call_target="tpu_custom_call" | custom-call | flops 1000000 | bytes 1000000 | tf_op jit(solution)/shard_map/pallas_call | solution.py:900
  146.2 17.0 %all_to_all.30 = f32[8,8,3072]{2,1,0:T(8,128)} all-to-all(f32[8,8,3072]{2,1,0:T(8,128)} %get-tuple-element.98), channel_id=1, replica_groups=mesh['gx'=4,'gy'=8,'gz'=8] {'gz'}, dimensions={0} | all-to-all | bytes 1572864 | tf_op jit(solution)/shard_map/all_to_all | solution.py:912
  163.3 14.0 %shard_map.70 = (f32[32,32,128]{2,1,0:T(8,128)}, f32[32,32,128]{2,1,0:T(8,128)}) custom-call(s32[3]{0:T(128)} %pad_add_fusion.where_ref, f32[5]{0:T(128)} %e_ref.15, f32[64,3072]{1,0:T(8,128)} %bitcast.10, f32[26,32,128]{2,1,0:T(8,128)} %get-tuple-element.99.c1_local, f32[32,32,128]{2,1,0:T(8,128)} %get-tuple-element.100.known_ref, ...), custom_call_target="tpu_custom_call" | custom-call | flops 1000000 | bytes 1000000 | tf_op jit(solution)/shard_map/pallas_call | solution.py:900
  (15 shorter events, 1.2 us)
Async XLA Ops:
  0.6 11.9 %copy-start = (f32[32,32,128]{2,1,0:T(8,128)S(1)}, f32[32,32,128]{2,1,0:T(8,128)}, u32[]{:S(2)}) copy-start(f32[32,32,128]{2,1,0:T(8,128)} %param.4) | copy-start | bytes 1572868
  1.8 10.7 %collective-permute-start.1 = (f32[32,12,128]{2,1,0:T(8,128)S(1)}, f32[32,12,128]{2,1,0:T(8,128)S(1)}, u32[]{:S(2)}, u32[]{:S(2)}) collective-permute-start(f32[32,12,128]{2,1,0:T(8,128)S(1)} %get-tuple-element.108), channel_id=1, source_target_pairs={{8,0},{16,8},{24,16},{32,24},{40,32},{48,40},{56,48},{9,1},{17,9},... | collective-permute-start | bytes 589832 | tf_op jit(solution)/shard_map/ppermute | solution.py:926
  3.1 9.5 %collective-permute-start = (f32[32,12,128]{2,1,0:T(8,128)S(1)}, f32[32,12,128]{2,1,0:T(8,128)S(1)}, u32[]{:S(2)}, u32[]{:S(2)}) collective-permute-start(f32[32,12,128]{2,1,0:T(8,128)S(1)} %get-tuple-element.109), channel_id=1, source_target_pairs={{0,8},{8,16},{16,24},{24,32},{32,40},{40,48},{48,56},{1,9},{9,17},... | collective-permute-start | bytes 589832 | tf_op jit(solution)/shard_map/ppermute | solution.py:926
  12.6 11.9 %collective-permute-start.2 = (f32[12,56,128]{2,1,0:T(8,128)S(1)}, f32[12,56,128]{2,1,0:T(8,128)S(1)}, u32[]{:S(2)}, u32[]{:S(2)}) collective-permute-start(f32[12,56,128]{2,1,0:T(8,128)S(1)} %get-tuple-element.106), channel_id=1, source_target_pairs={{0,64},{64,128},{128,192},{1,65},{65,129},{129,193},{2,66},{66,130... | collective-permute-start | bytes 1032200 | tf_op jit(solution)/shard_map/ppermute | solution.py:926
  16.2 9.6 %collective-permute-start.3 = (f32[12,56,128]{2,1,0:T(8,128)S(1)}, f32[12,56,128]{2,1,0:T(8,128)S(1)}, u32[]{:S(2)}, u32[]{:S(2)}) collective-permute-start(f32[12,56,128]{2,1,0:T(8,128)S(1)} %get-tuple-element.107), channel_id=1, source_target_pairs={{64,0},{128,64},{192,128},{65,1},{129,65},{193,129},{66,2},{130,66... | collective-permute-start | bytes 1032200 | tf_op jit(solution)/shard_map/ppermute | solution.py:926
  17.5 16.6 %all-to-all-start.1 = ((f32[8,11,8,128]{3,2,1,0:T(8,128)}), f32[8,11,8,128]{3,2,1,0:T(8,128)S(1)}, u32[]{:S(2)}, u32[]{:S(2)}) async-start(f32[8,11,8,128]{3,2,1,0:T(8,128)} %get-tuple-element.65), calls=%async_computation.1 | async-start | bytes 720896 | tf_op jit(solution)/shard_map/all_to_all | solution.py:912
  34.0 7.3 %copy-start.3 = (f32[8,11,8,128]{3,2,1,0:T(8,128)}, f32[8,11,8,128]{3,2,1,0:T(8,128)S(1)}, u32[]{:S(2)}) copy-start(f32[8,11,8,128]{3,2,1,0:T(8,128)S(1)} %all-to-all-done.1.table_ref) | copy-start | bytes 1081348
  34.0 22.6 %all-to-all-start = ((f32[8,8,4224]{2,1,0:T(8,128)}), f32[8,8,4224]{2,1,0:T(8,128)S(1)}, u32[]{:S(2)}, u32[]{:S(2)}) async-start(f32[8,8,4224]{2,1,0:T(8,128)} %get-tuple-element.62), calls=%async_computation | async-start | bytes 2162688 | tf_op jit(solution)/shard_map/all_to_all | solution.py:912
  56.6 1.0 copy-start.2
  64.5 40.3 %all-to-all-start.2 = ((f32[32,9,8,128]{3,2,1,0:T(8,128)}), f32[32,9,8,128]{3,2,1,0:T(8,128)S(1)}, u32[]{:S(2)}, u32[]{:S(2)}) async-start(f32[32,9,8,128]{3,2,1,0:T(8,128)} %get-tuple-element.70), calls=%async_computation.2 | async-start | bytes 2359296 | tf_op jit(solution)/shard_map/all_to_all | solution.py:989
  104.9 1.0 copy-start.1
  111.0 13.1 %all-to-all-start.3 = ((f32[8,8,512]{2,1,0:T(8,128)}), f32[8,8,512]{2,1,0:T(8,128)S(1)}, u32[]{:S(2)}, u32[]{:S(2)}) async-start(f32[8,8,512]{2,1,0:T(8,128)} %get-tuple-element.82), calls=%async_computation.3 | async-start | bytes 262144 | tf_op jit(solution)/shard_map/all_to_all | solution.py:912
  124.1 0.7 copy-start.4
  127.8 8.9 %all-to-all-start.4 = ((f32[8,8,128]{2,1,0:T(8,128)}), f32[8,8,128]{2,1,0:T(8,128)S(1)}, u32[]{:S(2)}, u32[]{:S(2)}) async-start(f32[8,8,128]{2,1,0:T(8,128)} %get-tuple-element.89), calls=%async_computation.4 | async-start | bytes 65536 | tf_op jit(solution)/shard_map/all_to_all | solution.py:912
  136.7 0.6 copy-start.5

commit v4 on v3

--- a/solution.py
+++ b/solution.py
@@ -11,6 +11,8 @@
 POWERS = 4
 HIGHEST = lax.Precision.HIGHEST
 F32 = jnp.float32
+KNOWN = (0.9984, 0.9728, 0.8192, 0.4096)
+TWICE = (0.0016, 0.0256, 0.1536, 0.4096, 0.4096)
 VMEM_LIMIT = 56 * 1024 * 1024
 
 
@@ -60,7 +62,7 @@
     return product(a, b, 0, 0)
 
 
-def rows(lo, hi, fn, step=4):
+def rows(lo, hi, fn, step=8):
     full = (hi - lo) // step
     if full:
         def group(k, carry):
@@ -114,18 +116,29 @@
     def around(self, ref, i):
         if self.whole:
             low, high = shifted(ref[i], True)
-            below = ref[jnp.maximum(i - 1, 0)] * jnp.where(i > 0, 1.0, 0.0).astype(F32)
-            above = ref[jnp.minimum(i + 1, self.x - 1)] * jnp.where(i < self.x - 1, 1.0, 0.0).astype(F32)
-            return (low + high) + (below + above)
+            total = low + high
+            if not (isinstance(i, int) and i == 0):
+                total = total + ref[i - 1]
+            if not (isinstance(i, int) and i == self.x - 1):
+                total = total + ref[i + 1]
+            return total
         y = self.y
         return (ref[i, 0 : y - 2] + ref[i, 2:y]) + (ref[i - 1, 1 : y - 1] + ref[i + 1, 1 : y - 1])
 
     def span(self, trim):
         return (0, self.x) if self.whole else (trim, self.x - trim)
 
+    def loop(self, trim, fn):
+        lo, hi = self.span(trim)
+        if self.whole:
+            fn(0)
+            rows(lo + 1, hi - 1, fn)
+            fn(hi - 1)
+        else:
+            rows(lo, hi, fn)
+
     def each(self, trim, out, fn):
-        lo, hi = self.span(trim)
-        rows(lo, hi, lambda i: self.put(out, i, fn(i)))
+        self.loop(trim, lambda i: self.put(out, i, fn(i)))
 
 
 def line_powers(field, ends, power_ref, link_ref, count, out_refs, exact=False):
@@ -257,13 +270,15 @@
     fourth = jnp.where(at < 16, exact_nt(ends_refs[1][...], basis_up_ref[...]), 0.0)
     fifth = exact_nt(up_ref[...], basis_up_ref[...])
     total = first + pltpu.roll(second, 4, 1) + pltpu.roll(third, 20, 1)
-    table_ref[0, 10] = total + pltpu.roll(fourth, 24, 1) + pltpu.roll(fifth, 40, 1)
+    sixth = jnp.where(at < 4, exact_nt(ends_refs[4][...], basis_up_ref[...]), 0.0)
+    total = total + pltpu.roll(fourth, 24, 1) + pltpu.roll(fifth, 40, 1)
+    table_ref[0, 10] = total + pltpu.roll(sixth, 92, 1)
     for m in range(1, table_ref.shape[0]):
         table_ref[m] = table_ref[0]
 
 
 def coupling_kernel(
-    where_ref, table_ref, e_ref, zf_ref, basis_ref, om0, om1, om2, om3, om4, om_up_ref, m_ref, m_link_ref, mix_ref, up_mix_ref, w2_ref, held, full
+    where_ref, table_ref, e_ref, zf_ref, basis_ref, basis_up_ref, om0, om1, om2, om3, om4, om_up_ref, m_ref, m_link_ref, mix_ref, up_mix_ref, w2_ref, w4_ref, held, full
 ):
     blocks, n = table_ref.shape[0], table_ref.shape[3]
     k_own = where_ref[2]
@@ -436,6 +451,13 @@
     full[...] = jnp.zeros_like(full)
     full[64:72] = up_rows
     up_mix_ref[12] = full[...].T
+    up_mix_ref[13] = jnp.where(row < 32, exact_tn(own_rows, basis_up_ref[...]), 0.0)
+    w4_ref[...] = exact_nn(om4[...], gathered(92, 4))
+    for q in range(POWERS):
+        full[...] = jnp.zeros_like(full)
+        for b in range(q + 1):
+            full[2 * b : 2 * b + 2] = KNOWN[q] * om3[2 * (q - b) : 2 * (q - b) + 2]
+        up_mix_ref[14 + q] = full[...].T
 
     above = jnp.minimum(k_own + 1, blocks - 1)
     top = table_ref[above, 8][0:1, 0:1]
@@ -559,10 +581,6 @@
         parts_ref[m] = parts_ref[0]
 
 
-KNOWN = (0.9984, 0.9728, 0.8192, 0.4096)
-TWICE = (0.0016, 0.0256, 0.1536, 0.4096, 0.4096)
-
-
 def lane_powers(field, coefficients, lane0, power_ref, link_ref, count, out_refs, exact=False):
     n = field.shape[1]
     if not exact:
@@ -657,7 +675,8 @@
 
 
 def gathered_down_kernel(
-    across, down, parts_ref, power_ref, link_ref, v_ref, coarse_ref, out_ref, f, fp, ap, x1, x2, t, r, pair
+    across, down, parts_ref, power_ref, link_ref, power3, v3, v4, coarse_ref, lower_ref, out_ref,
+    f, fp, ap, x1, x2, t, r, pair, y1, y2, ty, ry, pair3
 ):
     many, side = parts_ref.shape[0], parts_ref.shape[2]
     lines = side * side
@@ -676,34 +695,31 @@
     win = Window(f.shape[:2])
     smoothed_residual(win, f, x1, x2, t, r, 2)
     restrict(r, pair, coarse_ref, 0, 0)
-    send(out_ref, nt(v_ref[...], flat(coarse_ref)))
-
-
-def whole_down_kernel(
-    f_ref, got_ref, om_ref, power_ref, link_ref, v_ref, coarse_ref, out_ref, x1, x2, t, r, pair
-):
+    field = halves(flat(coarse_ref))
+    lanes = field[0].shape[0]
+    out_ref[0, :, 0:lanes] = nt(v3[...], field)
+    y1[...] = nt(field, power3[0]).reshape(y1.shape)
+    y2[...] = nt(field, power3[1]).reshape(y2.shape)
+    smoothed_residual(Window(y1.shape[:2]), coarse_ref, y1, y2, ty, ry, 2)
+    restrict(ry, pair3, lower_ref, 0, 0)
+    value = nt(v4[...], flat(lower_ref))
+    out_ref[0, :, lanes : lanes + value.shape[1]] = value
+    for m in range(1, out_ref.shape[0]):
+        out_ref[m] = out_ref[0]
+
+
+def local_known_kernel(level, e_ref, f_ref, power_ref, known_ref, x1, x2, x3, x4, t0, t1):
     win = Window(f_ref.shape[:2])
-    ends = ends_from(om_ref, got_ref)
-    line_powers(flat(f_ref), ends, power_ref, link_ref, 2, (x1, x2))
-    smoothed_residual(win, f_ref, x1, x2, t, r, 2)
-    restrict(r, pair, coarse_ref, 0, 0)
-    send(out_ref, nt(v_ref[...], flat(coarse_ref)))
-
-
-def whole_known_kernel(
-    level, e_ref, f_ref, got_ref, om_ref, power_ref, link_ref, known_ref, x1, x2, x3, x4, t0, t1
-):
-    win = Window(f_ref.shape[:2])
-    ends = ends_from(om_ref, got_ref)
     xs = (x1, x2, x3, x4)
-    line_powers(flat(f_ref), ends, power_ref, link_ref, POWERS, xs, exact=True)
+    for j in range(POWERS):
+        xs[j][...] = exact_nt(flat(f_ref), power_ref[j]).reshape(x1.shape)
     inverse_e = 1.0 / jnp.full((f_ref.shape[1], 128), e_ref[level], F32)
     src, scale = horner(win, xs, KNOWN, t0, t1, 4)
 
     def known(i):
         known_ref[i] = (KNOWN[0] * x1[i] + scale * win.around(src, i)) * inverse_e
 
-    rows(0, win.x, known)
+    win.loop(0, known)
 
 
 def clear_edges(pad, margin):
@@ -727,7 +743,7 @@
     rows(0, out_ref.shape[0], one)
 
 
-UP_LANES = (1664, 896, 512)
+UP_LANES = (896, 896, 512)
 
 
 def place_on_region(where_ref, fine, pad, out_ref, margin):
@@ -758,29 +774,52 @@
 
 
 def local_up_kernel(
-    s0, grids, margin, where_ref, e_ref, f_ref, got_ref, om_ref, power4, link4, known3, known2, known1,
-    power3, power2, power1, v3, v2, v1, v0, out_ref, c1_ref,
-    b1, b2, c4, w3, p1, p2, pt, c3, fine, pad, w2, q1, q2, qt, c2, w1, r1, r2, rt, w0
+    s0, grids, margin, where_ref, e_ref, f4_local, got_ref, om_ref, w4_ref, mix_ref, power4, link4,
+    known3_local, known2, known1, power3, power2, power1, v3, v2, v1, v0, out_ref, c1_ref,
+    d1, d2, d3, pair, y4, f4, known3, b1, b2, c4, w3, p1, p2, pt, c3, fine, pad, w2, q1, q2, qt, c2, w1, r1, r2, rt
 ):
-    win = Window(f_ref.shape[:2])
-    ends = ends_from(om_ref, got_ref)
-    line_powers(flat(f_ref), ends, power4, link4, 2, (b1, b2), exact=True)
-    inverse_e = 1.0 / jnp.full((f_ref.shape[1], 128), e_ref[LEVELS - 1], F32)
+    k = got_ref.shape[0]
+    win3 = Window(d1.shape[:2])
+    lanes = win3.x * win3.y
+    got3 = halves(got_ref[:, 0:lanes])
+    d1[...] = tn(got3, mix_ref[0, 0:k]).reshape(d1.shape)
+    d2[...] = tn(got3, mix_ref[1, 0:k]).reshape(d2.shape)
+    win3.each(0, d1, lambda i: win3.get(d1, i) + win3.around(d2, i))
+    win3.each(0, d3, lambda i: win3.around(d1, i))
+    restrict(d3, pair, y4, 0, 0)
+    f4[...] = f4_local[...] + exact_nn(flat(y4), mix_ref[13]).reshape(f4.shape)
+    ends = exact_nn(om_ref[:, 0:k], got_ref[:, lanes : lanes + y4.shape[0] * y4.shape[1]])
+    ends = ends + exact_nt(w4_ref[...], flat(y4))
+
+    src, buffers = d1, (d2, d3)
+    d1[...] = tn(got3, mix_ref[17, 0:k]).reshape(d1.shape)
+    for n, q in enumerate((2, 1, 0)):
+        dst = buffers[n % 2] if n < 2 else d1
+        dst[...] = tn(got3, mix_ref[14 + q, 0:k]).reshape(d1.shape)
+        win3.each(0, dst, lambda i, src=src, dst=dst: win3.get(dst, i) + win3.around(src, i))
+        src = dst
+    inverse_e = 1.0 / jnp.full((8, 128), e_ref[3], F32)
+    bases = v3[...] * inverse_e
+    bases = jnp.concatenate([bases * inverse_e, jnp.zeros((120, 128), F32)], 0)
+    known3[...] = known3_local[...] + exact_nn(flat(src), bases).reshape(known3.shape)
+
+    win = Window(f4.shape[:2])
+    line_powers(flat(f4), ends, power4, link4, 2, (b1, b2), exact=True)
+    inverse_e = 1.0 / jnp.full((f4.shape[1], 128), e_ref[LEVELS - 1], F32)
 
     def one(i):
         c4[i] = (0.96 * b1[i] + 0.64 * win.around(b2, i)) * inverse_e
 
-    rows(0, win.x, one)
-    win3 = Window(w3.shape[:2])
+    win.loop(0, one)
     prolong(c4, True, w3, win3, 0, 0, win.x, win.y)
-    win0, win1, win2 = up_windows(where_ref, s0, grids, w2.shape[:2], w1.shape[:2], w0.shape[:2])
+    _, win1, win2 = up_windows(where_ref, s0, grids, w2.shape[:2], w1.shape[:2], w1.shape[:2])
     at1, at2 = UP_LANES[0], UP_LANES[0] + UP_LANES[1]
     out_ref[0] = jnp.zeros(out_ref.shape[1:], F32)
 
     def local(win, w, known, power, x1, x2, t, c):
-        field = flat(w)
-        x1[...] = exact_nt(field, power[0]).reshape(x1.shape)
-        x2[...] = exact_nt(field, power[1]).reshape(x2.shape)
+        field = halves(flat(w))
+        x1[...] = nt(field, power[0]).reshape(x1.shape)
+        x2[...] = nt(field, power[1]).reshape(x2.shape)
         c[...] = jnp.zeros_like(c)
         smoothed_residual(win, w, x1, x2, t, c, 2, masked=True, add=known)
 
@@ -797,8 +836,7 @@
     to_level_one(c2, w1, win1)
     words(v1, w1, 0, at1)
     local(win1, w1, known1, power1, r1, r2, rt, c1_ref)
-    to_level_zero(c1_ref, w0, win0)
-    value = exact_nt(v0[...], flat(w0))
+    value = exact_nt(v0[...], flat(c1_ref))
     out_ref[0, :, 0 : value.shape[1]] = value
     for m in range(1, out_ref.shape[0]):
         out_ref[m] = out_ref[0]
@@ -810,7 +848,7 @@
     d1, d2, d3, fine, pad, y2, g1, g2, g3, y1, h1, h2, h3, c1, w, q, x1, x2, xm, t0, t1
 ):
     win0, win1, win2 = up_windows(where_ref, s0, grids, y2.shape[:2], y1.shape[:2], w.shape[:2])
-    lines0, lines1 = w.shape[0] * w.shape[1], y1.shape[0] * y1.shape[1]
+    lines1 = y1.shape[0] * y1.shape[1]
     lines2, lines3 = y2.shape[0] * y2.shape[1], d1.shape[0] * d1.shape[1]
     at1, at2 = UP_LANES[0], UP_LANES[0] + UP_LANES[1]
     k = got_ref.shape[0]
@@ -840,15 +878,15 @@
     got1 = got_ref[:, at1 : at1 + lines1]
     coefficients(win1, got1, y1, mix_ref[10], mix_ref[11], maps, h1, h2, h3, 2)
     c1[...] = c1_local[...] + exact_nn(flat(h3), basis_ref[...]).reshape(c1.shape)
+    h3[...] = h3[...] + tn(got_ref[:, 0:lines1], mix_ref[12, 0:k]).reshape(h3.shape)
     to_level_zero(c1, w, win0)
     to_level_zero(h3, q, win0)
-    q[...] = q[...] + tn(got_ref[:, 0:lines0], mix_ref[12, 0:k]).reshape(q.shape)
 
     hx, hy = (w.shape[0] - s0[0]) // 2, (w.shape[1] - s0[1]) // 2
     sy = s0[1]
     win = win0
     field, ends = flat(w), flat(q)
-    lane_powers(field, ends, 64, power_ref, link_ref, 2, (x1, x2), exact=True)
+    lane_powers(field, ends, 64, power_ref, link_ref, 2, (x1, x2))
     n = field.shape[1]
     m_link = jnp.concatenate([jnp.zeros((64, n), F32), m_link_ref[...], jnp.zeros((n - 72, n), F32)], 0)
     xm[...] = (exact_nt(field, m_ref[...]) + exact_nn(ends, m_link)).reshape(xm.shape)
@@ -957,12 +995,12 @@
     low, high, table = lax.optimization_barrier((*halo_y(right_side, 12), table))
     f0 = halo_x(jnp.concatenate([low, right_side, high], axis=1), 12)
     table = exchange(table)
-    *om, om_up, m_matrix, m_link, mix, up_mix, w2_map = call(
+    *om, om_up, m_matrix, m_link, mix, up_mix, w2_map, w4_map = call(
         coupling_kernel,
-        [(8, n)] * LEVELS + [(8, n), (n, n), (8, n), (11, n, n), (13, n, n), (8, n)],
+        [(8, n)] * LEVELS + [(8, n), (n, n), (8, n), (11, n, n), (18, n, n), (8, n), (8, n)],
         [(gz, 8, 8, n), (n, n)],
         (0, 2),
-        where, table, e, faces, basis,
+        where, table, e, faces, basis, basis_up,
     )
 
     s0, s1, s2 = (sx, sy), (sx // 2, sy // 2), (sx // 4, sy // 4)
@@ -978,15 +1016,14 @@
         where, f0, power[0], power[1], ends[0], ends[1], ends[2],
     )
     got = stacked(copies)
-    many = gx * gy
     f1, own1, parts = call(
         part(joined_down_kernel, s0, s1, ext0, grids),
-        [cube1, cube1, (many, s2[0] + 1, s2[1], n)],
+        [cube1, cube1, (gy, s2[0] + 1, s2[1], n)],
         [cube0] * 3 + [(ext1[0], ext0[1], n)] + [cube1] * 4 + [(s2[0], ext1[1], n), s2 + (n,)],
         (0,),
         where, got, f1_local, f2_local, mix, om[2], w2_map,
     )
-    parts = lax.all_to_all(parts, ("gx", "gy"), 0, 0, tiled=True)
+    parts = exchange(parts, "gy")
     inner0 = (sx + 8, sy + 8, n)
     known0, twice0 = call(
         part(known_zero_kernel, s0, ext0, grids[0]),
@@ -1004,54 +1041,53 @@
         where, e, f1, own1, power[1], link[1],
         flops=10000000000,
     )
-    parts, known0, twice0, known1 = lax.optimization_barrier((parts, known0, twice0, known1))
+    parts, known1 = lax.optimization_barrier((parts, known1))
+    parts = exchange(jnp.broadcast_to(parts[None], (gx,) + parts.shape), "gx")
+    parts, known0, twice0 = lax.optimization_barrier((parts, known0, twice0))
+    parts = parts.reshape((gx * gy,) + parts.shape[2:])
 
     cubes = [g + (n,) for g in grids]
     lines = [g[0] * g[1] for g in grids]
     margin = s2[0]
     region = (3 * s2[0], 3 * s2[1], n)
     padded = (grids[2][0] + 2 * margin, grids[2][1] + 2 * margin, n)
-    f3, copies = call(
+    f3, f4_local, copies = call(
         part(gathered_down_kernel, gx, gy),
-        [cubes[3], (gz, 8, lines[3])],
-        [cubes[2], (lines[2], n), (8, lines[2])] + [cubes[2]] * 4 + [(grids[3][0], grids[2][1], n)],
+        [cubes[3], cubes[4], (gz, 8, lines[3] + lines[4])],
+        [cubes[2], (lines[2], n), (8, lines[2])]
+        + [cubes[2]] * 4
+        + [(grids[3][0], grids[2][1], n)]
+        + [cubes[3]] * 4
+        + [(grids[4][0], grids[3][1], n)],
         (),
-        parts, power[2], link[2], ends[3],
-    )
-    got3 = stacked(copies)
+        parts, power[2], link[2], power[3], ends[3], ends[4],
+    )
+    got34 = stacked(copies)
+    parts, f3 = lax.optimization_barrier((parts, f3))
     (known2,) = call(
         part(known_two_kernel, gx, gy, grids[2]),
         [region],
         [(region[0] * region[1], n), (8, region[0] * region[1])] + [region] * 6,
         (0, 1),
         where, e, parts, power[2], link[2],
-        flops=8000000000,
-    )
-    got3, known2 = lax.optimization_barrier((got3, known2))
-    f4, copies = call(
-        whole_down_kernel,
-        [cubes[4], (gz, 8, lines[4])],
-        [cubes[3]] * 4 + [(grids[4][0], grids[3][1], n)],
-        (),
-        f3, got3, om[3], power[3], link[3], ends[4],
-    )
-    got4 = stacked(copies)
-    (known3,) = call(
-        part(whole_known_kernel, 3),
+        flops=500000000,
+    )
+    (known3_local,) = call(
+        part(local_known_kernel, 3),
         [cubes[3]],
         [cubes[3]] * 6,
         (0,),
-        e, f3, got3, om[3], power[3], link[3],
-        flops=8000000000,
-    )
-    got4, known3 = lax.optimization_barrier((got4, known3))
+        e, f3, power[3],
+        flops=500000000,
+    )
+    got34, known2, known3_local = lax.optimization_barrier((got34, known2, known3_local))
 
     copies, c1_local = call(
         part(local_up_kernel, s0, grids, margin),
         [(gz, 8, sum(UP_LANES)), cube1],
-        [cubes[4]] * 3 + [cubes[3]] * 5 + [cubes[2], padded] + [region] * 5 + [cube1] * 4 + [inner0],
+        [cubes[3]] * 3 + [(grids[4][0], grids[3][1], n)] + [cubes[4]] * 2 + [cubes[3]] + [cubes[4]] * 3 + [cubes[3]] * 5 + [cubes[2], padded] + [region] * 5 + [cube1] * 4,
         (0, 1),
-        where, e, f4, got4, om[4], power[4], link[4], known3, known2, known1,
+        where, e, f4_local, got34, om[4], w4_map, up_mix, power[4], link[4], known3_local, known2, known1,
         power[3], power[2], power[1], ends[3], ends[2], ends[1], ends_up,
     )
     u, r = call(

time: 178 us -> 162 us (0.910)
  Pallas kernels: 76.3 us -> 69.7 us
  waiting for transfers between devices: 27.3 us -> 22.5 us
  starting transfers between devices: 49.4 us -> 45.8 us
  blocking collectives: 17 us -> 15.2 us
    all_to_all x1 -> x0, waiting for transfers between devices: 14.4 us -> none  [body(): parts = lax.all_to_all(parts, ('gx', 'gy'), 0, 0, tiled=True)]
    all_to_all x1 -> x0, starting transfers between devices: 12.7 us -> none  [body(): parts = lax.all_to_all(parts, ('gx', 'gy'), 0, 0, tiled=True)]
    all_to_all x4 -> x5, waiting for transfers between devices: 11.6 us -> 21.2 us  [exchange(): got = lax.all_to_all(copies, axes, 0, 0, tiled=True)]
    all_to_all x4 -> x5, starting transfers between devices: 25.6 us -> 34.7 us  [exchange(): got = lax.all_to_all(copies, axes, 0, 0, tiled=True)]
    pallas_call x12 -> x11, Pallas kernels: 76.3 us -> 69.7 us  [call(): pl.pallas_call(kernel, out_shape=[jax.ShapeDtypeStruct(s, F32) for s in o...]
    all_to_all x1, blocking collectives: 17 us -> 15.2 us  [exchange(): got = lax.all_to_all(copies, axes, 0, 0, tiled=True)]
  transfers between devices with their start and end apart: 9 -> 9, of which waited for: 5 -> 4; matrix products, arithmetic and copies ran while one was open for 1% -> 1% of each run, Pallas kernels for 22% -> 23%
where the time goes in v4:
time: 162 us; the launch traced here: 161 us
  Pallas kernels  69.7 us (43%)
  starting transfers between devices  45.8 us (28%)
  waiting for transfers between devices  22.5 us (14%)
  blocking collectives  15.2 us (9%)
  local copies, waits for them, and re-layouts  4.94 us (3%)
  other arithmetic  1.95 us (1%)
    pallas_call x11, Pallas kernels, call(): pl.pallas_call(kernel, out_shape=[jax.ShapeDtypeStruct(s, F32) for s in o...  69.7 us
    all_to_all x5, starting transfers between devices, exchange(): got = lax.all_to_all(copies, axes, 0, 0, tiled=True)  34.7 us
    all_to_all x5, waiting for transfers between devices, exchange(): got = lax.all_to_all(copies, axes, 0, 0, tiled=True)  21.2 us
    all_to_all x1, blocking collectives, exchange(): got = lax.all_to_all(copies, axes, 0, 0, tiled=True)  15.2 us
    ppermute x2, starting transfers between devices, edges(): lax.ppermute(last, axis, up)  8.47 us
  transfers between devices with their start and end apart: 9, of which 4 were waited for; matrix products, arithmetic and copies ran while one was open for 1% of the time, Pallas kernels for 23%

profile of v4, /device:TPU:1, one launch (start us, length us, event | category | flops | bytes accessed | tf_op | source)
XLA Modules:
  0.0 160.9 jit_solution(18170655508089979025)
XLA Ops:
  0.6 1.1 fusion
  1.8 1.3 collective-permute-start.1
  3.1 5.0 %collective-permute-start = (f32[32,12,128]{2,1,0:T(8,128)S(1)}, f32[32,12,128]{2,1,0:T(8,128)S(1)}, u32[]{:S(2)}, u32[]{:S(2)}) collective-permute-start(f32[32,12,128]{2,1,0:T(8,128)S(1)} %get-tuple-element.109), channel_id=1, source_target_pairs={{0,8},{8,16},{16,24},{24,32},{32,40},{40,48},{48,56},{1,9},{9,17},... | collective-permute-start | bytes 589832 | tf_op jit(solution)/shard_map/ppermute | solution.py:964
  8.1 4.5 %shard_map.59 = (f32[4,128,128]{2,1,0:T(8,128)}, f32[4,128,128]{2,1,0:T(8,128)}, f32[4,128,128]{2,1,0:T(8,128)}, f32[4,128,128]{2,1,0:T(8,128)}, f32[4,128,128]{...) custom-call(f32[5,128,128]{2,1,0:T(8,128)} %g_ref.1, ...), custom_call_target="tpu_custom_call" | custom-call | flops 1000000 | bytes 1000000 | tf_op jit(solution)/shard_map/pallas_call | solution.py:938
  12.7 3.5 %collective-permute-start.2 = (f32[12,56,128]{2,1,0:T(8,128)S(1)}, f32[12,56,128]{2,1,0:T(8,128)S(1)}, u32[]{:S(2)}, u32[]{:S(2)}) collective-permute-start(f32[12,56,128]{2,1,0:T(8,128)S(1)} %get-tuple-element.106), channel_id=1, source_target_pairs={{0,64},{64,128},{128,192},{1,65},{65,129},{129,193},{2,66},{66,130... | collective-permute-start | bytes 1032200 | tf_op jit(solution)/shard_map/ppermute | solution.py:964
  16.2 1.3 collective-permute-start.3
  17.5 6.4 %all-to-all-start.1 = ((f32[8,11,8,128]{3,2,1,0:T(8,128)}), f32[8,11,8,128]{3,2,1,0:T(8,128)S(1)}, u32[]{:S(2)}, u32[]{:S(2)}) async-start(f32[8,11,8,128]{3,2,1,0:T(8,128)} %get-tuple-element.65), calls=%async_computation.1 | async-start | bytes 720896 | tf_op jit(solution)/shard_map/all_to_all | solution.py:950
  23.8 0.6 pad_add_fusion.where_ref
  24.4 1.4 collective-permute-done.3
  25.8 1.3 pad_maximum_fusion.f_ref
  27.1 6.9 %shard_map.60 = (f32[8,8,4224]{2,1,0:T(8,128)}, f32[26,32,128]{2,1,0:T(8,128)}, f32[8,8,128]{2,1,0:T(8,128)}) custom-call(s32[3]{0:T(128)} %pad_add_fusion.where_ref, f32[56,56,128]{2,1,0:T(8,128)} %pad_maximum_fusion.f_ref, f32[4,128,128]{2,1,0:T(8,128)} %get-tuple-element.57.power0.power_ref, f32[4,128,128]{2,1,0:T(8,128)} %get-tuple-element.58.power1.power_ref, ...), custom_call_target="tpu_custom_call" | custom-call | flops 1000000 | bytes 1000000 | tf_op jit(solution)/shard_map/pallas_call | solution.py:938
  34.0 7.2 %all-to-all-start = ((f32[8,8,4224]{2,1,0:T(8,128)}), f32[8,8,4224]{2,1,0:T(8,128)S(1)}, u32[]{:S(2)}, u32[]{:S(2)}) async-start(f32[8,8,4224]{2,1,0:T(8,128)} %get-tuple-element.62), calls=%async_computation | async-start | bytes 2162688 | tf_op jit(solution)/shard_map/all_to_all | solution.py:950
  41.2 5.4 %shard_map.61 = (f32[8,128]{1,0:T(8,128)}, f32[8,128]{1,0:T(8,128)}, f32[8,128]{1,0:T(8,128)}, f32[8,128]{1,0:T(8,128)}, f32[8,128]{1,0:T(8,128)}, /*index=5*/f3...) custom-call(s32[3]{0:T(128)} %pad_add_fusion.where_ref, ...), custom_call_target="tpu_custom_call" | custom-call | flops 1000000 | bytes 1000000 | tf_op jit(solution)/shard_map/pallas_call | solution.py:938
  46.6 9.9 %all-to-all-done = f32[8,8,4224]{2,1,0:T(8,128)S(1)} async-done(((f32[8,8,4224]{2,1,0:T(8,128)}), f32[8,8,4224]{2,1,0:T(8,128)S(1)}, u32[]{:S(2)}, u32[]{:S(2)}) %all-to-all-start) | async-done | bytes 1081376 | tf_op jit(solution)/shard_map/all_to_all | solution.py:950
  56.5 1.0 copy-done.2
  57.5 6.5 %shard_map.62 = (f32[26,32,128]{2,1,0:T(8,128)}, f32[26,32,128]{2,1,0:T(8,128)}, f32[8,9,8,128]{3,2,1,0:T(8,128)}) custom-call(s32[3]{0:T(128)} %pad_add_fusion.where_ref, f32[64,4224]{1,0:T(8,128)} %bitcast.10, f32[26,32,128]{2,1,0:T(8,128)} %get-tuple-element.63.f1_local, f32[8,8,128]{2,1,0:T(8,128)} %get-tuple-element.64.f2_local, ...), custom_call_target="tpu_custom_call" | custom-call | flops 1000000 | bytes 1000000 | tf_op jit(solution)/shard_map/pallas_call | solution.py:938
  64.0 10.0 %all-to-all-start.2 = ((f32[8,9,8,128]{3,2,1,0:T(8,128)}), f32[8,9,8,128]{3,2,1,0:T(8,128)S(1)}, u32[]{:S(2)}, u32[]{:S(2)}) async-start(f32[8,9,8,128]{3,2,1,0:T(8,128)} %get-tuple-element.71), calls=%async_computation.2 | async-start | bytes 589824 | tf_op jit(solution)/shard_map/all_to_all | solution.py:950
  73.9 5.1 %shard_map.63.known1 = f32[26,32,128]{2,1,0:T(8,128)} custom-call(s32[3]{0:T(128)} %pad_add_fusion.where_ref, f32[5]{0:T(128)} %e_ref.15, f32[26,32,128]{2,1,0:T(8,128)} %get-tuple-element.72.f_ref, f32[26,32,128]{2,1,0:T(8,128)} %get-tuple-element.73.own_ref, f32[4,128,128]{2,1,0:T(8,128)} %get-tuple-element.58.power1.power_ref, ...), custom_call_target="tpu_custom_call" | custom-call | flops 10000000000 | bytes 1000000 | tf_op jit(solution)/shard_map/pallas_call | solution.py:938
  79.0 5.7 %all-to-all-done.2 = f32[8,9,8,128]{3,2,1,0:T(8,128)S(1)} async-done(((f32[8,9,8,128]{3,2,1,0:T(8,128)}), f32[8,9,8,128]{3,2,1,0:T(8,128)S(1)}, u32[]{:S(2)}, u32[]{:S(2)}) %all-to-all-start.2) | async-done | bytes 294944 | tf_op jit(solution)/shard_map/all_to_all | solution.py:950
  84.7 1.1 broadcast_in_dim.2
  85.8 3.7 %all-to-all-start.3 = ((f32[4,8,9,8,128]{4,3,2,1,0:T(8,128)}), f32[4,8,9,8,128]{4,3,2,1,0:T(8,128)S(1)}, u32[]{:S(2)}, u32[]{:S(2)}) async-start(f32[4,8,9,8,128]{4,3,2,1,0:T(8,128)} %broadcast_in_dim.2), calls=%async_computation.3 | async-start | bytes 2359296 | tf_op jit(solution)/shard_map/all_to_all | solution.py:950
  89.5 7.7 %shard_map.64 = (f32[32,32,128]{2,1,0:T(8,128)}, f32[32,32,128]{2,1,0:T(8,128)}) custom-call(s32[3]{0:T(128)} %pad_add_fusion.where_ref, f32[5]{0:T(128)} %e_ref.15, f32[56,56,128]{2,1,0:T(8,128)} %pad_maximum_fusion.f_ref, f32[64,4224]{1,0:T(8,128)} %bitcast.11, f32[11,128,128]{2,1,0:T(8,128)} %get-tuple-element.68.mix_ref, ...), custom_call_target="tpu_custom_call" | custom-call | flops 20000000000 | bytes 1000000 | tf_op jit(solution)/shard_map/pallas_call | solution.py:938
  97.3 5.5 %all-to-all-done.3 = f32[4,8,9,8,128]{4,3,2,1,0:T(8,128)S(1)} async-done(((f32[4,8,9,8,128]{4,3,2,1,0:T(8,128)}), f32[4,8,9,8,128]{4,3,2,1,0:T(8,128)S(1)}, u32[]{:S(2)}, u32[]{:S(2)}) %all-to-all-start.3) | async-done | bytes 1179680 | tf_op jit(solution)/shard_map/all_to_all | solution.py:950
  102.8 1.0 copy-done.1
  103.9 5.6 %shard_map.65 = (f32[16,32,128]{2,1,0:T(8,128)}, f32[8,16,128]{2,1,0:T(8,128)}, f32[8,8,640]{2,1,0:T(8,128)}) custom-call(f32[32,9,8,128]{3,2,1,0:T(8,128)} %bitcast.8, f32[4,128,128]{2,1,0:T(8,128)} %get-tuple-element.80.power_ref.power2, f32[4,8,128]{2,1,0:T(8,128)} %get-tuple-element.81.link_ref, f32[4,128,128]{2,1,0:T(8,128)} %get-tuple-element.82.power3.power_ref, ...), custom_call_target="tpu_custom_call" | custom-call | flops 1000000 | bytes 1000000 | tf_op jit(solution)/shard_map/pallas_call | solution.py:938
  109.5 7.5 %all-to-all-start.4 = ((f32[8,8,640]{2,1,0:T(8,128)}), f32[8,8,640]{2,1,0:T(8,128)S(1)}, u32[]{:S(2)}, u32[]{:S(2)}) async-start(f32[8,8,640]{2,1,0:T(8,128)} %get-tuple-element.86), calls=%async_computation.4 | async-start | bytes 327680 | tf_op jit(solution)/shard_map/all_to_all | solution.py:950
  116.9 4.5 %shard_map.66.known2 = f32[24,24,128]{2,1,0:T(8,128)} custom-call(s32[3]{0:T(128)} %pad_add_fusion.where_ref, f32[5]{0:T(128)} %e_ref.15, f32[32,9,8,128]{3,2,1,0:T(8,128)} %bitcast.9, f32[4,128,128]{2,1,0:T(8,128)} %get-tuple-element.80.power_ref.power2, f32[4,8,128]{2,1,0:T(8,128)} %get-tuple-element.81.link_ref), custom_call_target="tpu_custom_call" | custom-call | flops 500000000 | bytes 1000000 | tf_op jit(solution)/shard_map/pallas_call | solution.py:938
  121.5 3.0 %shard_map.67.known3_local = f32[16,32,128]{2,1,0:T(8,128)} custom-call(f32[5]{0:T(128)} %e_ref.15, f32[16,32,128]{2,1,0:T(8,128)} %get-tuple-element.89.f_ref, f32[4,128,128]{2,1,0:T(8,128)} %get-tuple-element.82.power3.power_ref), custom_call_target="tpu_custom_call" | custom-call | flops 500000000 | bytes 1000000 | tf_op jit(solution)/shard_map/pallas_call | solution.py:938
  124.4 0.7 copy-done.4
  125.1 9.0 %shard_map.68 = (f32[8,8,2304]{2,1,0:T(8,128)}, f32[26,32,128]{2,1,0:T(8,128)}) custom-call(s32[3]{0:T(128)} %pad_add_fusion.where_ref, f32[5]{0:T(128)} %e_ref.15, f32[8,16,128]{2,1,0:T(8,128)} %get-tuple-element.85.f4_local, f32[64,640]{1,0:T(8,128)} %bitcast.13, f32[8,128]{1,0:T(8,128)} %get-tuple-element.91.om_ref, f32[8,128]{1,0:T(8,128)} %get-tuple-element.92.w4_ref, ...), custom_call_target="tpu_custom_call" | custom-call | flops 1000000 | bytes 1000000 | tf_op jit(solution)/shard_map/pallas_call | solution.py:938
  134.1 15.2 %all_to_all.30 = f32[8,8,2304]{2,1,0:T(8,128)} all-to-all(f32[8,8,2304]{2,1,0:T(8,128)} %get-tuple-element.100), channel_id=1, replica_groups=mesh['gx'=4,'gy'=8,'gz'=8] {'gz'}, dimensions={0} | all-to-all | bytes 1179648 | tf_op jit(solution)/shard_map/all_to_all | solution.py:950
  149.3 11.5 %shard_map.69 = (f32[32,32,128]{2,1,0:T(8,128)}, f32[32,32,128]{2,1,0:T(8,128)}) custom-call(s32[3]{0:T(128)} %pad_add_fusion.where_ref, f32[5]{0:T(128)} %e_ref.15, f32[64,2304]{1,0:T(8,128)} %bitcast.12, f32[26,32,128]{2,1,0:T(8,128)} %get-tuple-element.101.c1_local, f32[32,32,128]{2,1,0:T(8,128)} %get-tuple-element.102.known_ref, ...), custom_call_target="tpu_custom_call" | custom-call | flops 1000000 | bytes 1000000 | tf_op jit(solution)/shard_map/pallas_call | solution.py:938
  (13 shorter events, 0.1 us)
Async XLA Ops:
  0.6 12.0 %copy-start = (f32[32,32,128]{2,1,0:T(8,128)S(1)}, f32[32,32,128]{2,1,0:T(8,128)}, u32[]{:S(2)}) copy-start(f32[32,32,128]{2,1,0:T(8,128)} %param.4) | copy-start | bytes 1572868
  1.8 10.8 %collective-permute-start.1 = (f32[32,12,128]{2,1,0:T(8,128)S(1)}, f32[32,12,128]{2,1,0:T(8,128)S(1)}, u32[]{:S(2)}, u32[]{:S(2)}) collective-permute-start(f32[32,12,128]{2,1,0:T(8,128)S(1)} %get-tuple-element.108), channel_id=1, source_target_pairs={{8,0},{16,8},{24,16},{32,24},{40,32},{48,40},{56,48},{9,1},{17,9},... | collective-permute-start | bytes 589832 | tf_op jit(solution)/shard_map/ppermute | solution.py:964
  3.1 9.5 %collective-permute-start = (f32[32,12,128]{2,1,0:T(8,128)S(1)}, f32[32,12,128]{2,1,0:T(8,128)S(1)}, u32[]{:S(2)}, u32[]{:S(2)}) collective-permute-start(f32[32,12,128]{2,1,0:T(8,128)S(1)} %get-tuple-element.109), channel_id=1, source_target_pairs={{0,8},{8,16},{16,24},{24,32},{32,40},{40,48},{48,56},{1,9},{9,17},... | collective-permute-start | bytes 589832 | tf_op jit(solution)/shard_map/ppermute | solution.py:964
  12.7 11.7 %collective-permute-start.2 = (f32[12,56,128]{2,1,0:T(8,128)S(1)}, f32[12,56,128]{2,1,0:T(8,128)S(1)}, u32[]{:S(2)}, u32[]{:S(2)}) collective-permute-start(f32[12,56,128]{2,1,0:T(8,128)S(1)} %get-tuple-element.106), channel_id=1, source_target_pairs={{0,64},{64,128},{128,192},{1,65},{65,129},{129,193},{2,66},{66,130... | collective-permute-start | bytes 1032200 | tf_op jit(solution)/shard_map/ppermute | solution.py:964
  16.2 9.6 %collective-permute-start.3 = (f32[12,56,128]{2,1,0:T(8,128)S(1)}, f32[12,56,128]{2,1,0:T(8,128)S(1)}, u32[]{:S(2)}, u32[]{:S(2)}) collective-permute-start(f32[12,56,128]{2,1,0:T(8,128)S(1)} %get-tuple-element.107), channel_id=1, source_target_pairs={{64,0},{128,64},{192,128},{65,1},{129,65},{193,129},{66,2},{130,66... | collective-permute-start | bytes 1032200 | tf_op jit(solution)/shard_map/ppermute | solution.py:964
  17.5 16.5 %all-to-all-start.1 = ((f32[8,11,8,128]{3,2,1,0:T(8,128)}), f32[8,11,8,128]{3,2,1,0:T(8,128)S(1)}, u32[]{:S(2)}, u32[]{:S(2)}) async-start(f32[8,11,8,128]{3,2,1,0:T(8,128)} %get-tuple-element.65), calls=%async_computation.1 | async-start | bytes 720896 | tf_op jit(solution)/shard_map/all_to_all | solution.py:950
  34.0 7.3 %copy-start.3 = (f32[8,11,8,128]{3,2,1,0:T(8,128)}, f32[8,11,8,128]{3,2,1,0:T(8,128)S(1)}, u32[]{:S(2)}) copy-start(f32[8,11,8,128]{3,2,1,0:T(8,128)S(1)} %all-to-all-done.1.table_ref) | copy-start | bytes 1081348
  34.0 22.6 %all-to-all-start = ((f32[8,8,4224]{2,1,0:T(8,128)}), f32[8,8,4224]{2,1,0:T(8,128)S(1)}, u32[]{:S(2)}, u32[]{:S(2)}) async-start(f32[8,8,4224]{2,1,0:T(8,128)} %get-tuple-element.62), calls=%async_computation | async-start | bytes 2162688 | tf_op jit(solution)/shard_map/all_to_all | solution.py:950
  56.5 1.0 copy-start.2
  64.0 20.8 %all-to-all-start.2 = ((f32[8,9,8,128]{3,2,1,0:T(8,128)}), f32[8,9,8,128]{3,2,1,0:T(8,128)S(1)}, u32[]{:S(2)}, u32[]{:S(2)}) async-start(f32[8,9,8,128]{3,2,1,0:T(8,128)} %get-tuple-element.71), calls=%async_computation.2 | async-start | bytes 589824 | tf_op jit(solution)/shard_map/all_to_all | solution.py:950
  85.8 17.0 %all-to-all-start.3 = ((f32[4,8,9,8,128]{4,3,2,1,0:T(8,128)}), f32[4,8,9,8,128]{4,3,2,1,0:T(8,128)S(1)}, u32[]{:S(2)}, u32[]{:S(2)}) async-start(f32[4,8,9,8,128]{4,3,2,1,0:T(8,128)} %broadcast_in_dim.2), calls=%async_computation.3 | async-start | bytes 2359296 | tf_op jit(solution)/shard_map/all_to_all | solution.py:950
  102.8 1.0 copy-start.1
  109.5 15.0 %all-to-all-start.4 = ((f32[8,8,640]{2,1,0:T(8,128)}), f32[8,8,640]{2,1,0:T(8,128)S(1)}, u32[]{:S(2)}, u32[]{:S(2)}) async-start(f32[8,8,640]{2,1,0:T(8,128)} %get-tuple-element.86), calls=%async_computation.4 | async-start | bytes 327680 | tf_op jit(solution)/shard_map/all_to_all | solution.py:950
  124.4 0.7 copy-start.4

commit v5 on v4

--- a/solution.py
+++ b/solution.py
@@ -496,6 +496,30 @@
     return (count + 127) // 128 * 128
 
 
+def split_lanes(ext):
+    count = next(r for r in range(ext[0] // 2, ext[0] + 1) if r * ext[1] % 128 == 0)
+    return count * ext[1], count
+
+
+def part_maps(matrix):
+    low = (lax.broadcasted_iota(jnp.int32, matrix.shape, 0) & 7) < 4
+    first, second = jnp.where(low, matrix, 0.0), jnp.where(low, 0.0, matrix)
+    count = matrix.shape[0]
+    return (first, pltpu.roll(first, 4, 0)), (pltpu.roll(second, count - 4, 0), second)
+
+
+def late_words_kernel(inner, f_ref, v_ref, out_ref):
+    cx, cy = (f_ref.shape[0] - inner[0]) // 2, (f_ref.shape[1] - inner[1]) // 2
+    half = inner[0] // 2
+    out_ref[0] = jnp.zeros(out_ref.shape[1:], F32)
+    for p in range(2):
+        field = f_ref[cx + p * half : cx + (p + 1) * half, cy : cy + inner[1]]
+        value = nt(v_ref[...], field.reshape(half * inner[1], 128))
+        out_ref[0, 4 * p : 4 * p + 4, 0 : half * inner[1]] = value[4:8]
+    for m in range(1, out_ref.shape[0]):
+        out_ref[m] = out_ref[0]
+
+
 def windows(where_ref, s0, s1, ext0, ext1, grids):
     h0 = tuple((a - b) // 2 for a, b in zip(ext0, s0))
     h1 = tuple((a - b) // 2 for a, b in zip(ext1, s1))
@@ -514,13 +538,15 @@
     field = halves(flat(f_ref))
     lanes0 = ext0[0] * ext0[1]
     lanes1 = ext1[0] * ext1[1]
-    at1 = padded_lanes(lanes0)
+    at1 = split_lanes(ext0)[0]
     at2 = at1 + padded_lanes(lanes1)
     many = out_ref.shape[0]
-    out_ref[0, :, at1 - 128 : at1] = jnp.zeros((8, 128), F32)
+    out_ref[0, :, 0:at1] = jnp.zeros((8, at1), F32)
     out_ref[0, :, at2 - 128 : at2] = jnp.zeros((8, 128), F32)
     out_ref[0, :, at2 : at2 + 128] = jnp.zeros((8, 128), F32)
-    out_ref[0, :, 0:lanes0] = nt(v0[...], field)
+    value = nt(v0[...], field)
+    out_ref[0, 0:4, 0:at1] = value[0:4, 0:at1]
+    out_ref[0, 4:8, 0 : lanes0 - at1] = value[0:4, at1:lanes0]
     x1[...] = nt(field, power0[0]).reshape(x1.shape)
     x2[...] = nt(field, power0[1]).reshape(x2.shape)
     smoothed_residual(win0, f_ref, x1, x2, t, r, 2, masked=True)
@@ -547,12 +573,15 @@
     win0, win1, h0, h1 = windows(where_ref, s0, s1, ext0, ext1, grids)
     lanes0 = ext0[0] * ext0[1]
     lanes1 = ext1[0] * ext1[1]
-    at1 = padded_lanes(lanes0)
+    at1, cut_x = split_lanes(ext0)
     at2 = at1 + padded_lanes(lanes1)
-    got0 = halves(got_ref[:, 0:lanes0])
     rows_in = got_ref.shape[0]
-    d1[...] = tn(got0, mix_ref[0, 0:rows_in]).reshape(d1.shape)
-    d2[...] = tn(got0, mix_ref[1, 0:rows_in]).reshape(d2.shape)
+    spans = ((0, cut_x, at1), (cut_x, ext0[0], lanes0 - at1))
+    for p, (lo, hi, count) in enumerate(spans):
+        got0 = halves(got_ref[:, 0:count])
+        for d, slot in ((d1, 0), (d2, 1)):
+            matrix = part_maps(mix_ref[slot, 0:rows_in])[0][p]
+            d[lo:hi] = tn(got0, matrix).reshape(hi - lo, ext0[1], 128)
 
     win0.each(1, d1, lambda i: win0.get(d1, i) + win0.mask(i, win0.around(d2, i)))
     win0.each(2, f, lambda i: win0.mask(i, win0.around(d1, i)))
@@ -595,14 +624,23 @@
 
 
 def known_zero_kernel(
-    s0, ext0, grid, where_ref, e_ref, f_ref, got_ref, mix_ref, power_ref, link_ref,
-    known_out, twice_out, own, f, x1, x2, x3, x4, t0, t1
+    s0, ext0, late_at, grid, where_ref, e_ref, f_ref, got_ref, late_ref, mix_ref, power_ref, link_ref,
+    known_out, twice_out, wide, own, f, x1, x2, x3, x4, t0, t1
 ):
     hx, hy = (f.shape[0] - s0[0]) // 2, (f.shape[1] - s0[1]) // 2
     cx, cy = (ext0[0] - f.shape[0]) // 2, (ext0[1] - f.shape[1]) // 2
     win = Window(f.shape[:2], (where_ref[0] * s0[0] - hx, where_ref[1] * s0[1] - hy), grid)
-    coefficients = tn(got_ref[:, 0 : ext0[0] * ext0[1]], mix_ref[0, 0 : got_ref.shape[0]])
-    own[...] = coefficients.reshape(ext0 + (128,))[cx : cx + f.shape[0], cy : cy + f.shape[1]]
+    early, late = part_maps(mix_ref[0, 0 : got_ref.shape[0]])
+    at1, cut_x = split_lanes(ext0)
+    spans = ((0, cut_x, at1), (cut_x, ext0[0], ext0[0] * ext0[1] - at1))
+    for p, (lo, hi, count) in enumerate(spans):
+        wide[lo:hi] = tn(got_ref[:, 0:count], early[p]).reshape(hi - lo, ext0[1], 128)
+    own[...] = wide[cx : cx + f.shape[0], cy : cy + f.shape[1]]
+    half = f.shape[0] // 2
+    words = late_ref[:, late_at : late_at + half * f.shape[1]]
+    for p in range(2):
+        part = slice(p * half, (p + 1) * half)
+        own[part] = own[part] + tn(words, late[p]).reshape(half, f.shape[1], 128)
     f[...] = f_ref[cx : cx + f.shape[0], cy : cy + f.shape[1]]
     xs = (x1, x2, x3, x4)
     lane_powers(flat(f), flat(own), 64, power_ref, link_ref, POWERS, xs)
@@ -675,7 +713,7 @@
 
 
 def gathered_down_kernel(
-    across, down, parts_ref, power_ref, link_ref, power3, v3, v4, coarse_ref, lower_ref, out_ref,
+    across, down, parts_ref, late_ref, power_ref, link_ref, power3, v3, v4, coarse_ref, lower_ref, out_ref,
     f, fp, ap, x1, x2, t, r, pair, y1, y2, ty, ry, pair3
 ):
     many, side = parts_ref.shape[0], parts_ref.shape[2]
@@ -704,6 +742,7 @@
     restrict(ry, pair3, lower_ref, 0, 0)
     value = nt(v4[...], flat(lower_ref))
     out_ref[0, :, lanes : lanes + value.shape[1]] = value
+    out_ref[0, :, lanes + value.shape[1] :] = late_ref[0]
     for m in range(1, out_ref.shape[0]):
         out_ref[m] = out_ref[0]
 
@@ -887,9 +926,14 @@
     win = win0
     field, ends = flat(w), flat(q)
     lane_powers(field, ends, 64, power_ref, link_ref, 2, (x1, x2))
-    n = field.shape[1]
-    m_link = jnp.concatenate([jnp.zeros((64, n), F32), m_link_ref[...], jnp.zeros((n - 72, n), F32)], 0)
-    xm[...] = (exact_nt(field, m_ref[...]) + exact_nn(ends, m_link)).reshape(xm.shape)
+    xm[...] = exact_nt(field, m_ref[...]).reshape(xm.shape)
+    below, above = m_link_ref[4:5], m_link_ref[5:6]
+
+    def link_ends(i):
+        a = q[i]
+        xm[i] = xm[i] + (pltpu.roll(a, 128 - 68, 1) * below + pltpu.roll(a, 127 - 69, 1) * above)
+
+    rows(0, q.shape[0], link_ends)
     e = e_ref[0]
     w_ref = w
 
@@ -1007,7 +1051,7 @@
     ext0, ext1 = (sx + 24, sy + 24), (sx // 2 + 10, sy // 2 + 16)
     cube0, cube1 = ext0 + (n,), ext1 + (n,)
     lines0, lines1 = ext0[0] * ext0[1], ext1[0] * ext1[1]
-    lanes = padded_lanes(lines0) + padded_lanes(lines1) + padded_lanes(s2[0] * s2[1])
+    lanes = split_lanes(ext0)[0] + padded_lanes(lines1) + padded_lanes(s2[0] * s2[1])
     copies, f1_local, f2_local = call(
         part(local_down_kernel, s0, s1, grids),
         [(gz, 8, lanes), cube1, s2 + (n,)],
@@ -1016,6 +1060,12 @@
         where, f0, power[0], power[1], ends[0], ends[1], ends[2],
     )
     got = stacked(copies)
+    inner0 = (sx + 8, sy + 8, n)
+    late_lanes = padded_lanes(inner0[0] * inner0[1] // 2)
+    (late,) = call(
+        part(late_words_kernel, inner0[:2]), [(1, 8, late_lanes)], [], (), f0, ends[0], flops=500000000
+    )
+    got, late = lax.optimization_barrier((got, late))
     f1, own1, parts = call(
         part(joined_down_kernel, s0, s1, ext0, grids),
         [cube1, cube1, (gy, s2[0] + 1, s2[1], n)],
@@ -1024,15 +1074,6 @@
         where, got, f1_local, f2_local, mix, om[2], w2_map,
     )
     parts = exchange(parts, "gy")
-    inner0 = (sx + 8, sy + 8, n)
-    known0, twice0 = call(
-        part(known_zero_kernel, s0, ext0, grids[0]),
-        [s0 + (n,), s0 + (n,)],
-        [inner0] * 8,
-        (0, 1),
-        where, e, f0, got, mix, power[0], link[0],
-        flops=20000000000,
-    )
     (known1,) = call(
         part(known_one_kernel, s1, grids[1]),
         [cube1],
@@ -1041,9 +1082,8 @@
         where, e, f1, own1, power[1], link[1],
         flops=10000000000,
     )
+    parts = exchange(jnp.broadcast_to(parts[None], (gx,) + parts.shape), "gx")
     parts, known1 = lax.optimization_barrier((parts, known1))
-    parts = exchange(jnp.broadcast_to(parts[None], (gx,) + parts.shape), "gx")
-    parts, known0, twice0 = lax.optimization_barrier((parts, known0, twice0))
     parts = parts.reshape((gx * gy,) + parts.shape[2:])
 
     cubes = [g + (n,) for g in grids]
@@ -1053,14 +1093,14 @@
     padded = (grids[2][0] + 2 * margin, grids[2][1] + 2 * margin, n)
     f3, f4_local, copies = call(
         part(gathered_down_kernel, gx, gy),
-        [cubes[3], cubes[4], (gz, 8, lines[3] + lines[4])],
+        [cubes[3], cubes[4], (gz, 8, lines[3] + lines[4] + late_lanes)],
         [cubes[2], (lines[2], n), (8, lines[2])]
         + [cubes[2]] * 4
         + [(grids[3][0], grids[2][1], n)]
         + [cubes[3]] * 4
         + [(grids[4][0], grids[3][1], n)],
         (),
-        parts, power[2], link[2], power[3], ends[3], ends[4],
+        parts, late, power[2], link[2], power[3], ends[3], ends[4],
     )
     got34 = stacked(copies)
     parts, f3 = lax.optimization_barrier((parts, f3))
@@ -1090,12 +1130,23 @@
         where, e, f4_local, got34, om[4], w4_map, up_mix, power[4], link[4], known3_local, known2, known1,
         power[3], power[2], power[1], ends[3], ends[2], ends[1], ends_up,
     )
+    got_up = stacked(copies)
+    got, c1_local = lax.optimization_barrier((got, c1_local))
+    known0, twice0 = call(
+        part(known_zero_kernel, s0, ext0, lines[3] + lines[4], grids[0]),
+        [s0 + (n,), s0 + (n,)],
+        [ext0 + (n,)] + [inner0] * 8,
+        (0, 1),
+        where, e, f0, got, got34, mix, power[0], link[0],
+        flops=500000000,
+    )
+    got_up, known0, twice0 = lax.optimization_barrier((got_up, known0, twice0))
     u, r = call(
         part(finish_kernel, s0, grids, margin),
         [s0 + (n,), s0 + (n,)],
         [cubes[3]] * 3 + [cubes[2], padded] + [region] * 4 + [cube1] * 5 + [inner0] * 7,
         (0, 1),
-        where, e, stacked(copies), c1_local, known0, twice0, up_mix, basis_up,
+        where, e, got_up, c1_local, known0, twice0, up_mix, basis_up,
         power[0], link[0], m_matrix, m_link,
     )
     return u, r

time: 162 us -> 159 us (0.981)
  waiting for transfers between devices: 22.5 us -> 15.3 us
  blocking collectives: 15.2 us -> 20.7 us
  starting transfers between devices: 45.8 us -> 40.6 us
  Pallas kernels: 69.7 us -> 72.4 us
    all_to_all x5, waiting for transfers between devices: 21.2 us -> 14 us  [exchange(): got = lax.all_to_all(copies, axes, 0, 0, tiled=True)]
    all_to_all x1, blocking collectives: 15.2 us -> 20.7 us  [exchange(): got = lax.all_to_all(copies, axes, 0, 0, tiled=True)]
    all_to_all x5, starting transfers between devices: 34.7 us -> 29.6 us  [exchange(): got = lax.all_to_all(copies, axes, 0, 0, tiled=True)]
    pallas_call x11 -> x12, Pallas kernels: 69.7 us -> 72.4 us  [call(): pl.pallas_call(kernel, out_shape=[jax.ShapeDtypeStruct(s, F32) for s in o...]
    unnamed x10 -> x12, local copies, waits for them, and re-layouts: 2.7 us -> 3.5 us
  transfers between devices with their start and end apart: 9 -> 9, of which waited for: 4 -> 5; matrix products, arithmetic and copies ran while one was open for 1% -> 1% of each run, Pallas kernels for 23% -> 25%
where the time goes in v5:
time: 159 us; the launch traced here: 158 us
  Pallas kernels  72.4 us (46%)
  starting transfers between devices  40.6 us (26%)
  blocking collectives  20.7 us (13%)
  waiting for transfers between devices  15.3 us (10%)
  local copies, waits for them, and re-layouts  5.74 us (4%)
  other arithmetic  2.04 us (1%)
    pallas_call x12, Pallas kernels, call(): pl.pallas_call(kernel, out_shape=[jax.ShapeDtypeStruct(s, F32) for s in o...  72.4 us
    all_to_all x5, starting transfers between devices, exchange(): got = lax.all_to_all(copies, axes, 0, 0, tiled=True)  29.6 us
    all_to_all x1, blocking collectives, exchange(): got = lax.all_to_all(copies, axes, 0, 0, tiled=True)  20.7 us
    all_to_all x5, waiting for transfers between devices, exchange(): got = lax.all_to_all(copies, axes, 0, 0, tiled=True)  14 us
    ppermute x2, starting transfers between devices, edges(): lax.ppermute(last, axis, up)  8.47 us
    unnamed x12, local copies, waits for them, and re-layouts  3.5 us
  transfers between devices with their start and end apart: 9, of which 5 were waited for; matrix products, arithmetic and copies ran while one was open for 1% of the time, Pallas kernels for 25%

profile of v5, /device:TPU:1, one launch (start us, length us, event | category | flops | bytes accessed | tf_op | source)
XLA Modules:
  0.0 157.5 jit_solution(6092748324311020775)
XLA Ops:
  0.6 1.1 fusion
  1.8 1.3 collective-permute-start.1
  3.1 5.0 %collective-permute-start = (f32[32,12,128]{2,1,0:T(8,128)S(1)}, f32[32,12,128]{2,1,0:T(8,128)S(1)}, u32[]{:S(2)}, u32[]{:S(2)}) collective-permute-start(f32[32,12,128]{2,1,0:T(8,128)S(1)} %get-tuple-element.117), channel_id=1, source_target_pairs={{0,8},{8,16},{16,24},{24,32},{32,40},{40,48},{48,56},{1,9},{9,17},... | collective-permute-start | bytes 589832 | tf_op jit(solution)/shard_map/ppermute | solution.py:1008
  8.1 4.5 %shard_map.59 = (f32[4,128,128]{2,1,0:T(8,128)}, f32[4,128,128]{2,1,0:T(8,128)}, f32[4,128,128]{2,1,0:T(8,128)}, f32[4,128,128]{2,1,0:T(8,128)}, f32[4,128,128]{...) custom-call(f32[5,128,128]{2,1,0:T(8,128)} %g_ref.1, ...), custom_call_target="tpu_custom_call" | custom-call | flops 1000000 | bytes 1000000 | tf_op jit(solution)/shard_map/pallas_call | solution.py:982
  12.7 3.5 %collective-permute-start.2 = (f32[12,56,128]{2,1,0:T(8,128)S(1)}, f32[12,56,128]{2,1,0:T(8,128)S(1)}, u32[]{:S(2)}, u32[]{:S(2)}) collective-permute-start(f32[12,56,128]{2,1,0:T(8,128)S(1)} %get-tuple-element.114), channel_id=1, source_target_pairs={{0,64},{64,128},{128,192},{1,65},{65,129},{129,193},{2,66},{66,130... | collective-permute-start | bytes 1032200 | tf_op jit(solution)/shard_map/ppermute | solution.py:1008
  16.2 1.3 collective-permute-start.3
  17.5 6.4 %all-to-all-start.1 = ((f32[8,11,8,128]{3,2,1,0:T(8,128)}), f32[8,11,8,128]{3,2,1,0:T(8,128)S(1)}, u32[]{:S(2)}, u32[]{:S(2)}) async-start(f32[8,11,8,128]{3,2,1,0:T(8,128)} %get-tuple-element.70), calls=%async_computation.1 | async-start | bytes 720896 | tf_op jit(solution)/shard_map/all_to_all | solution.py:994
  24.5 1.3 collective-permute-done.3
  25.8 1.3 pad_maximum_fusion.f_ref
  27.1 6.7 %shard_map.60 = (f32[8,8,2816]{2,1,0:T(8,128)}, f32[26,32,128]{2,1,0:T(8,128)}, f32[8,8,128]{2,1,0:T(8,128)}) custom-call(s32[3]{0:T(128)} %pad_add_fusion.where_ref, f32[56,56,128]{2,1,0:T(8,128)} %pad_maximum_fusion.f_ref, f32[4,128,128]{2,1,0:T(8,128)} %get-tuple-element.61.power0.power_ref, f32[4,128,128]{2,1,0:T(8,128)} %get-tuple-element.62.power1.power_ref, ...), custom_call_target="tpu_custom_call" | custom-call | flops 1000000 | bytes 1000000 | tf_op jit(solution)/shard_map/pallas_call | solution.py:982
  33.8 7.2 %all-to-all-start = ((f32[8,8,2816]{2,1,0:T(8,128)}), f32[8,8,2816]{2,1,0:T(8,128)S(1)}, u32[]{:S(2)}, u32[]{:S(2)}) async-start(f32[8,8,2816]{2,1,0:T(8,128)} %get-tuple-element.66), calls=%async_computation | async-start | bytes 1441792 | tf_op jit(solution)/shard_map/all_to_all | solution.py:994
  41.1 5.3 %shard_map.62 = (f32[8,128]{1,0:T(8,128)}, f32[8,128]{1,0:T(8,128)}, f32[8,128]{1,0:T(8,128)}, f32[8,128]{1,0:T(8,128)}, f32[8,128]{1,0:T(8,128)}, /*index=5*/f3...) custom-call(s32[3]{0:T(128)} %pad_add_fusion.where_ref, ...), custom_call_target="tpu_custom_call" | custom-call | flops 1000000 | bytes 1000000 | tf_op jit(solution)/shard_map/pallas_call | solution.py:982
  46.4 2.5 %shard_map.61.late_ref = f32[1,8,896]{2,1,0:T(8,128)} custom-call(f32[56,56,128]{2,1,0:T(8,128)} %pad_maximum_fusion.f_ref, f32[8,128]{1,0:T(8,128)} %get-tuple-element.63.v0.v_ref), custom_call_target="tpu_custom_call" | custom-call | flops 500000000 | bytes 1000000 | tf_op jit(solution)/shard_map/pallas_call | solution.py:982
  48.9 3.6 %all-to-all-done = f32[8,8,2816]{2,1,0:T(8,128)S(1)} async-done(((f32[8,8,2816]{2,1,0:T(8,128)}), f32[8,8,2816]{2,1,0:T(8,128)S(1)}, u32[]{:S(2)}, u32[]{:S(2)}) %all-to-all-start) | async-done | bytes 720928 | tf_op jit(solution)/shard_map/all_to_all | solution.py:994
  52.5 0.9 copy-done
  53.4 6.3 %shard_map.63 = (f32[26,32,128]{2,1,0:T(8,128)}, f32[26,32,128]{2,1,0:T(8,128)}, f32[8,9,8,128]{3,2,1,0:T(8,128)}) custom-call(s32[3]{0:T(128)} %pad_add_fusion.where_ref, f32[64,2816]{1,0:T(8,128)} %bitcast.8, f32[26,32,128]{2,1,0:T(8,128)} %get-tuple-element.68.f1_local, f32[8,8,128]{2,1,0:T(8,128)} %get-tuple-element.69.f2_local, ...), custom_call_target="tpu_custom_call" | custom-call | flops 1000000 | bytes 1000000 | tf_op jit(solution)/shard_map/pallas_call | solution.py:982
  59.8 20.7 %all_to_all.30 = f32[8,9,8,128]{3,2,1,0:T(8,128)S(1)} all-to-all(f32[8,9,8,128]{3,2,1,0:T(8,128)} %get-tuple-element.76), channel_id=1, replica_groups=mesh['gx'=4,'gy'=8,'gz'=8] {'gy'}, dimensions={0} | all-to-all | bytes 589824 | tf_op jit(solution)/shard_map/all_to_all | solution.py:994
  80.4 1.1 broadcast_in_dim.2
  81.5 3.7 %all-to-all-start.3 = ((f32[4,8,9,8,128]{4,3,2,1,0:T(8,128)}), f32[4,8,9,8,128]{4,3,2,1,0:T(8,128)S(1)}, u32[]{:S(2)}, u32[]{:S(2)}) async-start(f32[4,8,9,8,128]{4,3,2,1,0:T(8,128)} %broadcast_in_dim.2), calls=%async_computation.3 | async-start | bytes 2359296 | tf_op jit(solution)/shard_map/all_to_all | solution.py:994
  85.2 5.1 %shard_map.64.known1 = f32[26,32,128]{2,1,0:T(8,128)} custom-call(s32[3]{0:T(128)} %pad_add_fusion.where_ref, f32[5]{0:T(128)} %e_ref.15, f32[26,32,128]{2,1,0:T(8,128)} %get-tuple-element.77.f_ref, f32[26,32,128]{2,1,0:T(8,128)} %get-tuple-element.78.own_ref, f32[4,128,128]{2,1,0:T(8,128)} %get-tuple-element.62.power1.power_ref, ...), custom_call_target="tpu_custom_call" | custom-call | flops 10000000000 | bytes 1000000 | tf_op jit(solution)/shard_map/pallas_call | solution.py:982
  90.3 8.1 %all-to-all-done.3 = f32[4,8,9,8,128]{4,3,2,1,0:T(8,128)S(1)} async-done(((f32[4,8,9,8,128]{4,3,2,1,0:T(8,128)}), f32[4,8,9,8,128]{4,3,2,1,0:T(8,128)S(1)}, u32[]{:S(2)}, u32[]{:S(2)}) %all-to-all-start.3) | async-done | bytes 1179680 | tf_op jit(solution)/shard_map/all_to_all | solution.py:994
  98.4 1.0 copy-done.2
  99.5 5.6 %shard_map.65 = (f32[16,32,128]{2,1,0:T(8,128)}, f32[8,16,128]{2,1,0:T(8,128)}, f32[8,8,1536]{2,1,0:T(8,128)}) custom-call(f32[32,9,8,128]{3,2,1,0:T(8,128)} %bitcast.10, f32[1,8,896]{2,1,0:T(8,128)} %shard_map.61.late_ref, f32[4,128,128]{2,1,0:T(8,128)} %get-tuple-element.82.power_ref.power2, f32[4,8,128]{2,1,0:T(8,128)} %get-tuple-element.83.link_ref, ...), custom_call_target="tpu_custom_call" | custom-call | flops 1000000 | bytes 1000000 | tf_op jit(solution)/shard_map/pallas_call | solution.py:982
  105.1 7.6 %all-to-all-start.4 = ((f32[8,8,1536]{2,1,0:T(8,128)}), f32[8,8,1536]{2,1,0:T(8,128)S(1)}, u32[]{:S(2)}, u32[]{:S(2)}) async-start(f32[8,8,1536]{2,1,0:T(8,128)} %get-tuple-element.88), calls=%async_computation.4 | async-start | bytes 786432 | tf_op jit(solution)/shard_map/all_to_all | solution.py:994
  112.7 4.5 %shard_map.66.known2 = f32[24,24,128]{2,1,0:T(8,128)} custom-call(s32[3]{0:T(128)} %pad_add_fusion.where_ref, f32[5]{0:T(128)} %e_ref.15, f32[32,9,8,128]{3,2,1,0:T(8,128)} %bitcast.11, f32[4,128,128]{2,1,0:T(8,128)} %get-tuple-element.82.power_ref.power2, f32[4,8,128]{2,1,0:T(8,128)} %get-tuple-element.83.link_ref), custom_call_target="tpu_custom_call" | custom-call | flops 500000000 | bytes 1000000 | tf_op jit(solution)/shard_map/pallas_call | solution.py:982
  117.3 3.0 %shard_map.67.known3_local = f32[16,32,128]{2,1,0:T(8,128)} custom-call(f32[5]{0:T(128)} %e_ref.15, f32[16,32,128]{2,1,0:T(8,128)} %get-tuple-element.91.f_ref, f32[4,128,128]{2,1,0:T(8,128)} %get-tuple-element.84.power3.power_ref), custom_call_target="tpu_custom_call" | custom-call | flops 500000000 | bytes 1000000 | tf_op jit(solution)/shard_map/pallas_call | solution.py:982
  121.2 9.0 %shard_map.68 = (f32[8,8,2304]{2,1,0:T(8,128)}, f32[26,32,128]{2,1,0:T(8,128)}) custom-call(s32[3]{0:T(128)} %pad_add_fusion.where_ref, f32[5]{0:T(128)} %e_ref.15, f32[8,16,128]{2,1,0:T(8,128)} %get-tuple-element.87.f4_local, f32[64,1536]{1,0:T(8,128)} %bitcast.12, f32[8,128]{1,0:T(8,128)} %get-tuple-element.93.om_ref, f32[8,128]{1,0:T(8,128)} %get-tuple-element.94.w4_ref, ...), custom_call_target="tpu_custom_call" | custom-call | flops 1000000 | bytes 1000000 | tf_op jit(solution)/shard_map/pallas_call | solution.py:982
  130.2 4.7 %all-to-all-start.5 = ((f32[8,8,2304]{2,1,0:T(8,128)}), f32[8,8,2304]{2,1,0:T(8,128)S(1)}, u32[]{:S(2)}, u32[]{:S(2)}) async-start(f32[8,8,2304]{2,1,0:T(8,128)} %get-tuple-element.102), calls=%async_computation.5 | async-start | bytes 1179648 | tf_op jit(solution)/shard_map/all_to_all | solution.py:994
  134.9 8.1 %shard_map.69 = (f32[32,32,128]{2,1,0:T(8,128)}, f32[32,32,128]{2,1,0:T(8,128)}) custom-call(s32[3]{0:T(128)} %pad_add_fusion.where_ref, f32[5]{0:T(128)} %e_ref.15, f32[56,56,128]{2,1,0:T(8,128)} %pad_maximum_fusion.f_ref, f32[64,2816]{1,0:T(8,128)} %bitcast.9, f32[64,1536]{1,0:T(8,128)} %bitcast.13, f32[11,128,128]{2,1,0:T(8,128)} %get-tuple-element.73.mix_ref, ...), custom_call_target="tpu_custom_call" | custom-call | flops 500000000 | bytes 1000000 | tf_op jit(solution)/shard_map/pallas_call | solution.py:982
  142.9 2.0 %all-to-all-done.5 = f32[8,8,2304]{2,1,0:T(8,128)S(1)} async-done(((f32[8,8,2304]{2,1,0:T(8,128)}), f32[8,8,2304]{2,1,0:T(8,128)S(1)}, u32[]{:S(2)}, u32[]{:S(2)}) %all-to-all-start.5) | async-done | bytes 589856 | tf_op jit(solution)/shard_map/all_to_all | solution.py:994
  144.9 0.8 copy-done.4
  145.8 11.7 %shard_map.70 = (f32[32,32,128]{2,1,0:T(8,128)}, f32[32,32,128]{2,1,0:T(8,128)}) custom-call(s32[3]{0:T(128)} %pad_add_fusion.where_ref, f32[5]{0:T(128)} %e_ref.15, f32[64,2304]{1,0:T(8,128)} %bitcast.14, f32[26,32,128]{2,1,0:T(8,128)} %get-tuple-element.109.c1_local, f32[32,32,128]{2,1,0:T(8,128)} %get-tuple-element.110.known_ref, ...), custom_call_target="tpu_custom_call" | custom-call | flops 1000000 | bytes 1000000 | tf_op jit(solution)/shard_map/pallas_call | solution.py:982
  (16 shorter events, 1.7 us)
Async XLA Ops:
  0.6 12.0 %copy-start.1 = (f32[32,32,128]{2,1,0:T(8,128)S(1)}, f32[32,32,128]{2,1,0:T(8,128)}, u32[]{:S(2)}) copy-start(f32[32,32,128]{2,1,0:T(8,128)} %param.4) | copy-start | bytes 1572868
  1.8 10.8 %collective-permute-start.1 = (f32[32,12,128]{2,1,0:T(8,128)S(1)}, f32[32,12,128]{2,1,0:T(8,128)S(1)}, u32[]{:S(2)}, u32[]{:S(2)}) collective-permute-start(f32[32,12,128]{2,1,0:T(8,128)S(1)} %get-tuple-element.116), channel_id=1, source_target_pairs={{8,0},{16,8},{24,16},{32,24},{40,32},{48,40},{56,48},{9,1},{17,9},... | collective-permute-start | bytes 589832 | tf_op jit(solution)/shard_map/ppermute | solution.py:1008
  3.1 9.5 %collective-permute-start = (f32[32,12,128]{2,1,0:T(8,128)S(1)}, f32[32,12,128]{2,1,0:T(8,128)S(1)}, u32[]{:S(2)}, u32[]{:S(2)}) collective-permute-start(f32[32,12,128]{2,1,0:T(8,128)S(1)} %get-tuple-element.117), channel_id=1, source_target_pairs={{0,8},{8,16},{16,24},{24,32},{32,40},{40,48},{48,56},{1,9},{9,17},... | collective-permute-start | bytes 589832 | tf_op jit(solution)/shard_map/ppermute | solution.py:1008
  12.7 11.8 %collective-permute-start.2 = (f32[12,56,128]{2,1,0:T(8,128)S(1)}, f32[12,56,128]{2,1,0:T(8,128)S(1)}, u32[]{:S(2)}, u32[]{:S(2)}) collective-permute-start(f32[12,56,128]{2,1,0:T(8,128)S(1)} %get-tuple-element.114), channel_id=1, source_target_pairs={{0,64},{64,128},{128,192},{1,65},{65,129},{129,193},{2,66},{66,130... | collective-permute-start | bytes 1032200 | tf_op jit(solution)/shard_map/ppermute | solution.py:1008
  16.2 9.6 %collective-permute-start.3 = (f32[12,56,128]{2,1,0:T(8,128)S(1)}, f32[12,56,128]{2,1,0:T(8,128)S(1)}, u32[]{:S(2)}, u32[]{:S(2)}) collective-permute-start(f32[12,56,128]{2,1,0:T(8,128)S(1)} %get-tuple-element.115), channel_id=1, source_target_pairs={{64,0},{128,64},{192,128},{65,1},{129,65},{193,129},{66,2},{130,66... | collective-permute-start | bytes 1032200 | tf_op jit(solution)/shard_map/ppermute | solution.py:1008
  17.5 16.4 %all-to-all-start.1 = ((f32[8,11,8,128]{3,2,1,0:T(8,128)}), f32[8,11,8,128]{3,2,1,0:T(8,128)S(1)}, u32[]{:S(2)}, u32[]{:S(2)}) async-start(f32[8,11,8,128]{3,2,1,0:T(8,128)} %get-tuple-element.70), calls=%async_computation.1 | async-start | bytes 720896 | tf_op jit(solution)/shard_map/all_to_all | solution.py:994
  33.8 7.3 %copy-start.5 = (f32[8,11,8,128]{3,2,1,0:T(8,128)}, f32[8,11,8,128]{3,2,1,0:T(8,128)S(1)}, u32[]{:S(2)}) copy-start(f32[8,11,8,128]{3,2,1,0:T(8,128)S(1)} %all-to-all-done.1.table_ref) | copy-start | bytes 1081348
  33.8 18.7 %all-to-all-start = ((f32[8,8,2816]{2,1,0:T(8,128)}), f32[8,8,2816]{2,1,0:T(8,128)S(1)}, u32[]{:S(2)}, u32[]{:S(2)}) async-start(f32[8,8,2816]{2,1,0:T(8,128)} %get-tuple-element.66), calls=%async_computation | async-start | bytes 1441792 | tf_op jit(solution)/shard_map/all_to_all | solution.py:994
  52.5 0.9 copy-start
  81.5 16.9 %all-to-all-start.3 = ((f32[4,8,9,8,128]{4,3,2,1,0:T(8,128)}), f32[4,8,9,8,128]{4,3,2,1,0:T(8,128)S(1)}, u32[]{:S(2)}, u32[]{:S(2)}) async-start(f32[4,8,9,8,128]{4,3,2,1,0:T(8,128)} %broadcast_in_dim.2), calls=%async_computation.3 | async-start | bytes 2359296 | tf_op jit(solution)/shard_map/all_to_all | solution.py:994
  98.4 1.0 copy-start.2
  105.1 15.3 %all-to-all-start.4 = ((f32[8,8,1536]{2,1,0:T(8,128)}), f32[8,8,1536]{2,1,0:T(8,128)S(1)}, u32[]{:S(2)}, u32[]{:S(2)}) async-start(f32[8,8,1536]{2,1,0:T(8,128)} %get-tuple-element.88), calls=%async_computation.4 | async-start | bytes 786432 | tf_op jit(solution)/shard_map/all_to_all | solution.py:994
  120.4 0.7 copy-start.3
  130.2 14.7 %all-to-all-start.5 = ((f32[8,8,2304]{2,1,0:T(8,128)}), f32[8,8,2304]{2,1,0:T(8,128)S(1)}, u32[]{:S(2)}, u32[]{:S(2)}) async-start(f32[8,8,2304]{2,1,0:T(8,128)} %get-tuple-element.102), calls=%async_computation.5 | async-start | bytes 1179648 | tf_op jit(solution)/shard_map/all_to_all | solution.py:994
  144.9 0.8 copy-start.4
